TPU v7x, 32 devices: a whole 2x2x4 slice. The times are simulated.
32 devices in a mesh: station: 4 (over y, x), dom: 8 (over z, core).
Axes of the slice: x: 2, y: 2, z: 4, core: 2. Of those that a mesh axis runs over, the one named last changes fastest.
Arguments:
- beam_first: float32 [4, 8, 4, 8192], P('station', 'dom'), may hold values from -3.5 to 3.5
- beam_second: float32 [4, 8, 4, 8192], P('station', 'dom'), may hold values from -3.5 to 3.5
- green_smooth: float32 [128, 128], replicated, may hold values from -0.5 to 0.5
- green_slope: float32 [128, 128], replicated, may hold values from -0.5 to 0.5
- destination: int32 [4, 512, 1], P('station', 'dom'), may hold values from 0 to 3; in each aligned block of 64 rows (0 to 63, 64 to 127, ..., all dimensions but the last counted through in order) at most 32 rows name the same one
Outputs:
- resliced: float32 [4, 8, 4, 32, 4, 128], P('station', 'dom')
- beam_second_out: float32 [4, 8, 4, 8192], P('station', 'dom')
Inputs may be any that keep to these rules, and one draw needn't show every extreme that they name: `destination`: in the rows of one device (the 64 blocks of one station and dom index) no station is named more than 32 times, a bound that some block reaches.
All inputs are finite; a program needn't handle non-finite values.
Results may differ from a plain program's by a relative error of at most 0.00095.
Values may be sent and summed in bfloat16 or wider, within the bound.
No kernel may reach another device: no remote copies, remote signals or barrier semaphores. Data moves between devices by JAX's collectives and lax.ppermute only.
A program may use at most 64 MiB of HBM per device.

v0:
```python
import functools

import jax
import jax.numpy as jnp
from jax import lax
from jax.experimental import pallas as pl
from jax.experimental.pallas import tpu as pltpu
from jax.sharding import PartitionSpec as P

GRID = 128
FRONTS = 4
BLOCK = 128
TILE = 4096
ROWS = 16


EDGE = 4.0
DRIFT = 0.05
STRENGTH = 0.06
HIGH = lax.Precision.HIGHEST
SPACING = 2.0 * EDGE / (GRID - 1)


def shifted(value, axis, steps):
    count = lax.axis_size(axis)
    pairs = [(source, (source + steps) % count) for source in range(count)]
    return lax.ppermute(value, axis, pairs)


def summed(value, axis):
    count = lax.axis_size(axis)
    step = 1
    while step < count:
        pairs = [(source, source ^ step) for source in range(count)]
        value = value + lax.ppermute(value.astype(jnp.bfloat16), axis, pairs).astype(jnp.float32)
        step *= 2
    return value


def hat_table(coordinate):
    count = coordinate.shape[1]
    place = jnp.clip((coordinate + EDGE) * (1.0 / SPACING), -2.0, GRID + 2.0)
    cell = jnp.floor(place)
    upper = place - cell
    lower = 1.0 - upper

    def spread(row):
        return jnp.broadcast_to(row, (ROWS, count)).astype(jnp.bfloat16)

    cell, lower, upper = spread(cell), spread(lower), spread(upper)
    none = jnp.zeros((ROWS, count), jnp.bfloat16)
    index = lax.broadcasted_iota(jnp.int32, (ROWS, count), 0).astype(jnp.float32)
    parts = []
    for start in range(0, GRID, ROWS):
        at = (index + float(start)).astype(jnp.bfloat16)
        before = (index + float(start - 1)).astype(jnp.bfloat16)
        parts.append(jnp.where(cell == at, lower, jnp.where(cell == before, upper, none)))
    return jnp.concatenate(parts, axis=0)


def deposit(x, y):
    return lax.dot_general(
        hat_table(y), hat_table(x), (((1,), (1,)), ((), ())), preferred_element_type=jnp.float32
    )


def kick(x, moment_x, y, moment_y, table):
    sampled = jnp.dot(table, hat_table(x), preferred_element_type=jnp.float32)
    weight_y = hat_table(y).astype(jnp.float32)
    moment_x = moment_x - jnp.sum(sampled[:GRID] * weight_y, axis=0, keepdims=True)
    moment_y = moment_y - jnp.sum(sampled[GRID:] * weight_y, axis=0, keepdims=True)
    return x + DRIFT * moment_x, moment_x, y + DRIFT * moment_y, moment_y


def tables(density, smooth, slope, scale):
    stacked = density.reshape(2 * GRID, GRID) * scale
    greens = jnp.concatenate([slope, smooth], axis=0)
    inner = lax.dot_general(
        stacked, greens, (((1,), (1,)), ((), ())), precision=HIGH, preferred_element_type=jnp.float32
    )
    by_slope = jnp.concatenate([inner[:GRID, :GRID], inner[GRID:, :GRID]], axis=1)
    by_smooth = jnp.concatenate([inner[:GRID, GRID:], inner[GRID:, GRID:]], axis=1)
    push_x = jnp.dot(smooth, by_slope, precision=HIGH, preferred_element_type=jnp.float32)
    push_y = jnp.dot(slope, by_smooth, precision=HIGH, preferred_element_type=jnp.float32)
    both = jnp.concatenate([push_x, push_y], axis=0).astype(jnp.bfloat16)
    return both[:, :GRID], both[:, GRID:]


def columns(count):
    width = min(TILE, count)
    return [pl.ds(start, width) for start in range(0, count, width)]


def first_kernel(resident_ref, opposing_ref, density_ref):
    for which, ref in enumerate((resident_ref, opposing_ref)):
        density_ref[which] = sum(
            deposit(ref[0:1, tile], ref[2:3, tile]) for tile in columns(ref.shape[1])
        )


def opposing_kernel(scale, split, density_ref, smooth_ref, slope_ref, *refs):
    own, other = tables(density_ref[...], smooth_ref[...], slope_ref[...], scale)
    *sources, place_ref, moment_ref, table_ref = refs
    table_ref[...] = other
    for tile in columns(place_ref.shape[1]):
        if split:
            x, y = (sources[0][row : row + 1, tile] for row in range(2))
            moment_x, moment_y = (sources[1][row : row + 1, tile] for row in range(2))
        else:
            x, moment_x, y, moment_y = (sources[0][row : row + 1, tile] for row in range(4))
        x, moment_x, y, moment_y = kick(x, moment_x, y, moment_y, own)
        place_ref[0:1, tile] = x
        place_ref[1:2, tile] = y
        moment_ref[0:1, tile] = moment_x
        moment_ref[1:2, tile] = moment_y


def resident_kernel(table_ref, beam_ref, moved_ref, density_ref):
    total = 0.0
    for tile in columns(beam_ref.shape[1]):
        new = kick(*(beam_ref[row : row + 1, tile] for row in range(4)), table_ref[...])
        for row in range(4):
            moved_ref[row : row + 1, tile] = new[row]
        total = total + deposit(new[0], new[2])
    density_ref[...] = total


def arrival_kernel(place_ref, resident_ref, density_ref):
    density_ref[0] = resident_ref[...]
    density_ref[1] = sum(
        deposit(place_ref[0:1, tile], place_ref[1:2, tile]) for tile in columns(place_ref.shape[1])
    )


def last_kernel(scale, slots_ref, density_ref, smooth_ref, slope_ref, beam_ref, packed_ref, table_ref, moved_ref):
    table_ref[...], other = tables(density_ref[...], smooth_ref[...], slope_ref[...], scale)
    packed_ref[...] = jnp.zeros_like(packed_ref)
    for tile in columns(beam_ref.shape[1]):
        new = kick(*(beam_ref[row : row + 1, tile] for row in range(4)), other)
        for row in range(4):
            moved_ref[row : row + 1, tile] = new[row]
    for block in range(beam_ref.shape[1] // BLOCK):
        packed_ref[slots_ref[block]] = moved_ref[:, block * BLOCK : (block + 1) * BLOCK]


def final_kernel(table_ref, place_ref, moment_ref, out_ref):
    for tile in columns(place_ref.shape[1]):
        new = kick(
            place_ref[0:1, tile],
            moment_ref[0:1, tile],
            place_ref[1:2, tile],
            moment_ref[1:2, tile],
            table_ref[...],
        )
        for row in range(4):
            out_ref[row : row + 1, tile] = new[row]


def local(kernel, out_shape, **options):
    return pl.pallas_call(
        kernel,
        out_shape=out_shape,
        compiler_params=pltpu.CompilerParams(vmem_limit_bytes=24 << 20),
        **options,
    )


def array(*shape, dtype=jnp.float32):
    return jax.ShapeDtypeStruct(shape, dtype)


def slots(routes, stations, capacity):
    onehot = (routes[:, None] == jnp.arange(stations, dtype=jnp.int32)[None, :]).astype(jnp.int32)
    ranking = jnp.sum((jnp.cumsum(onehot, axis=0) - onehot) * onehot, axis=1)
    return routes * capacity + jnp.minimum(ranking, capacity - 1)


def shards(beam_first, beam_second, green_smooth, green_slope, destination):
    resident = beam_first[0, 0]
    opposing = (beam_second[0, 0],)
    groups = lax.axis_size("dom")
    stations = lax.axis_size("station")
    count = resident.shape[1]
    block_count = count // BLOCK
    capacity = max(2, 2 * block_count // stations)
    scale = STRENGTH * GRID * GRID / (count * groups)
    half, whole = array(2, count), array(4, count)
    density, densities = array(GRID, GRID), array(2, GRID, GRID)
    table = array(2 * GRID, GRID, dtype=jnp.bfloat16)
    place = slots(destination[0, :, 0].astype(jnp.int32), stations, capacity)

    total = local(first_kernel, densities)(resident, opposing[0])
    for front_index in range(FRONTS - 1):
        total = summed(total, "dom")
        positions, moments, other = local(
            functools.partial(opposing_kernel, scale, len(opposing) == 2), (half, half, table)
        )(total, green_smooth, green_slope, *opposing)
        opposing = (shifted(positions, "station", 1), shifted(moments, "station", 1))
        resident, part = local(resident_kernel, (whole, density))(other, resident)
        total = local(arrival_kernel, densities)(opposing[0], part)
    total = summed(total, "dom")
    vmem = pl.BlockSpec(memory_space=pltpu.VMEM)
    outgoing, own = local(
        functools.partial(last_kernel, scale),
        (array(stations * capacity, 4, BLOCK), table),
        in_specs=[pl.BlockSpec(memory_space=pltpu.SMEM)] + [vmem] * 4,
        out_specs=(vmem, vmem),
        scratch_shapes=[pltpu.VMEM((4, count), jnp.float32)],
    )(place, total, green_smooth, green_slope, resident)
    outgoing = outgoing.reshape(stations, capacity, 4, BLOCK)
    arrived = lax.all_to_all(outgoing, "station", split_axis=0, concat_axis=0, tiled=True)
    opposing = local(final_kernel, whole)(own, *opposing)
    return (arrived[None, None], opposing[None, None])


def solution(mesh):
    placed = (
        P("station", "dom", None, None),
        P("station", "dom", None, None),
        P(),
        P(),
        P("station", "dom", None),
    )
    return jax.shard_map(
        shards,
        mesh=mesh,
        in_specs=placed,
        out_specs=(P("station", "dom", None, None, None, None), P("station", "dom", None, None)),
        check_vma=False,
    )
```

profile of v0, /device:TPU:0, one launch (start us, length us, event | category | flops | bytes accessed | tf_op | source)
XLA Modules:
  0.0 97.2 jit_solution(4383101252673689910)
XLA Ops:
  0.6 0.9 copy-done.2
  1.5 0.9 copy-done.4
  2.4 1.6 %shard_map.68 = f32[2,128,128]{2,1,0:T(8,128)S(1)} custom-call(f32[4,8192]{1,0:T(4,128)S(1)} %bitcast.9, f32[4,8192]{1,0:T(4,128)S(1)} %bitcast.7), custom_call_target="tpu_custom_call" | custom-call | tf_op jit(solution)/shard_map/pallas_call | solution.py:192
  4.0 0.6 collective-permute-start
  4.6 0.9 collective-permute-done
  5.5 3.0 %collective-permute-start.1 = (bf16[2,128,128]{2,1,0:T(8,128)(2,1)S(1)}, bf16[2,128,128]{2,1,0:T(8,128)(2,1)S(1)}, u32[]{:S(2)}, u32[]{:S(2)}) collective-permute-start(bf16[2,128,128]{2,1,0:T(8,128)(2,1)S(1)} %fusion), channel_id=1, source_target_pairs={{0,2},{1,3},{2,0},{3,1},{4,6},{5,7},{6,4},{7,5},{8,10},{9,11},{10,... | collective-permute-start | bytes 196616 | tf_op jit(solution)/shard_map/ppermute | solution.py:35
  8.5 2.4 %collective-permute-done.1 = bf16[2,128,128]{2,1,0:T(8,128)(2,1)S(1)} collective-permute-done((bf16[2,128,128]{2,1,0:T(8,128)(2,1)S(1)}, bf16[2,128,128]{2,1,0:T(8,128)(2,1)S(1)}, u32[]{:S(2)}, u32[]{:S(2)}) %collective-permute-start.1) | collective-permute-done | bytes 65568 | tf_op jit(solution)/shard_map/ppermute | solution.py:35
  11.0 2.9 %collective-permute-start.2 = (bf16[2,128,128]{2,1,0:T(8,128)(2,1)S(1)}, bf16[2,128,128]{2,1,0:T(8,128)(2,1)S(1)}, u32[]{:S(2)}, u32[]{:S(2)}) collective-permute-start(bf16[2,128,128]{2,1,0:T(8,128)(2,1)S(1)} %fusion.4), channel_id=1, source_target_pairs={{0,4},{1,5},{2,6},{3,7},{4,0},{5,1},{6,2},{7,3},{8,12},{9,13},{10,... | collective-permute-start | bytes 196616 | tf_op jit(solution)/shard_map/ppermute | solution.py:35
  13.9 2.3 %collective-permute-done.2 = bf16[2,128,128]{2,1,0:T(8,128)(2,1)S(1)} collective-permute-done((bf16[2,128,128]{2,1,0:T(8,128)(2,1)S(1)}, bf16[2,128,128]{2,1,0:T(8,128)(2,1)S(1)}, u32[]{:S(2)}, u32[]{:S(2)}) %collective-permute-start.2) | collective-permute-done | bytes 65568 | tf_op jit(solution)/shard_map/ppermute | solution.py:35
  16.3 2.8 %shard_map.69 = (f32[2,8192]{1,0:T(2,128)S(1)}, f32[2,8192]{1,0:T(2,128)S(1)}, bf16[256,128]{1,0:T(8,128)(2,1)S(1)}) custom-call(f32[2,128,128]{2,1,0:T(8,128)S(1)} %convert_add_fusion.9.density_ref, f32[128,128]{1,0:T(8,128)S(1)} %copy-done, f32[128,128]{1,0:T(8,128)S(1)} %copy-done.1, f32[4,8192]{1,0:T(4,128)S(1)} %bitcast.8), custom_call_target="tpu_custom_call" | custom-call | tf_op jit(solution)/shard_map/pallas_call | solution.py:195
  19.1 1.8 %collective-permute-start.3 = (f32[2,8192]{1,0:T(2,128)S(1)}, f32[2,8192]{1,0:T(2,128)S(1)}, u32[]{:S(2)}, u32[]{:S(2)}) collective-permute-start(f32[2,8192]{1,0:T(2,128)S(1)} %get-tuple-element.19), channel_id=1, source_target_pairs={{0,8},{8,16},{16,24},{24,0},{1,9},{9,17},{17,25},{25,1},{2,10},{10... | collective-permute-start | bytes 196616 | tf_op jit(solution)/shard_map/ppermute | solution.py:27
  20.9 3.0 %shard_map.70 = (f32[4,8192]{1,0:T(4,128)S(1)}, f32[128,128]{1,0:T(8,128)S(1)}) custom-call(bf16[256,128]{1,0:T(8,128)(2,1)S(1)} %get-tuple-element.20.table_ref, f32[4,8192]{1,0:T(4,128)S(1)} %bitcast.10), custom_call_target="tpu_custom_call" | custom-call | tf_op jit(solution)/shard_map/pallas_call | solution.py:199
  23.9 0.4 collective-permute-done.3.place_ref.refs_0_
  24.3 0.9 shard_map.71
  25.3 1.2 %collective-permute-done.4 = bf16[2,128,128]{2,1,0:T(8,128)(2,1)S(1)} collective-permute-done((bf16[2,128,128]{2,1,0:T(8,128)(2,1)S(1)}, bf16[2,128,128]{2,1,0:T(8,128)(2,1)S(1)}, u32[]{:S(2)}, u32[]{:S(2)}) %collective-permute-start.4) | collective-permute-done | bytes 65568 | tf_op jit(solution)/shard_map/ppermute | solution.py:35
  26.5 1.9 %collective-permute-start.5 = (bf16[2,128,128]{2,1,0:T(8,128)(2,1)S(1)}, bf16[2,128,128]{2,1,0:T(8,128)(2,1)S(1)}, u32[]{:S(2)}, u32[]{:S(2)}) collective-permute-start(bf16[2,128,128]{2,1,0:T(8,128)(2,1)S(1)} %fusion.1), channel_id=1, source_target_pairs={{0,2},{1,3},{2,0},{3,1},{4,6},{5,7},{6,4},{7,5},{8,10},{9,11},{10,... | collective-permute-start | bytes 196616 | tf_op jit(solution)/shard_map/ppermute | solution.py:35
  28.4 2.4 %collective-permute-done.5 = bf16[2,128,128]{2,1,0:T(8,128)(2,1)S(1)} collective-permute-done((bf16[2,128,128]{2,1,0:T(8,128)(2,1)S(1)}, bf16[2,128,128]{2,1,0:T(8,128)(2,1)S(1)}, u32[]{:S(2)}, u32[]{:S(2)}) %collective-permute-start.5) | collective-permute-done | bytes 65568 | tf_op jit(solution)/shard_map/ppermute | solution.py:35
  30.9 3.2 %collective-permute-start.6 = (bf16[2,128,128]{2,1,0:T(8,128)(2,1)S(1)}, bf16[2,128,128]{2,1,0:T(8,128)(2,1)S(1)}, u32[]{:S(2)}, u32[]{:S(2)}) collective-permute-start(bf16[2,128,128]{2,1,0:T(8,128)(2,1)S(1)} %fusion.5), channel_id=1, source_target_pairs={{0,4},{1,5},{2,6},{3,7},{4,0},{5,1},{6,2},{7,3},{8,12},{9,13},{10,... | collective-permute-start | bytes 196616 | tf_op jit(solution)/shard_map/ppermute | solution.py:35
  34.1 0.9 collective-permute-start.7
  35.0 1.7 %collective-permute-done.6 = bf16[2,128,128]{2,1,0:T(8,128)(2,1)S(1)} collective-permute-done((bf16[2,128,128]{2,1,0:T(8,128)(2,1)S(1)}, bf16[2,128,128]{2,1,0:T(8,128)(2,1)S(1)}, u32[]{:S(2)}, u32[]{:S(2)}) %collective-permute-start.6) | collective-permute-done | bytes 65568 | tf_op jit(solution)/shard_map/ppermute | solution.py:35
  36.7 2.6 %collective-permute-done.7.refs_1_ = f32[2,8192]{1,0:T(2,128)S(1)} collective-permute-done((f32[2,8192]{1,0:T(2,128)S(1)}, f32[2,8192]{1,0:T(2,128)S(1)}, u32[]{:S(2)}, u32[]{:S(2)}) %collective-permute-start.7) | collective-permute-done | bytes 65568 | tf_op jit(solution)/shard_map/ppermute | solution.py:27
  39.3 2.8 %shard_map.72 = (f32[2,8192]{1,0:T(2,128)S(1)}, f32[2,8192]{1,0:T(2,128)S(1)}, bf16[256,128]{1,0:T(8,128)(2,1)S(1)}) custom-call(f32[2,128,128]{2,1,0:T(8,128)S(1)} %convert_add_fusion.6.density_ref, f32[128,128]{1,0:T(8,128)S(1)} %copy-done, f32[128,128]{1,0:T(8,128)S(1)} %copy-done.1, f32[2,8192]{1,0:T(2,128)S(1)} %collective-permute-done.3.place_ref.refs_0_, ...), custom_call_target="tpu_custom_call" | custom-call | tf_op jit(solution)/shard_map/pallas_call | solution.py:195
  42.3 3.0 %shard_map.73 = (f32[4,8192]{1,0:T(4,128)S(1)}, f32[128,128]{1,0:T(8,128)S(1)}) custom-call(bf16[256,128]{1,0:T(8,128)(2,1)S(1)} %get-tuple-element.24.table_ref, f32[4,8192]{1,0:T(4,128)S(1)} %get-tuple-element.25.beam_ref), custom_call_target="tpu_custom_call" | custom-call | tf_op jit(solution)/shard_map/pallas_call | solution.py:199
  45.4 2.1 %collective-permute-done.8.place_ref.refs_0_ = f32[2,8192]{1,0:T(2,128)S(1)} collective-permute-done((f32[2,8192]{1,0:T(2,128)S(1)}, f32[2,8192]{1,0:T(2,128)S(1)}, u32[]{:S(2)}, u32[]{:S(2)}) %collective-permute-start.8) | collective-permute-done | bytes 65568 | tf_op jit(solution)/shard_map/ppermute | solution.py:27
  47.5 0.9 shard_map.74
  48.4 1.2 %collective-permute-done.9 = bf16[2,128,128]{2,1,0:T(8,128)(2,1)S(1)} collective-permute-done((bf16[2,128,128]{2,1,0:T(8,128)(2,1)S(1)}, bf16[2,128,128]{2,1,0:T(8,128)(2,1)S(1)}, u32[]{:S(2)}, u32[]{:S(2)}) %collective-permute-start.9) | collective-permute-done | bytes 65568 | tf_op jit(solution)/shard_map/ppermute | solution.py:35
  49.7 1.9 %collective-permute-start.10 = (bf16[2,128,128]{2,1,0:T(8,128)(2,1)S(1)}, bf16[2,128,128]{2,1,0:T(8,128)(2,1)S(1)}, u32[]{:S(2)}, u32[]{:S(2)}) collective-permute-start(bf16[2,128,128]{2,1,0:T(8,128)(2,1)S(1)} %fusion.2), channel_id=1, source_target_pairs={{0,2},{1,3},{2,0},{3,1},{4,6},{5,7},{6,4},{7,5},{8,10},{9,11},{10,... | collective-permute-start | bytes 196616 | tf_op jit(solution)/shard_map/ppermute | solution.py:35
  51.6 2.4 %collective-permute-done.10 = bf16[2,128,128]{2,1,0:T(8,128)(2,1)S(1)} collective-permute-done((bf16[2,128,128]{2,1,0:T(8,128)(2,1)S(1)}, bf16[2,128,128]{2,1,0:T(8,128)(2,1)S(1)}, u32[]{:S(2)}, u32[]{:S(2)}) %collective-permute-start.10) | collective-permute-done | bytes 65568 | tf_op jit(solution)/shard_map/ppermute | solution.py:35
  54.0 0.4 collective-permute-start.11
  54.5 0.9 collective-permute-start.12
  55.4 3.9 %collective-permute-done.11 = bf16[2,128,128]{2,1,0:T(8,128)(2,1)S(1)} collective-permute-done((bf16[2,128,128]{2,1,0:T(8,128)(2,1)S(1)}, bf16[2,128,128]{2,1,0:T(8,128)(2,1)S(1)}, u32[]{:S(2)}, u32[]{:S(2)}) %collective-permute-start.11) | collective-permute-done | bytes 65568 | tf_op jit(solution)/shard_map/ppermute | solution.py:35
  59.6 2.8 %shard_map.75 = (f32[2,8192]{1,0:T(2,128)S(1)}, f32[2,8192]{1,0:T(2,128)S(1)}, bf16[256,128]{1,0:T(8,128)(2,1)S(1)}) custom-call(f32[2,128,128]{2,1,0:T(8,128)S(1)} %convert_add_fusion.3.density_ref, f32[128,128]{1,0:T(8,128)S(1)} %copy-done, f32[128,128]{1,0:T(8,128)S(1)} %copy-done.1, f32[2,8192]{1,0:T(2,128)S(1)} %collective-permute-done.8.place_ref.refs_0_, ...), custom_call_target="tpu_custom_call" | custom-call | tf_op jit(solution)/shard_map/pallas_call | solution.py:195
  62.4 0.9 collective-permute-start.13
  63.3 3.0 %shard_map.76 = (f32[4,8192]{1,0:T(4,128)S(1)}, f32[128,128]{1,0:T(8,128)S(1)}) custom-call(bf16[256,128]{1,0:T(8,128)(2,1)S(1)} %get-tuple-element.29.table_ref, f32[4,8192]{1,0:T(4,128)S(1)} %get-tuple-element.30.beam_ref), custom_call_target="tpu_custom_call" | custom-call | tf_op jit(solution)/shard_map/pallas_call | solution.py:199
  66.3 1.5 %collective-permute-done.13.place_ref = f32[2,8192]{1,0:T(2,128)S(1)} collective-permute-done((f32[2,8192]{1,0:T(2,128)S(1)}, f32[2,8192]{1,0:T(2,128)S(1)}, u32[]{:S(2)}, u32[]{:S(2)}) %collective-permute-start.13) | collective-permute-done | bytes 65568 | tf_op jit(solution)/shard_map/ppermute | solution.py:27
  67.9 0.9 shard_map.77
  68.8 0.6 copy-done.6
  69.6 0.5 collective-permute-done.14
  70.1 1.9 %collective-permute-start.15 = (bf16[2,128,128]{2,1,0:T(8,128)(2,1)S(1)}, bf16[2,128,128]{2,1,0:T(8,128)(2,1)S(1)}, u32[]{:S(2)}, u32[]{:S(2)}) collective-permute-start(bf16[2,128,128]{2,1,0:T(8,128)(2,1)S(1)} %fusion.3), channel_id=1, source_target_pairs={{0,2},{1,3},{2,0},{3,1},{4,6},{5,7},{6,4},{7,5},{8,10},{9,11},{10,... | collective-permute-start | bytes 196616 | tf_op jit(solution)/shard_map/ppermute | solution.py:35
  72.2 2.3 %collective-permute-done.15 = bf16[2,128,128]{2,1,0:T(8,128)(2,1)S(1)} collective-permute-done((bf16[2,128,128]{2,1,0:T(8,128)(2,1)S(1)}, bf16[2,128,128]{2,1,0:T(8,128)(2,1)S(1)}, u32[]{:S(2)}, u32[]{:S(2)}) %collective-permute-start.15) | collective-permute-done | bytes 65568 | tf_op jit(solution)/shard_map/ppermute | solution.py:35
  74.5 2.6 %collective-permute-start.16 = (bf16[2,128,128]{2,1,0:T(8,128)(2,1)S(1)}, bf16[2,128,128]{2,1,0:T(8,128)(2,1)S(1)}, u32[]{:S(2)}, u32[]{:S(2)}) collective-permute-start(bf16[2,128,128]{2,1,0:T(8,128)(2,1)S(1)} %fusion.7), channel_id=1, source_target_pairs={{0,4},{1,5},{2,6},{3,7},{4,0},{5,1},{6,2},{7,3},{8,12},{9,13},{10,... | collective-permute-start | bytes 196616 | tf_op jit(solution)/shard_map/ppermute | solution.py:35
  77.1 2.6 %collective-permute-done.16 = bf16[2,128,128]{2,1,0:T(8,128)(2,1)S(1)} collective-permute-done((bf16[2,128,128]{2,1,0:T(8,128)(2,1)S(1)}, bf16[2,128,128]{2,1,0:T(8,128)(2,1)S(1)}, u32[]{:S(2)}, u32[]{:S(2)}) %collective-permute-start.16) | collective-permute-done | bytes 65568 | tf_op jit(solution)/shard_map/ppermute | solution.py:35
  79.7 4.0 %shard_map.78 = (f32[128,4,128]{2,1,0:T(4,128)}, bf16[256,128]{1,0:T(8,128)(2,1)S(1)}) custom-call(s32[64]{0:T(128)S(1)} %minimum_add_fusion.slots_ref, f32[2,128,128]{2,1,0:T(8,128)S(1)} %convert_add_fusion.density_ref, f32[128,128]{1,0:T(8,128)S(1)} %copy-done, f32[128,128]{1,0:T(8,128)S(1)} %copy-done.1, f32[4,8192]{1,0:T(4,128)S(1)} %get-tuple-element.32.beam_ref), custom_call_target="tpu_custom_call" | custom-call | tf_op jit(solution)/shard_map/pallas_call | solution.py:203
  83.8 3.4 %all-to-all-start = ((f32[4,32,4,128]{3,2,1,0:T(4,128)}), f32[4,32,4,128]{3,2,1,0:T(4,128)S(1)}, u32[]{:S(2)}, u32[]{:S(2)}) async-start(f32[4,32,4,128]{3,2,1,0:T(4,128)} %bitcast.3), calls=%async_computation | async-start | bytes 524288 | tf_op jit(solution)/shard_map/all_to_all | solution.py:211
  87.2 2.0 %collective-permute-start.17 = (f32[2,8192]{1,0:T(2,128)S(1)}, f32[2,8192]{1,0:T(2,128)S(1)}, u32[]{:S(2)}, u32[]{:S(2)}) collective-permute-start(f32[2,8192]{1,0:T(2,128)S(1)} %get-tuple-element.35), channel_id=1, source_target_pairs={{0,8},{8,16},{16,24},{24,0},{1,9},{9,17},{17,25},{25,1},{2,10},{10... | collective-permute-start | bytes 196616 | tf_op jit(solution)/shard_map/ppermute | solution.py:27
  89.2 4.8 %collective-permute-done.17.moment_ref = f32[2,8192]{1,0:T(2,128)S(1)} collective-permute-done((f32[2,8192]{1,0:T(2,128)S(1)}, f32[2,8192]{1,0:T(2,128)S(1)}, u32[]{:S(2)}, u32[]{:S(2)}) %collective-permute-start.17) | collective-permute-done | bytes 65568 | tf_op jit(solution)/shard_map/ppermute | solution.py:27
  93.9 2.6 %shard_map.79 = f32[4,8192]{1,0:T(4,128)} custom-call(bf16[256,128]{1,0:T(8,128)(2,1)S(1)} %get-tuple-element.34.table_ref, f32[2,8192]{1,0:T(2,128)S(1)} %collective-permute-done.13.place_ref, f32[2,8192]{1,0:T(2,128)S(1)} %collective-permute-done.17.moment_ref), custom_call_target="tpu_custom_call" | custom-call | tf_op jit(solution)/shard_map/pallas_call | solution.py:212
  96.5 0.7 copy.8
  (37 shorter events, 1.5 us)
Async XLA Ops:
  0.6 0.9 copy-start.2
  1.5 0.9 copy-start.4
  4.0 1.5 %collective-permute-start = (bf16[2,128,128]{2,1,0:T(8,128)(2,1)S(1)}, bf16[2,128,128]{2,1,0:T(8,128)(2,1)S(1)}, u32[]{:S(2)}, u32[]{:S(2)}) collective-permute-start(bf16[2,128,128]{2,1,0:T(8,128)(2,1)S(1)} %convert_element_type.76), channel_id=1, source_target_pairs={{0,1},{1,0},{2,3},{3,2},{4,5},{5,4},{6,7},{7,6},{8,9},{9,8},{10,11... | collective-permute-start | bytes 196616 | tf_op jit(solution)/shard_map/ppermute | solution.py:35
  5.5 5.4 %collective-permute-start.1 = (bf16[2,128,128]{2,1,0:T(8,128)(2,1)S(1)}, bf16[2,128,128]{2,1,0:T(8,128)(2,1)S(1)}, u32[]{:S(2)}, u32[]{:S(2)}) collective-permute-start(bf16[2,128,128]{2,1,0:T(8,128)(2,1)S(1)} %fusion), channel_id=1, source_target_pairs={{0,2},{1,3},{2,0},{3,1},{4,6},{5,7},{6,4},{7,5},{8,10},{9,11},{10,... | collective-permute-start | bytes 196616 | tf_op jit(solution)/shard_map/ppermute | solution.py:35
  10.9 5.3 %copy-start = (f32[128,128]{1,0:T(8,128)S(1)}, f32[128,128]{1,0:T(8,128)}, u32[]{:S(2)}) copy-start(f32[128,128]{1,0:T(8,128)} %smooth_ref.7) | copy-start | bytes 196612
  11.0 5.3 %copy-start.1 = (f32[128,128]{1,0:T(8,128)S(1)}, f32[128,128]{1,0:T(8,128)}, u32[]{:S(2)}) copy-start(f32[128,128]{1,0:T(8,128)} %slope_ref.7) | copy-start | bytes 196612
  11.0 5.3 %copy-start.3 = (f32[1,1,4,8192]{3,2,1,0:T(4,128)S(1)}, f32[1,1,4,8192]{3,2,1,0:T(4,128)}, u32[]{:S(2)}) copy-start(f32[1,1,4,8192]{3,2,1,0:T(4,128)} %param.6) | copy-start | bytes 393220
  11.0 5.3 %collective-permute-start.2 = (bf16[2,128,128]{2,1,0:T(8,128)(2,1)S(1)}, bf16[2,128,128]{2,1,0:T(8,128)(2,1)S(1)}, u32[]{:S(2)}, u32[]{:S(2)}) collective-permute-start(bf16[2,128,128]{2,1,0:T(8,128)(2,1)S(1)} %fusion.4), channel_id=1, source_target_pairs={{0,4},{1,5},{2,6},{3,7},{4,0},{5,1},{6,2},{7,3},{8,12},{9,13},{10,... | collective-permute-start | bytes 196616 | tf_op jit(solution)/shard_map/ppermute | solution.py:35
  16.3 4.6 %copy-start.5 = (f32[1,1,4,8192]{3,2,1,0:T(4,128)S(1)}, f32[1,1,4,8192]{3,2,1,0:T(4,128)}, u32[]{:S(2)}) copy-start(f32[1,1,4,8192]{3,2,1,0:T(4,128)} %param.5) | copy-start | bytes 393220
  19.1 5.2 %collective-permute-start.3 = (f32[2,8192]{1,0:T(2,128)S(1)}, f32[2,8192]{1,0:T(2,128)S(1)}, u32[]{:S(2)}, u32[]{:S(2)}) collective-permute-start(f32[2,8192]{1,0:T(2,128)S(1)} %get-tuple-element.19), channel_id=1, source_target_pairs={{0,8},{8,16},{16,24},{24,0},{1,9},{9,17},{17,25},{25,1},{2,10},{10... | collective-permute-start | bytes 196616 | tf_op jit(solution)/shard_map/ppermute | solution.py:27
  25.2 1.3 %collective-permute-start.4 = (bf16[2,128,128]{2,1,0:T(8,128)(2,1)S(1)}, bf16[2,128,128]{2,1,0:T(8,128)(2,1)S(1)}, u32[]{:S(2)}, u32[]{:S(2)}) collective-permute-start(bf16[2,128,128]{2,1,0:T(8,128)(2,1)S(1)} %convert_element_type.82), channel_id=1, source_target_pairs={{0,1},{1,0},{2,3},{3,2},{4,5},{5,4},{6,7},{7,6},{8,9},{9,8},{10,11... | collective-permute-start | bytes 196616 | tf_op jit(solution)/shard_map/ppermute | solution.py:35
  26.5 4.3 %collective-permute-start.5 = (bf16[2,128,128]{2,1,0:T(8,128)(2,1)S(1)}, bf16[2,128,128]{2,1,0:T(8,128)(2,1)S(1)}, u32[]{:S(2)}, u32[]{:S(2)}) collective-permute-start(bf16[2,128,128]{2,1,0:T(8,128)(2,1)S(1)} %fusion.1), channel_id=1, source_target_pairs={{0,2},{1,3},{2,0},{3,1},{4,6},{5,7},{6,4},{7,5},{8,10},{9,11},{10,... | collective-permute-start | bytes 196616 | tf_op jit(solution)/shard_map/ppermute | solution.py:35
  30.9 5.8 %collective-permute-start.6 = (bf16[2,128,128]{2,1,0:T(8,128)(2,1)S(1)}, bf16[2,128,128]{2,1,0:T(8,128)(2,1)S(1)}, u32[]{:S(2)}, u32[]{:S(2)}) collective-permute-start(bf16[2,128,128]{2,1,0:T(8,128)(2,1)S(1)} %fusion.5), channel_id=1, source_target_pairs={{0,4},{1,5},{2,6},{3,7},{4,0},{5,1},{6,2},{7,3},{8,12},{9,13},{10,... | collective-permute-start | bytes 196616 | tf_op jit(solution)/shard_map/ppermute | solution.py:35
  34.1 5.2 %collective-permute-start.7 = (f32[2,8192]{1,0:T(2,128)S(1)}, f32[2,8192]{1,0:T(2,128)S(1)}, u32[]{:S(2)}, u32[]{:S(2)}) collective-permute-start(f32[2,8192]{1,0:T(2,128)S(1)} %get-tuple-element.22), channel_id=1, source_target_pairs={{0,8},{8,16},{16,24},{24,0},{1,9},{9,17},{17,25},{25,1},{2,10},{10... | collective-permute-start | bytes 196616 | tf_op jit(solution)/shard_map/ppermute | solution.py:27
  42.1 5.4 %collective-permute-start.8 = (f32[2,8192]{1,0:T(2,128)S(1)}, f32[2,8192]{1,0:T(2,128)S(1)}, u32[]{:S(2)}, u32[]{:S(2)}) collective-permute-start(f32[2,8192]{1,0:T(2,128)S(1)} %get-tuple-element.23), channel_id=1, source_target_pairs={{0,8},{8,16},{16,24},{24,0},{1,9},{9,17},{17,25},{25,1},{2,10},{10... | collective-permute-start | bytes 196616 | tf_op jit(solution)/shard_map/ppermute | solution.py:27
  48.3 1.3 %collective-permute-start.9 = (bf16[2,128,128]{2,1,0:T(8,128)(2,1)S(1)}, bf16[2,128,128]{2,1,0:T(8,128)(2,1)S(1)}, u32[]{:S(2)}, u32[]{:S(2)}) collective-permute-start(bf16[2,128,128]{2,1,0:T(8,128)(2,1)S(1)} %convert_element_type.88), channel_id=1, source_target_pairs={{0,1},{1,0},{2,3},{3,2},{4,5},{5,4},{6,7},{7,6},{8,9},{9,8},{10,11... | collective-permute-start | bytes 196616 | tf_op jit(solution)/shard_map/ppermute | solution.py:35
  49.7 4.3 %collective-permute-start.10 = (bf16[2,128,128]{2,1,0:T(8,128)(2,1)S(1)}, bf16[2,128,128]{2,1,0:T(8,128)(2,1)S(1)}, u32[]{:S(2)}, u32[]{:S(2)}) collective-permute-start(bf16[2,128,128]{2,1,0:T(8,128)(2,1)S(1)} %fusion.2), channel_id=1, source_target_pairs={{0,2},{1,3},{2,0},{3,1},{4,6},{5,7},{6,4},{7,5},{8,10},{9,11},{10,... | collective-permute-start | bytes 196616 | tf_op jit(solution)/shard_map/ppermute | solution.py:35
  54.0 5.3 %collective-permute-start.11 = (bf16[2,128,128]{2,1,0:T(8,128)(2,1)S(1)}, bf16[2,128,128]{2,1,0:T(8,128)(2,1)S(1)}, u32[]{:S(2)}, u32[]{:S(2)}) collective-permute-start(bf16[2,128,128]{2,1,0:T(8,128)(2,1)S(1)} %fusion.6), channel_id=1, source_target_pairs={{0,4},{1,5},{2,6},{3,7},{4,0},{5,1},{6,2},{7,3},{8,12},{9,13},{10,... | collective-permute-start | bytes 196616 | tf_op jit(solution)/shard_map/ppermute | solution.py:35
  54.5 5.2 %collective-permute-start.12 = (f32[2,8192]{1,0:T(2,128)S(1)}, f32[2,8192]{1,0:T(2,128)S(1)}, u32[]{:S(2)}, u32[]{:S(2)}) collective-permute-start(f32[2,8192]{1,0:T(2,128)S(1)} %get-tuple-element.27), channel_id=1, source_target_pairs={{0,8},{8,16},{16,24},{24,0},{1,9},{9,17},{17,25},{25,1},{2,10},{10... | collective-permute-start | bytes 196616 | tf_op jit(solution)/shard_map/ppermute | solution.py:27
  62.4 5.4 %collective-permute-start.13 = (f32[2,8192]{1,0:T(2,128)S(1)}, f32[2,8192]{1,0:T(2,128)S(1)}, u32[]{:S(2)}, u32[]{:S(2)}) collective-permute-start(f32[2,8192]{1,0:T(2,128)S(1)} %get-tuple-element.28), channel_id=1, source_target_pairs={{0,8},{8,16},{16,24},{24,0},{1,9},{9,17},{17,25},{25,1},{2,10},{10... | collective-permute-start | bytes 196616 | tf_op jit(solution)/shard_map/ppermute | solution.py:27
  68.7 0.7 copy-start.6
  68.8 1.3 %collective-permute-start.14 = (bf16[2,128,128]{2,1,0:T(8,128)(2,1)S(1)}, bf16[2,128,128]{2,1,0:T(8,128)(2,1)S(1)}, u32[]{:S(2)}, u32[]{:S(2)}) collective-permute-start(bf16[2,128,128]{2,1,0:T(8,128)(2,1)S(1)} %convert_element_type.94), channel_id=1, source_target_pairs={{0,1},{1,0},{2,3},{3,2},{4,5},{5,4},{6,7},{7,6},{8,9},{9,8},{10,11... | collective-permute-start | bytes 196616 | tf_op jit(solution)/shard_map/ppermute | solution.py:35
  70.1 4.3 %collective-permute-start.15 = (bf16[2,128,128]{2,1,0:T(8,128)(2,1)S(1)}, bf16[2,128,128]{2,1,0:T(8,128)(2,1)S(1)}, u32[]{:S(2)}, u32[]{:S(2)}) collective-permute-start(bf16[2,128,128]{2,1,0:T(8,128)(2,1)S(1)} %fusion.3), channel_id=1, source_target_pairs={{0,2},{1,3},{2,0},{3,1},{4,6},{5,7},{6,4},{7,5},{8,10},{9,11},{10,... | collective-permute-start | bytes 196616 | tf_op jit(solution)/shard_map/ppermute | solution.py:35
  74.5 5.2 %collective-permute-start.16 = (bf16[2,128,128]{2,1,0:T(8,128)(2,1)S(1)}, bf16[2,128,128]{2,1,0:T(8,128)(2,1)S(1)}, u32[]{:S(2)}, u32[]{:S(2)}) collective-permute-start(bf16[2,128,128]{2,1,0:T(8,128)(2,1)S(1)} %fusion.7), channel_id=1, source_target_pairs={{0,4},{1,5},{2,6},{3,7},{4,0},{5,1},{6,2},{7,3},{8,12},{9,13},{10,... | collective-permute-start | bytes 196616 | tf_op jit(solution)/shard_map/ppermute | solution.py:35
  83.8 12.7 %all-to-all-start = ((f32[4,32,4,128]{3,2,1,0:T(4,128)}), f32[4,32,4,128]{3,2,1,0:T(4,128)S(1)}, u32[]{:S(2)}, u32[]{:S(2)}) async-start(f32[4,32,4,128]{3,2,1,0:T(4,128)} %bitcast.3), calls=%async_computation | async-start | bytes 524288 | tf_op jit(solution)/shard_map/all_to_all | solution.py:211
  87.2 6.7 %collective-permute-start.17 = (f32[2,8192]{1,0:T(2,128)S(1)}, f32[2,8192]{1,0:T(2,128)S(1)}, u32[]{:S(2)}, u32[]{:S(2)}) collective-permute-start(f32[2,8192]{1,0:T(2,128)S(1)} %get-tuple-element.35), channel_id=1, source_target_pairs={{0,8},{8,16},{16,24},{24,0},{1,9},{9,17},{17,25},{25,1},{2,10},{10... | collective-permute-start | bytes 196616 | tf_op jit(solution)/shard_map/ppermute | solution.py:27
where the time goes:
time: 97.4 us; the launch traced here: 97.2 us
  waiting for transfers between devices  35.6 us (37%)
  starting transfers between devices  28.7 us (29%)
  Pallas kernels  28.2 us (29%)
  local copies, waits for them, and re-layouts  3.1 us (3%)
    ppermute x12, waiting for transfers between devices, summed(): lax.ppermute(value.astype(jnp.bfloat16), axis, pairs).astype(jnp.float32)  23.9 us
    ppermute x12, starting transfers between devices, summed(): lax.ppermute(value.astype(jnp.bfloat16), axis, pairs).astype(jnp.float32)  18.7 us
    ppermute x6, waiting for transfers between devices, shifted(): return lax.ppermute(value, axis, pairs)  11.6 us
    pallas_call x3, Pallas kernels, shards(): resident, part = local(resident_kernel, (whole, density))(other, resident)  9.15 us
    pallas_call x3, Pallas kernels, shards(): local(functools.partial(opposing_kernel, scale, len(opposing) == 2), (hal...  8.33 us
    ppermute x6, starting transfers between devices, shifted(): return lax.ppermute(value, axis, pairs)  6.67 us
    pallas_call x1, Pallas kernels, shards(): local(functools.partial(last_kernel, scale), (array(stations * capacity,...  4.04 us
    all_to_all x1, starting transfers between devices, shards(): lax.all_to_all(outgoing, 'station', split_axis=0, concat_axis=0, tiled=True)  3.41 us
  transfers between devices with their start and end apart: 19, of which 18 were waited for; matrix products, arithmetic and copies ran while one was open for 0% of the time, Pallas kernels for 12%

commit v1 on v0

--- a/solution.py
+++ b/solution.py
@@ -6,6 +6,7 @@
 from jax.experimental import pallas as pl
 from jax.experimental.pallas import tpu as pltpu
 from jax.sharding import PartitionSpec as P
+
 
 GRID = 128
 FRONTS = 4
@@ -58,15 +59,20 @@
     return jnp.concatenate(parts, axis=0)
 
 
-def deposit(x, y):
+def weigh(x, y, hats_ref, tile):
+    hats_ref[:GRID, tile] = hat_table(x)
+    hats_ref[GRID:, tile] = hat_table(y)
     return lax.dot_general(
-        hat_table(y), hat_table(x), (((1,), (1,)), ((), ())), preferred_element_type=jnp.float32
-    )
-
-
-def kick(x, moment_x, y, moment_y, table):
-    sampled = jnp.dot(table, hat_table(x), preferred_element_type=jnp.float32)
-    weight_y = hat_table(y).astype(jnp.float32)
+        hats_ref[GRID:, tile],
+        hats_ref[:GRID, tile],
+        (((1,), (1,)), ((), ())),
+        preferred_element_type=jnp.float32,
+    )
+
+
+def kick(x, moment_x, y, moment_y, hats_ref, tile, table):
+    sampled = jnp.dot(table, hats_ref[:GRID, tile], preferred_element_type=jnp.float32)
+    weight_y = hats_ref[GRID:, tile].astype(jnp.float32)
     moment_x = moment_x - jnp.sum(sampled[:GRID] * weight_y, axis=0, keepdims=True)
     moment_y = moment_y - jnp.sum(sampled[GRID:] * weight_y, axis=0, keepdims=True)
     return x + DRIFT * moment_x, moment_x, y + DRIFT * moment_y, moment_y
@@ -91,67 +97,77 @@
     return [pl.ds(start, width) for start in range(0, count, width)]
 
 
-def first_kernel(resident_ref, opposing_ref, density_ref):
-    for which, ref in enumerate((resident_ref, opposing_ref)):
+def first_kernel(*refs):
+    sources, held, (density_ref, *hats), landed = refs[:4], refs[4:8], refs[8:11], refs[11]
+    copies = [
+        pltpu.make_async_copy(source, place, landed.at[which])
+        for which, (source, place) in enumerate(zip(sources, held))
+    ]
+    for copy in copies:
+        copy.start()
+    for which in range(2):
+        copies[which].wait()
+        beam = held[which]
         density_ref[which] = sum(
-            deposit(ref[0:1, tile], ref[2:3, tile]) for tile in columns(ref.shape[1])
+            weigh(beam[0:1, tile], beam[2:3, tile], hats[which], tile)
+            for tile in columns(beam.shape[1])
         )
-
-
-def opposing_kernel(scale, split, density_ref, smooth_ref, slope_ref, *refs):
+    for copy in copies[2:]:
+        copy.wait()
+
+
+def rows(sources, tile):
+    if len(sources) == 1:
+        return [sources[0][row : row + 1, tile] for row in range(4)]
+    return [sources[row % 2][row // 2 : row // 2 + 1, tile] for row in range(4)]
+
+
+def opposing_kernel(scale, density_ref, smooth_ref, slope_ref, hats_ref, *refs):
     own, other = tables(density_ref[...], smooth_ref[...], slope_ref[...], scale)
     *sources, place_ref, moment_ref, table_ref = refs
     table_ref[...] = other
     for tile in columns(place_ref.shape[1]):
-        if split:
-            x, y = (sources[0][row : row + 1, tile] for row in range(2))
-            moment_x, moment_y = (sources[1][row : row + 1, tile] for row in range(2))
-        else:
-            x, moment_x, y, moment_y = (sources[0][row : row + 1, tile] for row in range(4))
-        x, moment_x, y, moment_y = kick(x, moment_x, y, moment_y, own)
+        x, moment_x, y, moment_y = kick(*rows(sources, tile), hats_ref, tile, own)
         place_ref[0:1, tile] = x
         place_ref[1:2, tile] = y
         moment_ref[0:1, tile] = moment_x
         moment_ref[1:2, tile] = moment_y
 
 
-def resident_kernel(table_ref, beam_ref, moved_ref, density_ref):
+def resident_kernel(table_ref, hats_ref, beam_ref, moved_ref, density_ref, new_hats_ref):
     total = 0.0
     for tile in columns(beam_ref.shape[1]):
-        new = kick(*(beam_ref[row : row + 1, tile] for row in range(4)), table_ref[...])
+        new = kick(*rows([beam_ref], tile), hats_ref, tile, table_ref[...])
         for row in range(4):
             moved_ref[row : row + 1, tile] = new[row]
-        total = total + deposit(new[0], new[2])
+        total = total + weigh(new[0], new[2], new_hats_ref, tile)
     density_ref[...] = total
 
 
-def arrival_kernel(place_ref, resident_ref, density_ref):
+def arrival_kernel(place_ref, resident_ref, density_ref, hats_ref):
     density_ref[0] = resident_ref[...]
     density_ref[1] = sum(
-        deposit(place_ref[0:1, tile], place_ref[1:2, tile]) for tile in columns(place_ref.shape[1])
-    )
-
-
-def last_kernel(scale, slots_ref, density_ref, smooth_ref, slope_ref, beam_ref, packed_ref, table_ref, moved_ref):
+        weigh(place_ref[0:1, tile], place_ref[1:2, tile], hats_ref, tile)
+        for tile in columns(place_ref.shape[1])
+    )
+
+
+def last_kernel(scale, slots_ref, density_ref, smooth_ref, slope_ref, hats_ref, beam_ref, packed_ref, table_ref, moved_ref):
     table_ref[...], other = tables(density_ref[...], smooth_ref[...], slope_ref[...], scale)
     packed_ref[...] = jnp.zeros_like(packed_ref)
     for tile in columns(beam_ref.shape[1]):
-        new = kick(*(beam_ref[row : row + 1, tile] for row in range(4)), other)
+        new = kick(*rows([beam_ref], tile), hats_ref, tile, other)
         for row in range(4):
             moved_ref[row : row + 1, tile] = new[row]
     for block in range(beam_ref.shape[1] // BLOCK):
         packed_ref[slots_ref[block]] = moved_ref[:, block * BLOCK : (block + 1) * BLOCK]
 
 
-def final_kernel(table_ref, place_ref, moment_ref, out_ref):
+def final_kernel(table_ref, place_ref, moment_ref, out_ref, hats_ref):
     for tile in columns(place_ref.shape[1]):
-        new = kick(
-            place_ref[0:1, tile],
-            moment_ref[0:1, tile],
-            place_ref[1:2, tile],
-            moment_ref[1:2, tile],
-            table_ref[...],
-        )
+        hats_ref[:GRID, tile] = hat_table(place_ref[0:1, tile])
+        hats_ref[GRID:, tile] = hat_table(place_ref[1:2, tile])
+        new = kick(*rows([place_ref, moment_ref], tile), hats_ref, tile, table_ref[...])
         for row in range(4):
             out_ref[row : row + 1, tile] = new[row]
 
@@ -169,10 +185,18 @@
     return jax.ShapeDtypeStruct(shape, dtype)
 
 
-def slots(routes, stations, capacity):
-    onehot = (routes[:, None] == jnp.arange(stations, dtype=jnp.int32)[None, :]).astype(jnp.int32)
-    ranking = jnp.sum((jnp.cumsum(onehot, axis=0) - onehot) * onehot, axis=1)
-    return routes * capacity + jnp.minimum(ranking, capacity - 1)
+def slots_kernel(capacity, routes_ref, slots_ref, taken_ref):
+    for station in range(taken_ref.shape[0]):
+        taken_ref[station] = 0
+
+    def place(block, carry):
+        station = routes_ref[block]
+        taken = taken_ref[station]
+        slots_ref[block] = station * capacity + jnp.minimum(taken, capacity - 1)
+        taken_ref[station] = taken + 1
+        return carry
+
+    lax.fori_loop(0, routes_ref.shape[0], place, 0)
 
 
 def shards(beam_first, beam_second, green_smooth, green_slope, destination):
@@ -187,29 +211,53 @@
     half, whole = array(2, count), array(4, count)
     density, densities = array(GRID, GRID), array(2, GRID, GRID)
     table = array(2 * GRID, GRID, dtype=jnp.bfloat16)
-    place = slots(destination[0, :, 0].astype(jnp.int32), stations, capacity)
-
-    total = local(first_kernel, densities)(resident, opposing[0])
+    hats = array(2 * GRID, count, dtype=jnp.bfloat16)
+    vmem, smem = (pl.BlockSpec(memory_space=space) for space in (pltpu.VMEM, pltpu.SMEM))
+    place = local(
+        functools.partial(slots_kernel, capacity),
+        array(block_count, dtype=jnp.int32),
+        in_specs=[smem],
+        out_specs=smem,
+        scratch_shapes=[pltpu.SMEM((stations,), jnp.int32)],
+    )(destination[0, :, 0])
+
+    arguments = (resident, opposing[0], green_smooth, green_slope)
+    resident, *opposing, smooth, slope, total, resident_hats, opposing_hats = local(
+        first_kernel,
+        (whole, whole, density, density, densities, hats, hats),
+        in_specs=[pl.BlockSpec(memory_space=pltpu.HBM)] * 4,
+        out_specs=(vmem,) * 7,
+        scratch_shapes=[pltpu.SemaphoreType.DMA((4,))],
+    )(*(pltpu.with_memory_space_constraint(value, pltpu.HBM) for value in arguments))
     for front_index in range(FRONTS - 1):
         total = summed(total, "dom")
         positions, moments, other = local(
-            functools.partial(opposing_kernel, scale, len(opposing) == 2), (half, half, table)
-        )(total, green_smooth, green_slope, *opposing)
-        opposing = (shifted(positions, "station", 1), shifted(moments, "station", 1))
-        resident, part = local(resident_kernel, (whole, density))(other, resident)
-        total = local(arrival_kernel, densities)(opposing[0], part)
+            functools.partial(opposing_kernel, scale), (half, half, table)
+        )(total, smooth, slope, opposing_hats, *opposing)
+        positions = shifted(positions, "station", 1)
+        moments = shifted(moments, "station", 1)
+        opposing = (positions, moments)
+        resident, part, resident_hats = local(resident_kernel, (whole, density, hats))(
+            other, resident_hats, resident
+        )
+        last = front_index + 2 == FRONTS
+        total, *kept = local(
+            arrival_kernel,
+            (densities,) if last else (densities, hats),
+            scratch_shapes=[pltpu.VMEM(hats.shape, hats.dtype)] if last else [],
+        )(positions, part)
+        opposing_hats = None if last else kept[0]
     total = summed(total, "dom")
-    vmem = pl.BlockSpec(memory_space=pltpu.VMEM)
     outgoing, own = local(
         functools.partial(last_kernel, scale),
         (array(stations * capacity, 4, BLOCK), table),
-        in_specs=[pl.BlockSpec(memory_space=pltpu.SMEM)] + [vmem] * 4,
+        in_specs=[smem] + [vmem] * 5,
         out_specs=(vmem, vmem),
         scratch_shapes=[pltpu.VMEM((4, count), jnp.float32)],
-    )(place, total, green_smooth, green_slope, resident)
+    )(place, total, smooth, slope, resident_hats, resident)
     outgoing = outgoing.reshape(stations, capacity, 4, BLOCK)
     arrived = lax.all_to_all(outgoing, "station", split_axis=0, concat_axis=0, tiled=True)
-    opposing = local(final_kernel, whole)(own, *opposing)
+    opposing = local(final_kernel, whole, scratch_shapes=[pltpu.VMEM(hats.shape, hats.dtype)])(own, *opposing)
     return (arrived[None, None], opposing[None, None])
 
 

time: 97.4 us -> 95.5 us (0.980)
  local copies, waits for them, and re-layouts: 3.1 us -> 0.71 us
  Pallas kernels: 28.2 us -> 29.4 us
  starting transfers between devices: 28.7 us -> 27.7 us
    unnamed x15 -> x3, local copies, waits for them, and re-layouts: 3.1 us -> 0.71 us
    pallas_call x11 -> x12, Pallas kernels: 24.2 us -> 25.8 us  [the longest x3 8.34 us: shards(): local(resident_kernel, (whole, density, hats))]
    ppermute x6, waiting for transfers between devices: 11.6 us -> 12.7 us  [shifted(): return lax.ppermute(value, axis, pairs)]
    ppermute x6, starting transfers between devices: 6.67 us -> 5.63 us  [shifted(): return lax.ppermute(value, axis, pairs)]
  transfers between devices with their start and end apart: 19 -> 19, of which waited for: 18 -> 18; matrix products, arithmetic and copies ran while one was open for 0% -> 0% of each run, Pallas kernels for 12% -> 13%
where the time goes in v1:
time: 95.5 us; the launch traced here: 95.3 us
  waiting for transfers between devices  36.4 us (38%)
  Pallas kernels  29.4 us (31%)
  starting transfers between devices  27.7 us (29%)
    ppermute x12, waiting for transfers between devices, summed(): lax.ppermute(value.astype(jnp.bfloat16), axis, pairs).astype(jnp.float32)  23.7 us
    ppermute x12, starting transfers between devices, summed(): lax.ppermute(value.astype(jnp.bfloat16), axis, pairs).astype(jnp.float32)  18.7 us
    ppermute x6, waiting for transfers between devices, shifted(): return lax.ppermute(value, axis, pairs)  12.7 us
    pallas_call x3, Pallas kernels, shards(): local(resident_kernel, (whole, density, hats))  8.34 us
    pallas_call x3, Pallas kernels, shards(): local(functools.partial(opposing_kernel, scale), (half, half, table))  6.85 us
    ppermute x6, starting transfers between devices, shifted(): return lax.ppermute(value, axis, pairs)  5.63 us
    pallas_call x1, Pallas kernels, shards(): local(functools.partial(last_kernel, scale), (array(stations * capacity,...  3.57 us
    pallas_call x1, Pallas kernels, shards(): local(first_kernel, (whole, whole, density, density, densities, hats, hat...  3.42 us
  transfers between devices with their start and end apart: 19, of which 18 were waited for; matrix products, arithmetic and copies ran while one was open for 0% of the time, Pallas kernels for 13%

profile of v1, /device:TPU:0, one launch (start us, length us, event | category | flops | bytes accessed | tf_op | source)
XLA Modules:
  0.0 95.3 jit_solution(1165326300795015484)
XLA Ops:
  0.6 3.4 %shard_map.69 = (f32[4,8192]{1,0:T(4,128)S(1)}, f32[4,8192]{1,0:T(4,128)S(1)}, f32[128,128]{1,0:T(8,128)S(1)}, f32[128,128]{1,0:T(8,128)S(1)}, f32[2,128,128]{2,...) custom-call(f32[4,8192]{1,0:T(4,128)} %bitcast.8, f32[4,8192]{1,0:T(4,128)} %bitcast.9, ...), custom_call_target="tpu_custom_call" | custom-call | tf_op jit(solution)/shard_map/pallas_call | solution.py:225
  4.1 0.6 collective-permute-start
  4.6 0.9 collective-permute-done
  5.6 3.0 %collective-permute-start.1 = (bf16[2,128,128]{2,1,0:T(8,128)(2,1)S(1)}, bf16[2,128,128]{2,1,0:T(8,128)(2,1)S(1)}, u32[]{:S(2)}, u32[]{:S(2)}) collective-permute-start(bf16[2,128,128]{2,1,0:T(8,128)(2,1)S(1)} %fusion), channel_id=1, source_target_pairs={{0,2},{1,3},{2,0},{3,1},{4,6},{5,7},{6,4},{7,5},{8,10},{9,11},{10,... | collective-permute-start | bytes 196616 | tf_op jit(solution)/shard_map/ppermute | solution.py:36
  8.5 2.4 %collective-permute-done.1 = bf16[2,128,128]{2,1,0:T(8,128)(2,1)S(1)} collective-permute-done((bf16[2,128,128]{2,1,0:T(8,128)(2,1)S(1)}, bf16[2,128,128]{2,1,0:T(8,128)(2,1)S(1)}, u32[]{:S(2)}, u32[]{:S(2)}) %collective-permute-start.1) | collective-permute-done | bytes 65568 | tf_op jit(solution)/shard_map/ppermute | solution.py:36
  11.0 2.9 %collective-permute-start.2 = (bf16[2,128,128]{2,1,0:T(8,128)(2,1)S(1)}, bf16[2,128,128]{2,1,0:T(8,128)(2,1)S(1)}, u32[]{:S(2)}, u32[]{:S(2)}) collective-permute-start(bf16[2,128,128]{2,1,0:T(8,128)(2,1)S(1)} %fusion.4), channel_id=1, source_target_pairs={{0,4},{1,5},{2,6},{3,7},{4,0},{5,1},{6,2},{7,3},{8,12},{9,13},{10,... | collective-permute-start | bytes 196616 | tf_op jit(solution)/shard_map/ppermute | solution.py:36
  13.9 2.3 %collective-permute-done.2 = bf16[2,128,128]{2,1,0:T(8,128)(2,1)S(1)} collective-permute-done((bf16[2,128,128]{2,1,0:T(8,128)(2,1)S(1)}, bf16[2,128,128]{2,1,0:T(8,128)(2,1)S(1)}, u32[]{:S(2)}, u32[]{:S(2)}) %collective-permute-start.2) | collective-permute-done | bytes 65568 | tf_op jit(solution)/shard_map/ppermute | solution.py:36
  16.3 2.3 %shard_map.70 = (f32[2,8192]{1,0:T(2,128)S(1)}, f32[2,8192]{1,0:T(2,128)S(1)}, bf16[256,128]{1,0:T(8,128)(2,1)S(1)}) custom-call(f32[2,128,128]{2,1,0:T(8,128)S(1)} %convert_add_fusion.9.density_ref, f32[128,128]{1,0:T(8,128)S(1)} %get-tuple-element.34.smooth_ref, f32[128,128]{1,0:T(8,128)S(1)} %get-tuple-element.35.slope_ref, ...), custom_call_target="tpu_custom_call" | custom-call | tf_op jit(solution)/shard_map/pallas_call | solution.py:234
  18.6 1.8 %collective-permute-start.3 = (f32[2,8192]{1,0:T(2,128)S(1)}, f32[2,8192]{1,0:T(2,128)S(1)}, u32[]{:S(2)}, u32[]{:S(2)}) collective-permute-start(f32[2,8192]{1,0:T(2,128)S(1)} %get-tuple-element.38), channel_id=1, source_target_pairs={{0,8},{8,16},{16,24},{24,0},{1,9},{9,17},{17,25},{25,1},{2,10},{10... | collective-permute-start | bytes 196616 | tf_op jit(solution)/shard_map/ppermute | solution.py:28
  20.4 2.8 %shard_map.71 = (f32[4,8192]{1,0:T(4,128)S(1)}, f32[128,128]{1,0:T(8,128)S(1)}, bf16[256,8192]{1,0:T(8,128)(2,1)S(1)}) custom-call(bf16[256,128]{1,0:T(8,128)(2,1)S(1)} %get-tuple-element.39.table_ref, bf16[256,8192]{1,0:T(8,128)(2,1)S(1)} %get-tuple-element.40.hats_ref, f32[4,8192]{1,0:T(4,128)S(1)} %get-tuple-element.41.beam_ref), custom_call_target="tpu_custom_call" | custom-call | tf_op jit(solution)/shard_map/pallas_call | solution.py:240
  23.1 0.6 collective-permute-done.3.place_ref.refs_0_
  23.8 1.0 %shard_map.72 = (f32[2,128,128]{2,1,0:T(8,128)S(1)}, bf16[256,8192]{1,0:T(8,128)(2,1)S(1)}) custom-call(f32[2,8192]{1,0:T(2,128)S(1)} %collective-permute-done.3.place_ref.refs_0_, f32[128,128]{1,0:T(8,128)S(1)} %get-tuple-element.42.resident_ref), custom_call_target="tpu_custom_call" | custom-call | tf_op jit(solution)/shard_map/pallas_call | solution.py:244
  24.9 1.2 %collective-permute-done.4 = bf16[2,128,128]{2,1,0:T(8,128)(2,1)S(1)} collective-permute-done((bf16[2,128,128]{2,1,0:T(8,128)(2,1)S(1)}, bf16[2,128,128]{2,1,0:T(8,128)(2,1)S(1)}, u32[]{:S(2)}, u32[]{:S(2)}) %collective-permute-start.4) | collective-permute-done | bytes 65568 | tf_op jit(solution)/shard_map/ppermute | solution.py:36
  26.1 1.9 %collective-permute-start.5 = (bf16[2,128,128]{2,1,0:T(8,128)(2,1)S(1)}, bf16[2,128,128]{2,1,0:T(8,128)(2,1)S(1)}, u32[]{:S(2)}, u32[]{:S(2)}) collective-permute-start(bf16[2,128,128]{2,1,0:T(8,128)(2,1)S(1)} %fusion.1), channel_id=1, source_target_pairs={{0,2},{1,3},{2,0},{3,1},{4,6},{5,7},{6,4},{7,5},{8,10},{9,11},{10,... | collective-permute-start | bytes 196616 | tf_op jit(solution)/shard_map/ppermute | solution.py:36
  28.0 2.4 %collective-permute-done.5 = bf16[2,128,128]{2,1,0:T(8,128)(2,1)S(1)} collective-permute-done((bf16[2,128,128]{2,1,0:T(8,128)(2,1)S(1)}, bf16[2,128,128]{2,1,0:T(8,128)(2,1)S(1)}, u32[]{:S(2)}, u32[]{:S(2)}) %collective-permute-start.5) | collective-permute-done | bytes 65568 | tf_op jit(solution)/shard_map/ppermute | solution.py:36
  30.5 3.2 %collective-permute-start.6 = (bf16[2,128,128]{2,1,0:T(8,128)(2,1)S(1)}, bf16[2,128,128]{2,1,0:T(8,128)(2,1)S(1)}, u32[]{:S(2)}, u32[]{:S(2)}) collective-permute-start(bf16[2,128,128]{2,1,0:T(8,128)(2,1)S(1)} %fusion.5), channel_id=1, source_target_pairs={{0,4},{1,5},{2,6},{3,7},{4,0},{5,1},{6,2},{7,3},{8,12},{9,13},{10,... | collective-permute-start | bytes 196616 | tf_op jit(solution)/shard_map/ppermute | solution.py:36
  33.7 0.6 collective-permute-start.7
  34.3 1.9 %collective-permute-done.6 = bf16[2,128,128]{2,1,0:T(8,128)(2,1)S(1)} collective-permute-done((bf16[2,128,128]{2,1,0:T(8,128)(2,1)S(1)}, bf16[2,128,128]{2,1,0:T(8,128)(2,1)S(1)}, u32[]{:S(2)}, u32[]{:S(2)}) %collective-permute-start.6) | collective-permute-done | bytes 65568 | tf_op jit(solution)/shard_map/ppermute | solution.py:36
  36.3 2.6 %collective-permute-done.7.refs_1_ = f32[2,8192]{1,0:T(2,128)S(1)} collective-permute-done((f32[2,8192]{1,0:T(2,128)S(1)}, f32[2,8192]{1,0:T(2,128)S(1)}, u32[]{:S(2)}, u32[]{:S(2)}) %collective-permute-start.7) | collective-permute-done | bytes 65568 | tf_op jit(solution)/shard_map/ppermute | solution.py:28
  38.9 2.3 %shard_map.73 = (f32[2,8192]{1,0:T(2,128)S(1)}, f32[2,8192]{1,0:T(2,128)S(1)}, bf16[256,128]{1,0:T(8,128)(2,1)S(1)}) custom-call(f32[2,128,128]{2,1,0:T(8,128)S(1)} %convert_add_fusion.6.density_ref, f32[128,128]{1,0:T(8,128)S(1)} %get-tuple-element.34.smooth_ref, f32[128,128]{1,0:T(8,128)S(1)} %get-tuple-element.35.slope_ref, ...), custom_call_target="tpu_custom_call" | custom-call | tf_op jit(solution)/shard_map/pallas_call | solution.py:234
  41.2 0.2 collective-permute-start.8
  41.4 2.8 %shard_map.74 = (f32[4,8192]{1,0:T(4,128)S(1)}, f32[128,128]{1,0:T(8,128)S(1)}, bf16[256,8192]{1,0:T(8,128)(2,1)S(1)}) custom-call(bf16[256,128]{1,0:T(8,128)(2,1)S(1)} %get-tuple-element.47.table_ref, bf16[256,8192]{1,0:T(8,128)(2,1)S(1)} %get-tuple-element.48.hats_ref, f32[4,8192]{1,0:T(4,128)S(1)} %get-tuple-element.49.beam_ref), custom_call_target="tpu_custom_call" | custom-call | tf_op jit(solution)/shard_map/pallas_call | solution.py:240
  44.2 2.4 %collective-permute-done.8.place_ref.refs_0_ = f32[2,8192]{1,0:T(2,128)S(1)} collective-permute-done((f32[2,8192]{1,0:T(2,128)S(1)}, f32[2,8192]{1,0:T(2,128)S(1)}, u32[]{:S(2)}, u32[]{:S(2)}) %collective-permute-start.8) | collective-permute-done | bytes 65568 | tf_op jit(solution)/shard_map/ppermute | solution.py:28
  46.6 1.0 %shard_map.75 = (f32[2,128,128]{2,1,0:T(8,128)S(1)}, bf16[256,8192]{1,0:T(8,128)(2,1)S(1)}) custom-call(f32[2,8192]{1,0:T(2,128)S(1)} %collective-permute-done.8.place_ref.refs_0_, f32[128,128]{1,0:T(8,128)S(1)} %get-tuple-element.50.resident_ref), custom_call_target="tpu_custom_call" | custom-call | tf_op jit(solution)/shard_map/pallas_call | solution.py:244
  47.6 1.2 %collective-permute-done.9 = bf16[2,128,128]{2,1,0:T(8,128)(2,1)S(1)} collective-permute-done((bf16[2,128,128]{2,1,0:T(8,128)(2,1)S(1)}, bf16[2,128,128]{2,1,0:T(8,128)(2,1)S(1)}, u32[]{:S(2)}, u32[]{:S(2)}) %collective-permute-start.9) | collective-permute-done | bytes 65568 | tf_op jit(solution)/shard_map/ppermute | solution.py:36
  48.9 1.9 %collective-permute-start.10 = (bf16[2,128,128]{2,1,0:T(8,128)(2,1)S(1)}, bf16[2,128,128]{2,1,0:T(8,128)(2,1)S(1)}, u32[]{:S(2)}, u32[]{:S(2)}) collective-permute-start(bf16[2,128,128]{2,1,0:T(8,128)(2,1)S(1)} %fusion.2), channel_id=1, source_target_pairs={{0,2},{1,3},{2,0},{3,1},{4,6},{5,7},{6,4},{7,5},{8,10},{9,11},{10,... | collective-permute-start | bytes 196616 | tf_op jit(solution)/shard_map/ppermute | solution.py:36
  50.8 2.4 %collective-permute-done.10 = bf16[2,128,128]{2,1,0:T(8,128)(2,1)S(1)} collective-permute-done((bf16[2,128,128]{2,1,0:T(8,128)(2,1)S(1)}, bf16[2,128,128]{2,1,0:T(8,128)(2,1)S(1)}, u32[]{:S(2)}, u32[]{:S(2)}) %collective-permute-start.10) | collective-permute-done | bytes 65568 | tf_op jit(solution)/shard_map/ppermute | solution.py:36
  53.3 0.4 collective-permute-start.11
  53.7 0.6 collective-permute-start.12
  54.3 4.2 %collective-permute-done.11 = bf16[2,128,128]{2,1,0:T(8,128)(2,1)S(1)} collective-permute-done((bf16[2,128,128]{2,1,0:T(8,128)(2,1)S(1)}, bf16[2,128,128]{2,1,0:T(8,128)(2,1)S(1)}, u32[]{:S(2)}, u32[]{:S(2)}) %collective-permute-start.11) | collective-permute-done | bytes 65568 | tf_op jit(solution)/shard_map/ppermute | solution.py:36
  58.6 0.3 collective-permute-done.12.refs_1_
  58.9 2.3 %shard_map.76 = (f32[2,8192]{1,0:T(2,128)S(1)}, f32[2,8192]{1,0:T(2,128)S(1)}, bf16[256,128]{1,0:T(8,128)(2,1)S(1)}) custom-call(f32[2,128,128]{2,1,0:T(8,128)S(1)} %convert_add_fusion.3.density_ref, f32[128,128]{1,0:T(8,128)S(1)} %get-tuple-element.34.smooth_ref, f32[128,128]{1,0:T(8,128)S(1)} %get-tuple-element.35.slope_ref, ...), custom_call_target="tpu_custom_call" | custom-call | tf_op jit(solution)/shard_map/pallas_call | solution.py:234
  61.2 0.4 collective-permute-start.13
  61.5 2.8 %shard_map.77 = (f32[4,8192]{1,0:T(4,128)S(1)}, f32[128,128]{1,0:T(8,128)S(1)}, bf16[256,8192]{1,0:T(8,128)(2,1)S(1)}) custom-call(bf16[256,128]{1,0:T(8,128)(2,1)S(1)} %get-tuple-element.55.table_ref, bf16[256,8192]{1,0:T(8,128)(2,1)S(1)} %get-tuple-element.56.hats_ref, f32[4,8192]{1,0:T(4,128)S(1)} %get-tuple-element.57.beam_ref), custom_call_target="tpu_custom_call" | custom-call | tf_op jit(solution)/shard_map/pallas_call | solution.py:240
  64.3 2.0 %collective-permute-done.13.place_ref = f32[2,8192]{1,0:T(2,128)S(1)} collective-permute-done((f32[2,8192]{1,0:T(2,128)S(1)}, f32[2,8192]{1,0:T(2,128)S(1)}, u32[]{:S(2)}, u32[]{:S(2)}) %collective-permute-start.13) | collective-permute-done | bytes 65568 | tf_op jit(solution)/shard_map/ppermute | solution.py:28
  66.4 0.9 shard_map.78
  67.3 1.2 %collective-permute-done.14 = bf16[2,128,128]{2,1,0:T(8,128)(2,1)S(1)} collective-permute-done((bf16[2,128,128]{2,1,0:T(8,128)(2,1)S(1)}, bf16[2,128,128]{2,1,0:T(8,128)(2,1)S(1)}, u32[]{:S(2)}, u32[]{:S(2)}) %collective-permute-start.14) | collective-permute-done | bytes 65568 | tf_op jit(solution)/shard_map/ppermute | solution.py:36
  68.6 1.9 %collective-permute-start.15 = (bf16[2,128,128]{2,1,0:T(8,128)(2,1)S(1)}, bf16[2,128,128]{2,1,0:T(8,128)(2,1)S(1)}, u32[]{:S(2)}, u32[]{:S(2)}) collective-permute-start(bf16[2,128,128]{2,1,0:T(8,128)(2,1)S(1)} %fusion.3), channel_id=1, source_target_pairs={{0,2},{1,3},{2,0},{3,1},{4,6},{5,7},{6,4},{7,5},{8,10},{9,11},{10,... | collective-permute-start | bytes 196616 | tf_op jit(solution)/shard_map/ppermute | solution.py:36
  70.5 2.4 %collective-permute-done.15 = bf16[2,128,128]{2,1,0:T(8,128)(2,1)S(1)} collective-permute-done((bf16[2,128,128]{2,1,0:T(8,128)(2,1)S(1)}, bf16[2,128,128]{2,1,0:T(8,128)(2,1)S(1)}, u32[]{:S(2)}, u32[]{:S(2)}) %collective-permute-start.15) | collective-permute-done | bytes 65568 | tf_op jit(solution)/shard_map/ppermute | solution.py:36
  73.0 2.6 %collective-permute-start.16 = (bf16[2,128,128]{2,1,0:T(8,128)(2,1)S(1)}, bf16[2,128,128]{2,1,0:T(8,128)(2,1)S(1)}, u32[]{:S(2)}, u32[]{:S(2)}) collective-permute-start(bf16[2,128,128]{2,1,0:T(8,128)(2,1)S(1)} %fusion.7), channel_id=1, source_target_pairs={{0,4},{1,5},{2,6},{3,7},{4,0},{5,1},{6,2},{7,3},{8,12},{9,13},{10,... | collective-permute-start | bytes 196616 | tf_op jit(solution)/shard_map/ppermute | solution.py:36
  75.6 1.7 %shard_map.68.slots_ref = s32[64]{0:T(128)S(1)} custom-call(s32[64]{0:T(128)S(1)} %bitcast.6), custom_call_target="tpu_custom_call" | custom-call | tf_op jit(solution)/shard_map/pallas_call | solution.py:216
  77.3 0.9 collective-permute-done.16
  78.3 3.6 %shard_map.79 = (f32[128,4,128]{2,1,0:T(4,128)}, bf16[256,128]{1,0:T(8,128)(2,1)S(1)}) custom-call(s32[64]{0:T(128)S(1)} %shard_map.68.slots_ref, f32[2,128,128]{2,1,0:T(8,128)S(1)} %convert_add_fusion.density_ref, f32[128,128]{1,0:T(8,128)S(1)} %get-tuple-element.34.smooth_ref, f32[128,128]{1,0:T(8,128)S(1)} %get-tuple-element.35.slope_ref, ...), custom_call_target="tpu_custom_call" | custom-call | tf_op jit(solution)/shard_map/pallas_call | solution.py:251
  81.8 3.4 %all-to-all-start = ((f32[4,32,4,128]{3,2,1,0:T(4,128)}), f32[4,32,4,128]{3,2,1,0:T(4,128)S(1)}, u32[]{:S(2)}, u32[]{:S(2)}) async-start(f32[4,32,4,128]{3,2,1,0:T(4,128)} %bitcast.3), calls=%async_computation | async-start | bytes 524288 | tf_op jit(solution)/shard_map/all_to_all | solution.py:259
  85.2 2.0 %collective-permute-start.17 = (f32[2,8192]{1,0:T(2,128)S(1)}, f32[2,8192]{1,0:T(2,128)S(1)}, u32[]{:S(2)}, u32[]{:S(2)}) collective-permute-start(f32[2,8192]{1,0:T(2,128)S(1)} %get-tuple-element.63), channel_id=1, source_target_pairs={{0,8},{8,16},{16,24},{24,0},{1,9},{9,17},{17,25},{25,1},{2,10},{10... | collective-permute-start | bytes 196616 | tf_op jit(solution)/shard_map/ppermute | solution.py:28
  87.2 4.8 %collective-permute-done.17.moment_ref = f32[2,8192]{1,0:T(2,128)S(1)} collective-permute-done((f32[2,8192]{1,0:T(2,128)S(1)}, f32[2,8192]{1,0:T(2,128)S(1)}, u32[]{:S(2)}, u32[]{:S(2)}) %collective-permute-start.17) | collective-permute-done | bytes 65568 | tf_op jit(solution)/shard_map/ppermute | solution.py:28
  92.0 2.6 %shard_map.80 = f32[4,8192]{1,0:T(4,128)} custom-call(bf16[256,128]{1,0:T(8,128)(2,1)S(1)} %get-tuple-element.62.table_ref, f32[2,8192]{1,0:T(2,128)S(1)} %collective-permute-done.13.place_ref, f32[2,8192]{1,0:T(2,128)S(1)} %collective-permute-done.17.moment_ref), custom_call_target="tpu_custom_call" | custom-call | tf_op jit(solution)/shard_map/pallas_call | solution.py:260
  94.6 0.7 copy.8
  (22 shorter events, 0.6 us)
Async XLA Ops:
  4.1 1.5 %collective-permute-start = (bf16[2,128,128]{2,1,0:T(8,128)(2,1)S(1)}, bf16[2,128,128]{2,1,0:T(8,128)(2,1)S(1)}, u32[]{:S(2)}, u32[]{:S(2)}) collective-permute-start(bf16[2,128,128]{2,1,0:T(8,128)(2,1)S(1)} %convert_element_type.72), channel_id=1, source_target_pairs={{0,1},{1,0},{2,3},{3,2},{4,5},{5,4},{6,7},{7,6},{8,9},{9,8},{10,11... | collective-permute-start | bytes 196616 | tf_op jit(solution)/shard_map/ppermute | solution.py:36
  5.6 5.4 %collective-permute-start.1 = (bf16[2,128,128]{2,1,0:T(8,128)(2,1)S(1)}, bf16[2,128,128]{2,1,0:T(8,128)(2,1)S(1)}, u32[]{:S(2)}, u32[]{:S(2)}) collective-permute-start(bf16[2,128,128]{2,1,0:T(8,128)(2,1)S(1)} %fusion), channel_id=1, source_target_pairs={{0,2},{1,3},{2,0},{3,1},{4,6},{5,7},{6,4},{7,5},{8,10},{9,11},{10,... | collective-permute-start | bytes 196616 | tf_op jit(solution)/shard_map/ppermute | solution.py:36
  11.0 5.3 %collective-permute-start.2 = (bf16[2,128,128]{2,1,0:T(8,128)(2,1)S(1)}, bf16[2,128,128]{2,1,0:T(8,128)(2,1)S(1)}, u32[]{:S(2)}, u32[]{:S(2)}) collective-permute-start(bf16[2,128,128]{2,1,0:T(8,128)(2,1)S(1)} %fusion.4), channel_id=1, source_target_pairs={{0,4},{1,5},{2,6},{3,7},{4,0},{5,1},{6,2},{7,3},{8,12},{9,13},{10,... | collective-permute-start | bytes 196616 | tf_op jit(solution)/shard_map/ppermute | solution.py:36
  18.6 5.2 %collective-permute-start.3 = (f32[2,8192]{1,0:T(2,128)S(1)}, f32[2,8192]{1,0:T(2,128)S(1)}, u32[]{:S(2)}, u32[]{:S(2)}) collective-permute-start(f32[2,8192]{1,0:T(2,128)S(1)} %get-tuple-element.38), channel_id=1, source_target_pairs={{0,8},{8,16},{16,24},{24,0},{1,9},{9,17},{17,25},{25,1},{2,10},{10... | collective-permute-start | bytes 196616 | tf_op jit(solution)/shard_map/ppermute | solution.py:28
  24.8 1.3 %collective-permute-start.4 = (bf16[2,128,128]{2,1,0:T(8,128)(2,1)S(1)}, bf16[2,128,128]{2,1,0:T(8,128)(2,1)S(1)}, u32[]{:S(2)}, u32[]{:S(2)}) collective-permute-start(bf16[2,128,128]{2,1,0:T(8,128)(2,1)S(1)} %convert_element_type.78), channel_id=1, source_target_pairs={{0,1},{1,0},{2,3},{3,2},{4,5},{5,4},{6,7},{7,6},{8,9},{9,8},{10,11... | collective-permute-start | bytes 196616 | tf_op jit(solution)/shard_map/ppermute | solution.py:36
  26.1 4.3 %collective-permute-start.5 = (bf16[2,128,128]{2,1,0:T(8,128)(2,1)S(1)}, bf16[2,128,128]{2,1,0:T(8,128)(2,1)S(1)}, u32[]{:S(2)}, u32[]{:S(2)}) collective-permute-start(bf16[2,128,128]{2,1,0:T(8,128)(2,1)S(1)} %fusion.1), channel_id=1, source_target_pairs={{0,2},{1,3},{2,0},{3,1},{4,6},{5,7},{6,4},{7,5},{8,10},{9,11},{10,... | collective-permute-start | bytes 196616 | tf_op jit(solution)/shard_map/ppermute | solution.py:36
  30.5 5.8 %collective-permute-start.6 = (bf16[2,128,128]{2,1,0:T(8,128)(2,1)S(1)}, bf16[2,128,128]{2,1,0:T(8,128)(2,1)S(1)}, u32[]{:S(2)}, u32[]{:S(2)}) collective-permute-start(bf16[2,128,128]{2,1,0:T(8,128)(2,1)S(1)} %fusion.5), channel_id=1, source_target_pairs={{0,4},{1,5},{2,6},{3,7},{4,0},{5,1},{6,2},{7,3},{8,12},{9,13},{10,... | collective-permute-start | bytes 196616 | tf_op jit(solution)/shard_map/ppermute | solution.py:36
  33.7 5.2 %collective-permute-start.7 = (f32[2,8192]{1,0:T(2,128)S(1)}, f32[2,8192]{1,0:T(2,128)S(1)}, u32[]{:S(2)}, u32[]{:S(2)}) collective-permute-start(f32[2,8192]{1,0:T(2,128)S(1)} %get-tuple-element.45), channel_id=1, source_target_pairs={{0,8},{8,16},{16,24},{24,0},{1,9},{9,17},{17,25},{25,1},{2,10},{10... | collective-permute-start | bytes 196616 | tf_op jit(solution)/shard_map/ppermute | solution.py:28
  41.2 5.4 %collective-permute-start.8 = (f32[2,8192]{1,0:T(2,128)S(1)}, f32[2,8192]{1,0:T(2,128)S(1)}, u32[]{:S(2)}, u32[]{:S(2)}) collective-permute-start(f32[2,8192]{1,0:T(2,128)S(1)} %get-tuple-element.46), channel_id=1, source_target_pairs={{0,8},{8,16},{16,24},{24,0},{1,9},{9,17},{17,25},{25,1},{2,10},{10... | collective-permute-start | bytes 196616 | tf_op jit(solution)/shard_map/ppermute | solution.py:28
  47.6 1.3 %collective-permute-start.9 = (bf16[2,128,128]{2,1,0:T(8,128)(2,1)S(1)}, bf16[2,128,128]{2,1,0:T(8,128)(2,1)S(1)}, u32[]{:S(2)}, u32[]{:S(2)}) collective-permute-start(bf16[2,128,128]{2,1,0:T(8,128)(2,1)S(1)} %convert_element_type.84), channel_id=1, source_target_pairs={{0,1},{1,0},{2,3},{3,2},{4,5},{5,4},{6,7},{7,6},{8,9},{9,8},{10,11... | collective-permute-start | bytes 196616 | tf_op jit(solution)/shard_map/ppermute | solution.py:36
  48.9 4.3 %collective-permute-start.10 = (bf16[2,128,128]{2,1,0:T(8,128)(2,1)S(1)}, bf16[2,128,128]{2,1,0:T(8,128)(2,1)S(1)}, u32[]{:S(2)}, u32[]{:S(2)}) collective-permute-start(bf16[2,128,128]{2,1,0:T(8,128)(2,1)S(1)} %fusion.2), channel_id=1, source_target_pairs={{0,2},{1,3},{2,0},{3,1},{4,6},{5,7},{6,4},{7,5},{8,10},{9,11},{10,... | collective-permute-start | bytes 196616 | tf_op jit(solution)/shard_map/ppermute | solution.py:36
  53.3 5.3 %collective-permute-start.11 = (bf16[2,128,128]{2,1,0:T(8,128)(2,1)S(1)}, bf16[2,128,128]{2,1,0:T(8,128)(2,1)S(1)}, u32[]{:S(2)}, u32[]{:S(2)}) collective-permute-start(bf16[2,128,128]{2,1,0:T(8,128)(2,1)S(1)} %fusion.6), channel_id=1, source_target_pairs={{0,4},{1,5},{2,6},{3,7},{4,0},{5,1},{6,2},{7,3},{8,12},{9,13},{10,... | collective-permute-start | bytes 196616 | tf_op jit(solution)/shard_map/ppermute | solution.py:36
  53.7 5.2 %collective-permute-start.12 = (f32[2,8192]{1,0:T(2,128)S(1)}, f32[2,8192]{1,0:T(2,128)S(1)}, u32[]{:S(2)}, u32[]{:S(2)}) collective-permute-start(f32[2,8192]{1,0:T(2,128)S(1)} %get-tuple-element.53), channel_id=1, source_target_pairs={{0,8},{8,16},{16,24},{24,0},{1,9},{9,17},{17,25},{25,1},{2,10},{10... | collective-permute-start | bytes 196616 | tf_op jit(solution)/shard_map/ppermute | solution.py:28
  58.9 16.7 %copy-start = (s32[1,64,1]{1,2,0:T(1,128)S(1)}, s32[1,64,1]{1,2,0:T(1,128)}, u32[]{:S(2)}) copy-start(s32[1,64,1]{1,2,0:T(1,128)} %param.9) | copy-start | bytes 772
  61.2 5.2 %collective-permute-start.13 = (f32[2,8192]{1,0:T(2,128)S(1)}, f32[2,8192]{1,0:T(2,128)S(1)}, u32[]{:S(2)}, u32[]{:S(2)}) collective-permute-start(f32[2,8192]{1,0:T(2,128)S(1)} %get-tuple-element.54), channel_id=1, source_target_pairs={{0,8},{8,16},{16,24},{24,0},{1,9},{9,17},{17,25},{25,1},{2,10},{10... | collective-permute-start | bytes 196616 | tf_op jit(solution)/shard_map/ppermute | solution.py:28
  67.3 1.3 %collective-permute-start.14 = (bf16[2,128,128]{2,1,0:T(8,128)(2,1)S(1)}, bf16[2,128,128]{2,1,0:T(8,128)(2,1)S(1)}, u32[]{:S(2)}, u32[]{:S(2)}) collective-permute-start(bf16[2,128,128]{2,1,0:T(8,128)(2,1)S(1)} %convert_element_type.90), channel_id=1, source_target_pairs={{0,1},{1,0},{2,3},{3,2},{4,5},{5,4},{6,7},{7,6},{8,9},{9,8},{10,11... | collective-permute-start | bytes 196616 | tf_op jit(solution)/shard_map/ppermute | solution.py:36
  68.6 4.3 %collective-permute-start.15 = (bf16[2,128,128]{2,1,0:T(8,128)(2,1)S(1)}, bf16[2,128,128]{2,1,0:T(8,128)(2,1)S(1)}, u32[]{:S(2)}, u32[]{:S(2)}) collective-permute-start(bf16[2,128,128]{2,1,0:T(8,128)(2,1)S(1)} %fusion.3), channel_id=1, source_target_pairs={{0,2},{1,3},{2,0},{3,1},{4,6},{5,7},{6,4},{7,5},{8,10},{9,11},{10,... | collective-permute-start | bytes 196616 | tf_op jit(solution)/shard_map/ppermute | solution.py:36
  73.0 5.3 %collective-permute-start.16 = (bf16[2,128,128]{2,1,0:T(8,128)(2,1)S(1)}, bf16[2,128,128]{2,1,0:T(8,128)(2,1)S(1)}, u32[]{:S(2)}, u32[]{:S(2)}) collective-permute-start(bf16[2,128,128]{2,1,0:T(8,128)(2,1)S(1)} %fusion.7), channel_id=1, source_target_pairs={{0,4},{1,5},{2,6},{3,7},{4,0},{5,1},{6,2},{7,3},{8,12},{9,13},{10,... | collective-permute-start | bytes 196616 | tf_op jit(solution)/shard_map/ppermute | solution.py:36
  81.8 12.8 %all-to-all-start = ((f32[4,32,4,128]{3,2,1,0:T(4,128)}), f32[4,32,4,128]{3,2,1,0:T(4,128)S(1)}, u32[]{:S(2)}, u32[]{:S(2)}) async-start(f32[4,32,4,128]{3,2,1,0:T(4,128)} %bitcast.3), calls=%async_computation | async-start | bytes 524288 | tf_op jit(solution)/shard_map/all_to_all | solution.py:259
  85.2 6.7 %collective-permute-start.17 = (f32[2,8192]{1,0:T(2,128)S(1)}, f32[2,8192]{1,0:T(2,128)S(1)}, u32[]{:S(2)}, u32[]{:S(2)}) collective-permute-start(f32[2,8192]{1,0:T(2,128)S(1)} %get-tuple-element.63), channel_id=1, source_target_pairs={{0,8},{8,16},{16,24},{24,0},{1,9},{9,17},{17,25},{25,1},{2,10},{10... | collective-permute-start | bytes 196616 | tf_op jit(solution)/shard_map/ppermute | solution.py:28

commit v2 on v0

v2 whole, which is shorter than its diff:
```python
import functools

import jax
import jax.numpy as jnp
from jax import lax
from jax.experimental import pallas as pl
from jax.experimental.pallas import tpu as pltpu
from jax.sharding import PartitionSpec as P


GRID = 128
FRONTS = 4
BLOCK = 128
TILE = 2048
LINES = 8


EDGE = 4.0
DRIFT = 0.05
STRENGTH = 0.06
HIGH = lax.Precision.HIGHEST
SPACING = 2.0 * EDGE / (GRID - 1)


def shifted(value, axis, steps):
    count = lax.axis_size(axis)
    pairs = [(source, (source + steps) % count) for source in range(count)]
    return lax.ppermute(value, axis, pairs)


def summed(value, axis):
    count = lax.axis_size(axis)
    step = 1
    while step < count:
        pairs = [(source, source ^ step) for source in range(count)]
        other = lax.ppermute(value.astype(jnp.bfloat16), axis, pairs)
        value = value + other.astype(jnp.float32)
        step *= 2
    return value


def cells(coordinate):
    place = jnp.clip((coordinate + EDGE) * (1.0 / SPACING), -2.0, GRID + 2.0)
    cell = jnp.floor(place)
    upper = place - cell
    lower = 1.0 - upper
    odd = jnp.floor(cell * 0.5)
    even = cell - odd
    is_even = even == odd
    return (even, jnp.where(is_even, lower, upper)), (odd, jnp.where(is_even, upper, lower))


def hat_table(coordinate):
    count = coordinate.shape[1]
    none = jnp.zeros((2 * LINES, count), jnp.bfloat16)
    index = lax.broadcasted_iota(jnp.int32, none.shape, 0).astype(jnp.float32)
    parts = []
    for pair in cells(coordinate):
        cell, weight = (jnp.concatenate([row, row], axis=0).astype(jnp.bfloat16) for row in pair)
        for start in range(0, GRID // 2, 2 * LINES):
            at = (index + float(start)).astype(jnp.bfloat16)
            parts.append(jnp.where(cell == at, weight, none))
    return jnp.concatenate(parts, axis=0)


def deposit(x, y):
    return lax.dot_general(
        hat_table(y), hat_table(x), (((1,), (1,)), ((), ())), preferred_element_type=jnp.float32
    )


def kick(x, moment_x, y, moment_y, table):
    sampled = jnp.dot(table, hat_table(x), preferred_element_type=jnp.float32)
    index = lax.broadcasted_iota(jnp.int32, x.shape, 0).astype(jnp.float32)
    moments = [moment_x, moment_y]
    pushes = [0.0, 0.0]
    block = 0
    for cell, weight in cells(y):
        weight = weight.astype(jnp.bfloat16).astype(jnp.float32)
        found = [jnp.zeros(x.shape, jnp.float32)] * 2
        for start in range(0, GRID // 2, LINES):
            here = cell == index + float(start)
            for which in range(2):
                part = sampled[block * LINES : (block + 1) * LINES]
                found[which] = jnp.where(here, part, found[which])
                block += 1
        pushes = [push + weight * part for push, part in zip(pushes, found)]
    for which, push in enumerate(pushes):
        shift = LINES // 2
        while shift:
            push = push + pltpu.roll(push, shift, 0)
            shift //= 2
        moments[which] = moments[which] - push
    moment_x, moment_y = moments
    return x + DRIFT * moment_x, moment_x, y + DRIFT * moment_y, moment_y


def halves(value):
    high = value.astype(jnp.bfloat16)
    return high, (value - high.astype(jnp.float32)).astype(jnp.bfloat16)


def tables(density, smooth, slope, scale):
    high, low = halves(density.reshape(2 * GRID, GRID) * scale)
    left = jnp.concatenate([high, low, high], axis=1)
    inner = lax.dot_general(
        left,
        jnp.concatenate([slope, smooth], axis=0),
        (((1,), (1,)), ((), ())),
        preferred_element_type=jnp.float32,
    )
    pushes = []
    for which, green in enumerate((smooth, slope)):
        part = inner[:, which * GRID : (which + 1) * GRID]
        high, low = halves(jnp.concatenate([part[:GRID], part[GRID:]], axis=1))
        right = jnp.concatenate([high, low, high], axis=0)
        pushes.append(jnp.dot(green, right, preferred_element_type=jnp.float32))
    both = jnp.concatenate(
        [push[start : start + LINES] for start in range(0, GRID, LINES) for push in pushes], axis=0
    ).astype(jnp.bfloat16)
    return both[:, :GRID], both[:, GRID:]


def greens_kernel(smooth_ref, slope_ref, *outs):
    row = lax.broadcasted_iota(jnp.int32, (GRID, GRID), 0)
    column = lax.broadcasted_iota(jnp.int32, (GRID, GRID), 1)
    chosen = jnp.where(row < GRID // 2, 2 * row, 2 * row - (GRID - 1))
    order = (column == chosen).astype(jnp.float32)
    for ref, out_ref in zip((smooth_ref, slope_ref), outs):
        moved = jnp.dot(order, ref[...], precision=HIGH, preferred_element_type=jnp.float32)
        moved = lax.dot_general(
            moved, order, (((1,), (1,)), ((), ())), precision=HIGH, preferred_element_type=jnp.float32
        )
        high, low = halves(moved)
        for place, part in enumerate((high, high, low)):
            out_ref[:, place * GRID : (place + 1) * GRID] = part


def columns(count):
    width = min(TILE, count)
    return [pl.ds(start, width) for start in range(0, count, width)]


def first_kernel(resident_hbm, opposing_hbm, resident_ref, opposing_ref, density_ref, landed):
    held = (resident_ref, opposing_ref)
    copies = [
        pltpu.make_async_copy(source, place, landed.at[which])
        for which, (source, place) in enumerate(zip((resident_hbm, opposing_hbm), held))
    ]
    for copy in copies:
        copy.start()
    for which, copy in enumerate(copies):
        copy.wait()
        beam = held[which]
        density_ref[which] = sum(
            deposit(line(beam, 0, tile), line(beam, 2, tile)) for tile in columns(beam.shape[1])
        )


def line(ref, row, tile):
    return jnp.broadcast_to(ref[row : row + 1, tile], (LINES, tile.size))


def rows(sources, tile):
    if len(sources) == 1:
        return [line(sources[0], row, tile) for row in range(4)]
    return [line(sources[row % 2], row // 2, tile) for row in range(4)]


def opposing_kernel(scale, density_ref, smooth_ref, slope_ref, *refs):
    own, other = tables(density_ref[...], smooth_ref[...], slope_ref[...], scale)
    *sources, place_ref, moment_ref, table_ref = refs
    table_ref[...] = other
    for tile in columns(place_ref.shape[1]):
        x, moment_x, y, moment_y = kick(*rows(sources, tile), own)
        place_ref[0:1, tile] = x[:1]
        place_ref[1:2, tile] = y[:1]
        moment_ref[0:1, tile] = moment_x[:1]
        moment_ref[1:2, tile] = moment_y[:1]


def resident_kernel(table_ref, beam_ref, moved_ref, density_ref):
    total = 0.0
    for tile in columns(beam_ref.shape[1]):
        new = kick(*rows([beam_ref], tile), table_ref[...])
        for row in range(4):
            moved_ref[row : row + 1, tile] = new[row][:1]
        total = total + deposit(new[0], new[2])
    density_ref[...] = total


def arrival_kernel(place_ref, resident_ref, density_ref):
    density_ref[0] = resident_ref[...]
    density_ref[1] = sum(
        deposit(line(place_ref, 0, tile), line(place_ref, 1, tile)) for tile in columns(place_ref.shape[1])
    )


def last_kernel(scale, slots_ref, density_ref, smooth_ref, slope_ref, beam_ref, packed_ref, table_ref, moved_ref):
    table_ref[...], other = tables(density_ref[...], smooth_ref[...], slope_ref[...], scale)
    packed_ref[...] = jnp.zeros_like(packed_ref)
    for tile in columns(beam_ref.shape[1]):
        new = kick(*rows([beam_ref], tile), other)
        for row in range(4):
            moved_ref[row : row + 1, tile] = new[row][:1]
    for block in range(beam_ref.shape[1] // BLOCK):
        packed_ref[slots_ref[block]] = moved_ref[:, block * BLOCK : (block + 1) * BLOCK]


def final_kernel(table_ref, place_ref, moment_ref, out_ref):
    for tile in columns(place_ref.shape[1]):
        new = kick(*rows([place_ref, moment_ref], tile), table_ref[...])
        for row in range(4):
            out_ref[row : row + 1, tile] = new[row][:1]


def local(kernel, out_shape, **options):
    return pl.pallas_call(
        kernel,
        out_shape=out_shape,
        compiler_params=pltpu.CompilerParams(vmem_limit_bytes=24 << 20),
        **options,
    )


def array(*shape, dtype=jnp.float32):
    return jax.ShapeDtypeStruct(shape, dtype)


def slots_kernel(capacity, routes_ref, slots_ref, taken_ref):
    for station in range(taken_ref.shape[0]):
        taken_ref[station] = 0

    def place(block, carry):
        station = routes_ref[block]
        taken = taken_ref[station]
        slots_ref[block] = station * capacity + jnp.minimum(taken, capacity - 1)
        taken_ref[station] = taken + 1
        return carry

    lax.fori_loop(0, routes_ref.shape[0], place, 0)


def shards(beam_first, beam_second, green_smooth, green_slope, destination):
    resident = beam_first[0, 0]
    opposing = (beam_second[0, 0],)
    groups = lax.axis_size("dom")
    stations = lax.axis_size("station")
    count = resident.shape[1]
    block_count = count // BLOCK
    capacity = max(2, 2 * block_count // stations)
    scale = STRENGTH * GRID * GRID / (count * groups)
    half, whole = array(2, count), array(4, count)
    density, densities = array(GRID, GRID), array(2, GRID, GRID)
    table = array(2 * GRID, GRID, dtype=jnp.bfloat16)
    vmem, smem = (pl.BlockSpec(memory_space=space) for space in (pltpu.VMEM, pltpu.SMEM))
    place = local(
        functools.partial(slots_kernel, capacity),
        array(block_count, dtype=jnp.int32),
        in_specs=[smem],
        out_specs=smem,
        scratch_shapes=[pltpu.SMEM((stations,), jnp.int32)],
    )(destination[0, :, 0])

    resident, *opposing, total = local(
        first_kernel,
        (whole, whole, densities),
        in_specs=[pl.BlockSpec(memory_space=pltpu.HBM)] * 2,
        out_specs=(vmem,) * 3,
        scratch_shapes=[pltpu.SemaphoreType.DMA((2,))],
    )(*(pltpu.with_memory_space_constraint(value, pltpu.HBM) for value in (resident, opposing[0])))
    wide = array(GRID, 3 * GRID, dtype=jnp.bfloat16)
    smooth, slope = local(greens_kernel, (wide, wide))(green_smooth, green_slope)
    total = summed(total, "dom")
    for _ in range(FRONTS - 1):
        positions, moments, other = local(
            functools.partial(opposing_kernel, scale), (half, half, table)
        )(total, smooth, slope, *opposing)
        positions = shifted(positions, "station", 1)
        moments = shifted(moments, "station", 1)
        opposing = (positions, moments)
        resident, part = local(resident_kernel, (whole, density))(other, resident)
        total = local(arrival_kernel, densities)(positions, part)
        total = summed(total, "dom")
    outgoing, own = local(
        functools.partial(last_kernel, scale),
        (array(stations * capacity, 4, BLOCK), table),
        in_specs=[smem] + [vmem] * 4,
        out_specs=(vmem, vmem),
        scratch_shapes=[pltpu.VMEM((4, count), jnp.float32)],
    )(place, total, smooth, slope, resident)
    outgoing = outgoing.reshape(stations, capacity, 4, BLOCK)
    arrived = lax.all_to_all(outgoing, "station", split_axis=0, concat_axis=0, tiled=True)
    opposing = local(final_kernel, whole)(own, *opposing)
    return (arrived[None, None], opposing[None, None])


def solution(mesh):
    placed = (
        P("station", "dom", None, None),
        P("station", "dom", None, None),
        P(),
        P(),
        P("station", "dom", None),
    )
    return jax.shard_map(
        shards,
        mesh=mesh,
        in_specs=placed,
        out_specs=(P("station", "dom", None, None, None, None), P("station", "dom", None, None)),
        check_vma=False,
    )
```

time: 97.4 us -> 92.9 us (0.954)
  waiting for transfers between devices: 35.6 us -> 38.5 us
  Pallas kernels: 28.2 us -> 25.4 us
  local copies, waits for them, and re-layouts: 3.1 us -> 0.72 us
  starting transfers between devices: 28.7 us -> 26.8 us
    ppermute x6, waiting for transfers between devices: 11.6 us -> 14.9 us  [shifted(): return lax.ppermute(value, axis, pairs)]
    pallas_call x3, Pallas kernels: 9.15 us -> 6.48 us  [shards(): resident, part = local(resident_kernel, (whole, density))(other, resident)]
    unnamed x15 -> x7, local copies, waits for them, and re-layouts: 3.1 us -> 0.72 us
    ppermute x6, starting transfers between devices: 6.67 us -> 4.66 us  [shifted(): return lax.ppermute(value, axis, pairs)]
    pallas_call x7 -> x9, Pallas kernels: 12.5 us -> 13.7 us  [the longest x3 5.74 us: shards(): local(functools.partial(opposing_kernel, scale), (half, half, table))]
where the time goes in v2:
time: 92.9 us; the launch traced here: 92.7 us
  waiting for transfers between devices  38.5 us (41%)
  starting transfers between devices  26.8 us (29%)
  Pallas kernels  25.4 us (27%)
    ppermute x12, waiting for transfers between devices, summed(): other = lax.ppermute(value.astype(jnp.bfloat16), axis, pairs)  23.7 us
    ppermute x12, starting transfers between devices, summed(): other = lax.ppermute(value.astype(jnp.bfloat16), axis, pairs)  18.7 us
    ppermute x6, waiting for transfers between devices, shifted(): return lax.ppermute(value, axis, pairs)  14.9 us
    pallas_call x3, Pallas kernels, shards(): resident, part = local(resident_kernel, (whole, density))(other, resident)  6.48 us
    pallas_call x3, Pallas kernels, shards(): local(functools.partial(opposing_kernel, scale), (half, half, table))  5.74 us
    ppermute x6, starting transfers between devices, shifted(): return lax.ppermute(value, axis, pairs)  4.66 us
    all_to_all x1, starting transfers between devices, shards(): lax.all_to_all(outgoing, 'station', split_axis=0, concat_axis=0, tiled=True)  3.41 us
    pallas_call x1, Pallas kernels, shards(): local(first_kernel, (whole, whole, densities), in_specs=[pl.BlockSpec(mem...  3.4 us
  transfers between devices with their start and end apart: 19, of which 18 were waited for; matrix products, arithmetic and copies ran while one was open for 0% of the time, Pallas kernels for 12%

profile of v2, /device:TPU:0, one launch (start us, length us, event | category | flops | bytes accessed | tf_op | source)
XLA Modules:
  0.0 92.7 jit_solution(6600252206490300865)
XLA Ops:
  0.6 3.4 %shard_map.69 = (f32[4,8192]{1,0:T(4,128)S(1)}, f32[4,8192]{1,0:T(4,128)S(1)}, f32[2,128,128]{2,1,0:T(8,128)S(1)}) custom-call(f32[4,8192]{1,0:T(4,128)} %bitcast.8, f32[4,8192]{1,0:T(4,128)} %bitcast.9), custom_call_target="tpu_custom_call" | custom-call | tf_op jit(solution)/shard_map/pallas_call | solution.py:265
  4.1 0.6 collective-permute-start
  4.6 0.9 collective-permute-done
  5.6 3.0 %collective-permute-start.1 = (bf16[2,128,128]{2,1,0:T(8,128)(2,1)S(1)}, bf16[2,128,128]{2,1,0:T(8,128)(2,1)S(1)}, u32[]{:S(2)}, u32[]{:S(2)}) collective-permute-start(bf16[2,128,128]{2,1,0:T(8,128)(2,1)S(1)} %fusion), channel_id=1, source_target_pairs={{0,2},{1,3},{2,0},{3,1},{4,6},{5,7},{6,4},{7,5},{8,10},{9,11},{10,... | collective-permute-start | bytes 196616 | tf_op jit(solution)/shard_map/ppermute | solution.py:36
  8.5 2.4 %collective-permute-done.1 = bf16[2,128,128]{2,1,0:T(8,128)(2,1)S(1)} collective-permute-done((bf16[2,128,128]{2,1,0:T(8,128)(2,1)S(1)}, bf16[2,128,128]{2,1,0:T(8,128)(2,1)S(1)}, u32[]{:S(2)}, u32[]{:S(2)}) %collective-permute-start.1) | collective-permute-done | bytes 65568 | tf_op jit(solution)/shard_map/ppermute | solution.py:36
  11.0 2.9 %collective-permute-start.2 = (bf16[2,128,128]{2,1,0:T(8,128)(2,1)S(1)}, bf16[2,128,128]{2,1,0:T(8,128)(2,1)S(1)}, u32[]{:S(2)}, u32[]{:S(2)}) collective-permute-start(bf16[2,128,128]{2,1,0:T(8,128)(2,1)S(1)} %fusion.4), channel_id=1, source_target_pairs={{0,4},{1,5},{2,6},{3,7},{4,0},{5,1},{6,2},{7,3},{8,12},{9,13},{10,... | collective-permute-start | bytes 196616 | tf_op jit(solution)/shard_map/ppermute | solution.py:36
  13.9 0.7 shard_map.70
  14.6 1.6 %collective-permute-done.2 = bf16[2,128,128]{2,1,0:T(8,128)(2,1)S(1)} collective-permute-done((bf16[2,128,128]{2,1,0:T(8,128)(2,1)S(1)}, bf16[2,128,128]{2,1,0:T(8,128)(2,1)S(1)}, u32[]{:S(2)}, u32[]{:S(2)}) %collective-permute-start.2) | collective-permute-done | bytes 65568 | tf_op jit(solution)/shard_map/ppermute | solution.py:36
  16.3 1.9 %shard_map.71 = (f32[2,8192]{1,0:T(2,128)S(1)}, f32[2,8192]{1,0:T(2,128)S(1)}, bf16[256,128]{1,0:T(8,128)(2,1)S(1)}) custom-call(f32[2,128,128]{2,1,0:T(8,128)S(1)} %convert_add_fusion.9.density_ref, bf16[128,384]{1,0:T(8,128)(2,1)S(1)} %get-tuple-element.25.smooth_ref, bf16[128,384]{1,0:T(8,128)(2,1)S(1)} %get-tuple-element.26.slope_ref, ...), custom_call_target="tpu_custom_call" | custom-call | tf_op jit(solution)/shard_map/pallas_call | solution.py:276
  18.2 1.8 %collective-permute-start.3 = (f32[2,8192]{1,0:T(2,128)S(1)}, f32[2,8192]{1,0:T(2,128)S(1)}, u32[]{:S(2)}, u32[]{:S(2)}) collective-permute-start(f32[2,8192]{1,0:T(2,128)S(1)} %get-tuple-element.28), channel_id=1, source_target_pairs={{0,8},{8,16},{16,24},{24,0},{1,9},{9,17},{17,25},{25,1},{2,10},{10... | collective-permute-start | bytes 196616 | tf_op jit(solution)/shard_map/ppermute | solution.py:28
  20.0 2.2 %shard_map.72 = (f32[4,8192]{1,0:T(4,128)S(1)}, f32[128,128]{1,0:T(8,128)S(1)}) custom-call(bf16[256,128]{1,0:T(8,128)(2,1)S(1)} %get-tuple-element.29.table_ref, f32[4,8192]{1,0:T(4,128)S(1)} %get-tuple-element.30.beam_ref), custom_call_target="tpu_custom_call" | custom-call | tf_op jit(solution)/shard_map/pallas_call | solution.py:282
  22.2 1.3 %collective-permute-done.3.place_ref.refs_0_ = f32[2,8192]{1,0:T(2,128)S(1)} collective-permute-done((f32[2,8192]{1,0:T(2,128)S(1)}, f32[2,8192]{1,0:T(2,128)S(1)}, u32[]{:S(2)}, u32[]{:S(2)}) %collective-permute-start.3) | collective-permute-done | bytes 65568 | tf_op jit(solution)/shard_map/ppermute | solution.py:28
  23.4 0.7 shard_map.73
  24.3 1.2 %collective-permute-done.4 = bf16[2,128,128]{2,1,0:T(8,128)(2,1)S(1)} collective-permute-done((bf16[2,128,128]{2,1,0:T(8,128)(2,1)S(1)}, bf16[2,128,128]{2,1,0:T(8,128)(2,1)S(1)}, u32[]{:S(2)}, u32[]{:S(2)}) %collective-permute-start.4) | collective-permute-done | bytes 65568 | tf_op jit(solution)/shard_map/ppermute | solution.py:36
  25.5 1.9 %collective-permute-start.5 = (bf16[2,128,128]{2,1,0:T(8,128)(2,1)S(1)}, bf16[2,128,128]{2,1,0:T(8,128)(2,1)S(1)}, u32[]{:S(2)}, u32[]{:S(2)}) collective-permute-start(bf16[2,128,128]{2,1,0:T(8,128)(2,1)S(1)} %fusion.1), channel_id=1, source_target_pairs={{0,2},{1,3},{2,0},{3,1},{4,6},{5,7},{6,4},{7,5},{8,10},{9,11},{10,... | collective-permute-start | bytes 196616 | tf_op jit(solution)/shard_map/ppermute | solution.py:36
  27.4 2.4 %collective-permute-done.5 = bf16[2,128,128]{2,1,0:T(8,128)(2,1)S(1)} collective-permute-done((bf16[2,128,128]{2,1,0:T(8,128)(2,1)S(1)}, bf16[2,128,128]{2,1,0:T(8,128)(2,1)S(1)}, u32[]{:S(2)}, u32[]{:S(2)}) %collective-permute-start.5) | collective-permute-done | bytes 65568 | tf_op jit(solution)/shard_map/ppermute | solution.py:36
  29.9 3.2 %collective-permute-start.6 = (bf16[2,128,128]{2,1,0:T(8,128)(2,1)S(1)}, bf16[2,128,128]{2,1,0:T(8,128)(2,1)S(1)}, u32[]{:S(2)}, u32[]{:S(2)}) collective-permute-start(bf16[2,128,128]{2,1,0:T(8,128)(2,1)S(1)} %fusion.5), channel_id=1, source_target_pairs={{0,4},{1,5},{2,6},{3,7},{4,0},{5,1},{6,2},{7,3},{8,12},{9,13},{10,... | collective-permute-start | bytes 196616 | tf_op jit(solution)/shard_map/ppermute | solution.py:36
  33.1 0.6 collective-permute-start.7
  33.7 2.0 %collective-permute-done.6 = bf16[2,128,128]{2,1,0:T(8,128)(2,1)S(1)} collective-permute-done((bf16[2,128,128]{2,1,0:T(8,128)(2,1)S(1)}, bf16[2,128,128]{2,1,0:T(8,128)(2,1)S(1)}, u32[]{:S(2)}, u32[]{:S(2)}) %collective-permute-start.6) | collective-permute-done | bytes 65568 | tf_op jit(solution)/shard_map/ppermute | solution.py:36
  35.7 2.6 %collective-permute-done.7.refs_1_ = f32[2,8192]{1,0:T(2,128)S(1)} collective-permute-done((f32[2,8192]{1,0:T(2,128)S(1)}, f32[2,8192]{1,0:T(2,128)S(1)}, u32[]{:S(2)}, u32[]{:S(2)}) %collective-permute-start.7) | collective-permute-done | bytes 65568 | tf_op jit(solution)/shard_map/ppermute | solution.py:28
  38.3 1.9 %shard_map.74 = (f32[2,8192]{1,0:T(2,128)S(1)}, f32[2,8192]{1,0:T(2,128)S(1)}, bf16[256,128]{1,0:T(8,128)(2,1)S(1)}) custom-call(f32[2,128,128]{2,1,0:T(8,128)S(1)} %convert_add_fusion.6.density_ref, bf16[128,384]{1,0:T(8,128)(2,1)S(1)} %get-tuple-element.25.smooth_ref, bf16[128,384]{1,0:T(8,128)(2,1)S(1)} %get-tuple-element.26.slope_ref, ...), custom_call_target="tpu_custom_call" | custom-call | tf_op jit(solution)/shard_map/pallas_call | solution.py:276
  40.2 0.2 collective-permute-start.8
  40.4 2.2 %shard_map.75 = (f32[4,8192]{1,0:T(4,128)S(1)}, f32[128,128]{1,0:T(8,128)S(1)}) custom-call(bf16[256,128]{1,0:T(8,128)(2,1)S(1)} %get-tuple-element.34.table_ref, f32[4,8192]{1,0:T(4,128)S(1)} %get-tuple-element.35.beam_ref), custom_call_target="tpu_custom_call" | custom-call | tf_op jit(solution)/shard_map/pallas_call | solution.py:282
  42.6 3.0 %collective-permute-done.8.place_ref.refs_0_ = f32[2,8192]{1,0:T(2,128)S(1)} collective-permute-done((f32[2,8192]{1,0:T(2,128)S(1)}, f32[2,8192]{1,0:T(2,128)S(1)}, u32[]{:S(2)}, u32[]{:S(2)}) %collective-permute-start.8) | collective-permute-done | bytes 65568 | tf_op jit(solution)/shard_map/ppermute | solution.py:28
  45.6 0.7 shard_map.76
  46.3 0.1 collective-permute-start.9
  46.4 1.2 %collective-permute-done.9 = bf16[2,128,128]{2,1,0:T(8,128)(2,1)S(1)} collective-permute-done((bf16[2,128,128]{2,1,0:T(8,128)(2,1)S(1)}, bf16[2,128,128]{2,1,0:T(8,128)(2,1)S(1)}, u32[]{:S(2)}, u32[]{:S(2)}) %collective-permute-start.9) | collective-permute-done | bytes 65568 | tf_op jit(solution)/shard_map/ppermute | solution.py:36
  47.7 1.9 %collective-permute-start.10 = (bf16[2,128,128]{2,1,0:T(8,128)(2,1)S(1)}, bf16[2,128,128]{2,1,0:T(8,128)(2,1)S(1)}, u32[]{:S(2)}, u32[]{:S(2)}) collective-permute-start(bf16[2,128,128]{2,1,0:T(8,128)(2,1)S(1)} %fusion.2), channel_id=1, source_target_pairs={{0,2},{1,3},{2,0},{3,1},{4,6},{5,7},{6,4},{7,5},{8,10},{9,11},{10,... | collective-permute-start | bytes 196616 | tf_op jit(solution)/shard_map/ppermute | solution.py:36
  49.6 2.4 %collective-permute-done.10 = bf16[2,128,128]{2,1,0:T(8,128)(2,1)S(1)} collective-permute-done((bf16[2,128,128]{2,1,0:T(8,128)(2,1)S(1)}, bf16[2,128,128]{2,1,0:T(8,128)(2,1)S(1)}, u32[]{:S(2)}, u32[]{:S(2)}) %collective-permute-start.10) | collective-permute-done | bytes 65568 | tf_op jit(solution)/shard_map/ppermute | solution.py:36
  52.0 0.4 collective-permute-start.11
  52.5 4.8 %collective-permute-done.11 = bf16[2,128,128]{2,1,0:T(8,128)(2,1)S(1)} collective-permute-done((bf16[2,128,128]{2,1,0:T(8,128)(2,1)S(1)}, bf16[2,128,128]{2,1,0:T(8,128)(2,1)S(1)}, u32[]{:S(2)}, u32[]{:S(2)}) %collective-permute-start.11) | collective-permute-done | bytes 65568 | tf_op jit(solution)/shard_map/ppermute | solution.py:36
  57.3 0.3 collective-permute-done.12.refs_1_
  57.6 1.9 %shard_map.77 = (f32[2,8192]{1,0:T(2,128)S(1)}, f32[2,8192]{1,0:T(2,128)S(1)}, bf16[256,128]{1,0:T(8,128)(2,1)S(1)}) custom-call(f32[2,128,128]{2,1,0:T(8,128)S(1)} %convert_add_fusion.3.density_ref, bf16[128,384]{1,0:T(8,128)(2,1)S(1)} %get-tuple-element.25.smooth_ref, bf16[128,384]{1,0:T(8,128)(2,1)S(1)} %get-tuple-element.26.slope_ref, ...), custom_call_target="tpu_custom_call" | custom-call | tf_op jit(solution)/shard_map/pallas_call | solution.py:276
  59.6 2.2 %shard_map.78 = (f32[4,8192]{1,0:T(4,128)S(1)}, f32[128,128]{1,0:T(8,128)S(1)}) custom-call(bf16[256,128]{1,0:T(8,128)(2,1)S(1)} %get-tuple-element.39.table_ref, f32[4,8192]{1,0:T(4,128)S(1)} %get-tuple-element.40.beam_ref), custom_call_target="tpu_custom_call" | custom-call | tf_op jit(solution)/shard_map/pallas_call | solution.py:282
  61.8 3.0 %collective-permute-done.13.place_ref = f32[2,8192]{1,0:T(2,128)S(1)} collective-permute-done((f32[2,8192]{1,0:T(2,128)S(1)}, f32[2,8192]{1,0:T(2,128)S(1)}, u32[]{:S(2)}, u32[]{:S(2)}) %collective-permute-start.13) | collective-permute-done | bytes 65568 | tf_op jit(solution)/shard_map/ppermute | solution.py:28
  64.8 0.7 shard_map.79
  65.6 1.2 %collective-permute-done.14 = bf16[2,128,128]{2,1,0:T(8,128)(2,1)S(1)} collective-permute-done((bf16[2,128,128]{2,1,0:T(8,128)(2,1)S(1)}, bf16[2,128,128]{2,1,0:T(8,128)(2,1)S(1)}, u32[]{:S(2)}, u32[]{:S(2)}) %collective-permute-start.14) | collective-permute-done | bytes 65568 | tf_op jit(solution)/shard_map/ppermute | solution.py:36
  66.8 1.9 %collective-permute-start.15 = (bf16[2,128,128]{2,1,0:T(8,128)(2,1)S(1)}, bf16[2,128,128]{2,1,0:T(8,128)(2,1)S(1)}, u32[]{:S(2)}, u32[]{:S(2)}) collective-permute-start(bf16[2,128,128]{2,1,0:T(8,128)(2,1)S(1)} %fusion.3), channel_id=1, source_target_pairs={{0,2},{1,3},{2,0},{3,1},{4,6},{5,7},{6,4},{7,5},{8,10},{9,11},{10,... | collective-permute-start | bytes 196616 | tf_op jit(solution)/shard_map/ppermute | solution.py:36
  68.8 2.4 %collective-permute-done.15 = bf16[2,128,128]{2,1,0:T(8,128)(2,1)S(1)} collective-permute-done((bf16[2,128,128]{2,1,0:T(8,128)(2,1)S(1)}, bf16[2,128,128]{2,1,0:T(8,128)(2,1)S(1)}, u32[]{:S(2)}, u32[]{:S(2)}) %collective-permute-start.15) | collective-permute-done | bytes 65568 | tf_op jit(solution)/shard_map/ppermute | solution.py:36
  71.2 2.6 %collective-permute-start.16 = (bf16[2,128,128]{2,1,0:T(8,128)(2,1)S(1)}, bf16[2,128,128]{2,1,0:T(8,128)(2,1)S(1)}, u32[]{:S(2)}, u32[]{:S(2)}) collective-permute-start(bf16[2,128,128]{2,1,0:T(8,128)(2,1)S(1)} %fusion.7), channel_id=1, source_target_pairs={{0,4},{1,5},{2,6},{3,7},{4,0},{5,1},{6,2},{7,3},{8,12},{9,13},{10,... | collective-permute-start | bytes 196616 | tf_op jit(solution)/shard_map/ppermute | solution.py:36
  73.9 1.7 %shard_map.68.slots_ref = s32[64]{0:T(128)S(1)} custom-call(s32[64]{0:T(128)S(1)} %bitcast.6), custom_call_target="tpu_custom_call" | custom-call | tf_op jit(solution)/shard_map/pallas_call | solution.py:257
  75.6 0.9 collective-permute-done.16
  76.5 3.2 %shard_map.80 = (f32[128,4,128]{2,1,0:T(4,128)}, bf16[256,128]{1,0:T(8,128)(2,1)S(1)}) custom-call(s32[64]{0:T(128)S(1)} %shard_map.68.slots_ref, f32[2,128,128]{2,1,0:T(8,128)S(1)} %convert_add_fusion.density_ref, bf16[128,384]{1,0:T(8,128)(2,1)S(1)} %get-tuple-element.25.smooth_ref, bf16[128,384]{1,0:T(8,128)(2,1)S(1)} %get-tuple-element.26.slope_ref, ...), custom_call_target="tpu_custom_call" | custom-call | tf_op jit(solution)/shard_map/pallas_call | solution.py:285
  79.8 3.4 %all-to-all-start = ((f32[4,32,4,128]{3,2,1,0:T(4,128)}), f32[4,32,4,128]{3,2,1,0:T(4,128)S(1)}, u32[]{:S(2)}, u32[]{:S(2)}) async-start(f32[4,32,4,128]{3,2,1,0:T(4,128)} %bitcast.3), calls=%async_computation | async-start | bytes 524288 | tf_op jit(solution)/shard_map/all_to_all | solution.py:293
  83.2 2.0 %collective-permute-start.17 = (f32[2,8192]{1,0:T(2,128)S(1)}, f32[2,8192]{1,0:T(2,128)S(1)}, u32[]{:S(2)}, u32[]{:S(2)}) collective-permute-start(f32[2,8192]{1,0:T(2,128)S(1)} %get-tuple-element.45), channel_id=1, source_target_pairs={{0,8},{8,16},{16,24},{24,0},{1,9},{9,17},{17,25},{25,1},{2,10},{10... | collective-permute-start | bytes 196616 | tf_op jit(solution)/shard_map/ppermute | solution.py:28
  85.2 4.8 %collective-permute-done.17.moment_ref = f32[2,8192]{1,0:T(2,128)S(1)} collective-permute-done((f32[2,8192]{1,0:T(2,128)S(1)}, f32[2,8192]{1,0:T(2,128)S(1)}, u32[]{:S(2)}, u32[]{:S(2)}) %collective-permute-start.17) | collective-permute-done | bytes 65568 | tf_op jit(solution)/shard_map/ppermute | solution.py:28
  89.9 2.0 %shard_map.81 = f32[4,8192]{1,0:T(4,128)} custom-call(bf16[256,128]{1,0:T(8,128)(2,1)S(1)} %get-tuple-element.44.table_ref, f32[2,8192]{1,0:T(2,128)S(1)} %collective-permute-done.13.place_ref, f32[2,8192]{1,0:T(2,128)S(1)} %collective-permute-done.17.moment_ref), custom_call_target="tpu_custom_call" | custom-call | tf_op jit(solution)/shard_map/pallas_call | solution.py:294
  92.0 0.7 copy.8
  (27 shorter events, 0.6 us)
Async XLA Ops:
  4.1 1.5 %collective-permute-start = (bf16[2,128,128]{2,1,0:T(8,128)(2,1)S(1)}, bf16[2,128,128]{2,1,0:T(8,128)(2,1)S(1)}, u32[]{:S(2)}, u32[]{:S(2)}) collective-permute-start(bf16[2,128,128]{2,1,0:T(8,128)(2,1)S(1)} %convert_element_type.72), channel_id=1, source_target_pairs={{0,1},{1,0},{2,3},{3,2},{4,5},{5,4},{6,7},{7,6},{8,9},{9,8},{10,11... | collective-permute-start | bytes 196616 | tf_op jit(solution)/shard_map/ppermute | solution.py:36
  5.5 8.4 %copy-start = (f32[128,128]{1,0:T(8,128)S(1)}, f32[128,128]{1,0:T(8,128)}, u32[]{:S(2)}) copy-start(f32[128,128]{1,0:T(8,128)} %smooth_ref.1) | copy-start | bytes 196612
  5.5 8.4 %copy-start.1 = (f32[128,128]{1,0:T(8,128)S(1)}, f32[128,128]{1,0:T(8,128)}, u32[]{:S(2)}) copy-start(f32[128,128]{1,0:T(8,128)} %slope_ref.1) | copy-start | bytes 196612
  5.6 5.4 %collective-permute-start.1 = (bf16[2,128,128]{2,1,0:T(8,128)(2,1)S(1)}, bf16[2,128,128]{2,1,0:T(8,128)(2,1)S(1)}, u32[]{:S(2)}, u32[]{:S(2)}) collective-permute-start(bf16[2,128,128]{2,1,0:T(8,128)(2,1)S(1)} %fusion), channel_id=1, source_target_pairs={{0,2},{1,3},{2,0},{3,1},{4,6},{5,7},{6,4},{7,5},{8,10},{9,11},{10,... | collective-permute-start | bytes 196616 | tf_op jit(solution)/shard_map/ppermute | solution.py:36
  11.0 5.3 %collective-permute-start.2 = (bf16[2,128,128]{2,1,0:T(8,128)(2,1)S(1)}, bf16[2,128,128]{2,1,0:T(8,128)(2,1)S(1)}, u32[]{:S(2)}, u32[]{:S(2)}) collective-permute-start(bf16[2,128,128]{2,1,0:T(8,128)(2,1)S(1)} %fusion.4), channel_id=1, source_target_pairs={{0,4},{1,5},{2,6},{3,7},{4,0},{5,1},{6,2},{7,3},{8,12},{9,13},{10,... | collective-permute-start | bytes 196616 | tf_op jit(solution)/shard_map/ppermute | solution.py:36
  18.2 5.2 %collective-permute-start.3 = (f32[2,8192]{1,0:T(2,128)S(1)}, f32[2,8192]{1,0:T(2,128)S(1)}, u32[]{:S(2)}, u32[]{:S(2)}) collective-permute-start(f32[2,8192]{1,0:T(2,128)S(1)} %get-tuple-element.28), channel_id=1, source_target_pairs={{0,8},{8,16},{16,24},{24,0},{1,9},{9,17},{17,25},{25,1},{2,10},{10... | collective-permute-start | bytes 196616 | tf_op jit(solution)/shard_map/ppermute | solution.py:28
  24.2 1.3 %collective-permute-start.4 = (bf16[2,128,128]{2,1,0:T(8,128)(2,1)S(1)}, bf16[2,128,128]{2,1,0:T(8,128)(2,1)S(1)}, u32[]{:S(2)}, u32[]{:S(2)}) collective-permute-start(bf16[2,128,128]{2,1,0:T(8,128)(2,1)S(1)} %convert_element_type.78), channel_id=1, source_target_pairs={{0,1},{1,0},{2,3},{3,2},{4,5},{5,4},{6,7},{7,6},{8,9},{9,8},{10,11... | collective-permute-start | bytes 196616 | tf_op jit(solution)/shard_map/ppermute | solution.py:36
  25.5 4.3 %collective-permute-start.5 = (bf16[2,128,128]{2,1,0:T(8,128)(2,1)S(1)}, bf16[2,128,128]{2,1,0:T(8,128)(2,1)S(1)}, u32[]{:S(2)}, u32[]{:S(2)}) collective-permute-start(bf16[2,128,128]{2,1,0:T(8,128)(2,1)S(1)} %fusion.1), channel_id=1, source_target_pairs={{0,2},{1,3},{2,0},{3,1},{4,6},{5,7},{6,4},{7,5},{8,10},{9,11},{10,... | collective-permute-start | bytes 196616 | tf_op jit(solution)/shard_map/ppermute | solution.py:36
  29.9 5.8 %collective-permute-start.6 = (bf16[2,128,128]{2,1,0:T(8,128)(2,1)S(1)}, bf16[2,128,128]{2,1,0:T(8,128)(2,1)S(1)}, u32[]{:S(2)}, u32[]{:S(2)}) collective-permute-start(bf16[2,128,128]{2,1,0:T(8,128)(2,1)S(1)} %fusion.5), channel_id=1, source_target_pairs={{0,4},{1,5},{2,6},{3,7},{4,0},{5,1},{6,2},{7,3},{8,12},{9,13},{10,... | collective-permute-start | bytes 196616 | tf_op jit(solution)/shard_map/ppermute | solution.py:36
  33.1 5.2 %collective-permute-start.7 = (f32[2,8192]{1,0:T(2,128)S(1)}, f32[2,8192]{1,0:T(2,128)S(1)}, u32[]{:S(2)}, u32[]{:S(2)}) collective-permute-start(f32[2,8192]{1,0:T(2,128)S(1)} %get-tuple-element.32), channel_id=1, source_target_pairs={{0,8},{8,16},{16,24},{24,0},{1,9},{9,17},{17,25},{25,1},{2,10},{10... | collective-permute-start | bytes 196616 | tf_op jit(solution)/shard_map/ppermute | solution.py:28
  40.2 5.4 %collective-permute-start.8 = (f32[2,8192]{1,0:T(2,128)S(1)}, f32[2,8192]{1,0:T(2,128)S(1)}, u32[]{:S(2)}, u32[]{:S(2)}) collective-permute-start(f32[2,8192]{1,0:T(2,128)S(1)} %get-tuple-element.33), channel_id=1, source_target_pairs={{0,8},{8,16},{16,24},{24,0},{1,9},{9,17},{17,25},{25,1},{2,10},{10... | collective-permute-start | bytes 196616 | tf_op jit(solution)/shard_map/ppermute | solution.py:28
  46.3 1.3 %collective-permute-start.9 = (bf16[2,128,128]{2,1,0:T(8,128)(2,1)S(1)}, bf16[2,128,128]{2,1,0:T(8,128)(2,1)S(1)}, u32[]{:S(2)}, u32[]{:S(2)}) collective-permute-start(bf16[2,128,128]{2,1,0:T(8,128)(2,1)S(1)} %convert_element_type.84), channel_id=1, source_target_pairs={{0,1},{1,0},{2,3},{3,2},{4,5},{5,4},{6,7},{7,6},{8,9},{9,8},{10,11... | collective-permute-start | bytes 196616 | tf_op jit(solution)/shard_map/ppermute | solution.py:36
  47.7 4.3 %collective-permute-start.10 = (bf16[2,128,128]{2,1,0:T(8,128)(2,1)S(1)}, bf16[2,128,128]{2,1,0:T(8,128)(2,1)S(1)}, u32[]{:S(2)}, u32[]{:S(2)}) collective-permute-start(bf16[2,128,128]{2,1,0:T(8,128)(2,1)S(1)} %fusion.2), channel_id=1, source_target_pairs={{0,2},{1,3},{2,0},{3,1},{4,6},{5,7},{6,4},{7,5},{8,10},{9,11},{10,... | collective-permute-start | bytes 196616 | tf_op jit(solution)/shard_map/ppermute | solution.py:36
  52.0 5.3 %collective-permute-start.11 = (bf16[2,128,128]{2,1,0:T(8,128)(2,1)S(1)}, bf16[2,128,128]{2,1,0:T(8,128)(2,1)S(1)}, u32[]{:S(2)}, u32[]{:S(2)}) collective-permute-start(bf16[2,128,128]{2,1,0:T(8,128)(2,1)S(1)} %fusion.6), channel_id=1, source_target_pairs={{0,4},{1,5},{2,6},{3,7},{4,0},{5,1},{6,2},{7,3},{8,12},{9,13},{10,... | collective-permute-start | bytes 196616 | tf_op jit(solution)/shard_map/ppermute | solution.py:36
  52.5 5.2 %collective-permute-start.12 = (f32[2,8192]{1,0:T(2,128)S(1)}, f32[2,8192]{1,0:T(2,128)S(1)}, u32[]{:S(2)}, u32[]{:S(2)}) collective-permute-start(f32[2,8192]{1,0:T(2,128)S(1)} %get-tuple-element.37), channel_id=1, source_target_pairs={{0,8},{8,16},{16,24},{24,0},{1,9},{9,17},{17,25},{25,1},{2,10},{10... | collective-permute-start | bytes 196616 | tf_op jit(solution)/shard_map/ppermute | solution.py:28
  59.5 5.2 %collective-permute-start.13 = (f32[2,8192]{1,0:T(2,128)S(1)}, f32[2,8192]{1,0:T(2,128)S(1)}, u32[]{:S(2)}, u32[]{:S(2)}) collective-permute-start(f32[2,8192]{1,0:T(2,128)S(1)} %get-tuple-element.38), channel_id=1, source_target_pairs={{0,8},{8,16},{16,24},{24,0},{1,9},{9,17},{17,25},{25,1},{2,10},{10... | collective-permute-start | bytes 196616 | tf_op jit(solution)/shard_map/ppermute | solution.py:28
  65.5 1.3 %collective-permute-start.14 = (bf16[2,128,128]{2,1,0:T(8,128)(2,1)S(1)}, bf16[2,128,128]{2,1,0:T(8,128)(2,1)S(1)}, u32[]{:S(2)}, u32[]{:S(2)}) collective-permute-start(bf16[2,128,128]{2,1,0:T(8,128)(2,1)S(1)} %convert_element_type.90), channel_id=1, source_target_pairs={{0,1},{1,0},{2,3},{3,2},{4,5},{5,4},{6,7},{7,6},{8,9},{9,8},{10,11... | collective-permute-start | bytes 196616 | tf_op jit(solution)/shard_map/ppermute | solution.py:36
  66.8 4.3 %collective-permute-start.15 = (bf16[2,128,128]{2,1,0:T(8,128)(2,1)S(1)}, bf16[2,128,128]{2,1,0:T(8,128)(2,1)S(1)}, u32[]{:S(2)}, u32[]{:S(2)}) collective-permute-start(bf16[2,128,128]{2,1,0:T(8,128)(2,1)S(1)} %fusion.3), channel_id=1, source_target_pairs={{0,2},{1,3},{2,0},{3,1},{4,6},{5,7},{6,4},{7,5},{8,10},{9,11},{10,... | collective-permute-start | bytes 196616 | tf_op jit(solution)/shard_map/ppermute | solution.py:36
  71.2 2.7 %copy-start.2 = (s32[1,64,1]{1,2,0:T(1,128)S(1)}, s32[1,64,1]{1,2,0:T(1,128)}, u32[]{:S(2)}) copy-start(s32[1,64,1]{1,2,0:T(1,128)} %param.9) | copy-start | bytes 772
  71.2 5.3 %collective-permute-start.16 = (bf16[2,128,128]{2,1,0:T(8,128)(2,1)S(1)}, bf16[2,128,128]{2,1,0:T(8,128)(2,1)S(1)}, u32[]{:S(2)}, u32[]{:S(2)}) collective-permute-start(bf16[2,128,128]{2,1,0:T(8,128)(2,1)S(1)} %fusion.7), channel_id=1, source_target_pairs={{0,4},{1,5},{2,6},{3,7},{4,0},{5,1},{6,2},{7,3},{8,12},{9,13},{10,... | collective-permute-start | bytes 196616 | tf_op jit(solution)/shard_map/ppermute | solution.py:36
  79.8 12.2 %all-to-all-start = ((f32[4,32,4,128]{3,2,1,0:T(4,128)}), f32[4,32,4,128]{3,2,1,0:T(4,128)S(1)}, u32[]{:S(2)}, u32[]{:S(2)}) async-start(f32[4,32,4,128]{3,2,1,0:T(4,128)} %bitcast.3), calls=%async_computation | async-start | bytes 524288 | tf_op jit(solution)/shard_map/all_to_all | solution.py:293
  83.2 6.7 %collective-permute-start.17 = (f32[2,8192]{1,0:T(2,128)S(1)}, f32[2,8192]{1,0:T(2,128)S(1)}, u32[]{:S(2)}, u32[]{:S(2)}) collective-permute-start(f32[2,8192]{1,0:T(2,128)S(1)} %get-tuple-element.45), channel_id=1, source_target_pairs={{0,8},{8,16},{16,24},{24,0},{1,9},{9,17},{17,25},{25,1},{2,10},{10... | collective-permute-start | bytes 196616 | tf_op jit(solution)/shard_map/ppermute | solution.py:28

commit v3 on v2

--- a/solution.py
+++ b/solution.py
@@ -100,25 +100,22 @@
     return high, (value - high.astype(jnp.float32)).astype(jnp.bfloat16)
 
 
-def tables(density, smooth, slope, scale):
-    high, low = halves(density.reshape(2 * GRID, GRID) * scale)
-    left = jnp.concatenate([high, low, high], axis=1)
+def table_of(density, smooth, slope, scale):
+    high, low = halves(density * scale)
     inner = lax.dot_general(
-        left,
+        jnp.concatenate([high, low, high], axis=1),
         jnp.concatenate([slope, smooth], axis=0),
         (((1,), (1,)), ((), ())),
         preferred_element_type=jnp.float32,
     )
     pushes = []
     for which, green in enumerate((smooth, slope)):
-        part = inner[:, which * GRID : (which + 1) * GRID]
-        high, low = halves(jnp.concatenate([part[:GRID], part[GRID:]], axis=1))
+        high, low = halves(inner[:, which * GRID : (which + 1) * GRID])
         right = jnp.concatenate([high, low, high], axis=0)
         pushes.append(jnp.dot(green, right, preferred_element_type=jnp.float32))
-    both = jnp.concatenate(
+    return jnp.concatenate(
         [push[start : start + LINES] for start in range(0, GRID, LINES) for push in pushes], axis=0
     ).astype(jnp.bfloat16)
-    return both[:, :GRID], both[:, GRID:]
 
 
 def greens_kernel(smooth_ref, slope_ref, *outs):
@@ -168,25 +165,25 @@
 
 
 def opposing_kernel(scale, density_ref, smooth_ref, slope_ref, *refs):
-    own, other = tables(density_ref[...], smooth_ref[...], slope_ref[...], scale)
-    *sources, place_ref, moment_ref, table_ref = refs
-    table_ref[...] = other
+    table = table_of(density_ref[0], smooth_ref[...], slope_ref[...], scale)
+    *sources, place_ref, moment_ref = refs
     for tile in columns(place_ref.shape[1]):
-        x, moment_x, y, moment_y = kick(*rows(sources, tile), own)
+        x, moment_x, y, moment_y = kick(*rows(sources, tile), table)
         place_ref[0:1, tile] = x[:1]
         place_ref[1:2, tile] = y[:1]
         moment_ref[0:1, tile] = moment_x[:1]
         moment_ref[1:2, tile] = moment_y[:1]
 
 
-def resident_kernel(table_ref, beam_ref, moved_ref, density_ref):
+def resident_kernel(scale, density_ref, smooth_ref, slope_ref, beam_ref, moved_ref, part_ref):
+    table = table_of(density_ref[1], smooth_ref[...], slope_ref[...], scale)
     total = 0.0
     for tile in columns(beam_ref.shape[1]):
-        new = kick(*rows([beam_ref], tile), table_ref[...])
+        new = kick(*rows([beam_ref], tile), table)
         for row in range(4):
             moved_ref[row : row + 1, tile] = new[row][:1]
         total = total + deposit(new[0], new[2])
-    density_ref[...] = total
+    part_ref[...] = total
 
 
 def arrival_kernel(place_ref, resident_ref, density_ref):
@@ -196,22 +193,39 @@
     )
 
 
-def last_kernel(scale, slots_ref, density_ref, smooth_ref, slope_ref, beam_ref, packed_ref, table_ref, moved_ref):
-    table_ref[...], other = tables(density_ref[...], smooth_ref[...], slope_ref[...], scale)
-    packed_ref[...] = jnp.zeros_like(packed_ref)
+def last_kernel(scale, slots_ref, density_ref, smooth_ref, slope_ref, beam_ref, *refs):
+    *packed, moved_ref, slots_out = refs
+    table = table_of(density_ref[1], smooth_ref[...], slope_ref[...], scale)
+    slots_out[...] = jnp.zeros_like(slots_out)
     for tile in columns(beam_ref.shape[1]):
-        new = kick(*rows([beam_ref], tile), other)
+        new = kick(*rows([beam_ref], tile), table)
         for row in range(4):
             moved_ref[row : row + 1, tile] = new[row][:1]
     for block in range(beam_ref.shape[1] // BLOCK):
-        packed_ref[slots_ref[block]] = moved_ref[:, block * BLOCK : (block + 1) * BLOCK]
-
-
-def final_kernel(table_ref, place_ref, moment_ref, out_ref):
+        slots_out[slots_ref[block]] = moved_ref[:, block * BLOCK : (block + 1) * BLOCK]
+    for distance, ref in enumerate(packed):
+        capacity = ref.shape[0]
+        ref[...] = slots_out[distance * capacity : (distance + 1) * capacity]
+
+
+def final_kernel(scale, density_ref, smooth_ref, slope_ref, place_ref, moment_ref, out_ref):
+    table = table_of(density_ref[0], smooth_ref[...], slope_ref[...], scale)
     for tile in columns(place_ref.shape[1]):
-        new = kick(*rows([place_ref, moment_ref], tile), table_ref[...])
+        new = kick(*rows([place_ref, moment_ref], tile), table)
         for row in range(4):
             out_ref[row : row + 1, tile] = new[row][:1]
+
+
+def gather_kernel(me_ref, *refs):
+    *parts, out_hbm, landed = refs
+    copies = [
+        pltpu.make_async_copy(part, out_hbm.at[me_ref[0] ^ distance], landed.at[distance])
+        for distance, part in enumerate(parts)
+    ]
+    for copy in copies:
+        copy.start()
+    for copy in copies:
+        copy.wait()
 
 
 def local(kernel, out_shape, **options):
@@ -227,15 +241,15 @@
     return jax.ShapeDtypeStruct(shape, dtype)
 
 
-def slots_kernel(capacity, routes_ref, slots_ref, taken_ref):
+def slots_kernel(capacity, me_ref, routes_ref, slots_ref, taken_ref):
     for station in range(taken_ref.shape[0]):
         taken_ref[station] = 0
 
     def place(block, carry):
-        station = routes_ref[block]
-        taken = taken_ref[station]
-        slots_ref[block] = station * capacity + jnp.minimum(taken, capacity - 1)
-        taken_ref[station] = taken + 1
+        distance = routes_ref[block] ^ me_ref[0]
+        taken = taken_ref[distance]
+        slots_ref[block] = distance * capacity + jnp.minimum(taken, capacity - 1)
+        taken_ref[distance] = taken + 1
         return carry
 
     lax.fori_loop(0, routes_ref.shape[0], place, 0)
@@ -252,15 +266,15 @@
     scale = STRENGTH * GRID * GRID / (count * groups)
     half, whole = array(2, count), array(4, count)
     density, densities = array(GRID, GRID), array(2, GRID, GRID)
-    table = array(2 * GRID, GRID, dtype=jnp.bfloat16)
+    me = jnp.full((1,), lax.axis_index("station"), jnp.int32)
     vmem, smem = (pl.BlockSpec(memory_space=space) for space in (pltpu.VMEM, pltpu.SMEM))
     place = local(
         functools.partial(slots_kernel, capacity),
         array(block_count, dtype=jnp.int32),
-        in_specs=[smem],
+        in_specs=[smem] * 2,
         out_specs=smem,
         scratch_shapes=[pltpu.SMEM((stations,), jnp.int32)],
-    )(destination[0, :, 0])
+    )(me, destination[0, :, 0])
 
     resident, *opposing, total = local(
         first_kernel,
@@ -273,25 +287,42 @@
     smooth, slope = local(greens_kernel, (wide, wide))(green_smooth, green_slope)
     total = summed(total, "dom")
     for _ in range(FRONTS - 1):
-        positions, moments, other = local(
-            functools.partial(opposing_kernel, scale), (half, half, table)
-        )(total, smooth, slope, *opposing)
+        positions, moments = local(functools.partial(opposing_kernel, scale), (half, half))(
+            total, smooth, slope, *opposing
+        )
         positions = shifted(positions, "station", 1)
         moments = shifted(moments, "station", 1)
         opposing = (positions, moments)
-        resident, part = local(resident_kernel, (whole, density))(other, resident)
+        resident, part = local(
+            functools.partial(resident_kernel, scale), (whole, density)
+        )(total, smooth, slope, resident)
         total = local(arrival_kernel, densities)(positions, part)
         total = summed(total, "dom")
-    outgoing, own = local(
+    blocks = array(capacity, 4, BLOCK)
+    parts = local(
         functools.partial(last_kernel, scale),
-        (array(stations * capacity, 4, BLOCK), table),
+        (blocks,) * stations,
         in_specs=[smem] + [vmem] * 4,
-        out_specs=(vmem, vmem),
-        scratch_shapes=[pltpu.VMEM((4, count), jnp.float32)],
+        out_specs=(vmem,) * stations,
+        scratch_shapes=[
+            pltpu.VMEM((4, count), jnp.float32),
+            pltpu.VMEM((stations * capacity, 4, BLOCK), jnp.float32),
+        ],
     )(place, total, smooth, slope, resident)
-    outgoing = outgoing.reshape(stations, capacity, 4, BLOCK)
-    arrived = lax.all_to_all(outgoing, "station", split_axis=0, concat_axis=0, tiled=True)
-    opposing = local(final_kernel, whole)(own, *opposing)
+    parts = [
+        lax.ppermute(part, "station", [(source, source ^ distance) for source in range(stations)])
+        if distance
+        else part
+        for distance, part in enumerate(parts)
+    ]
+    opposing = local(functools.partial(final_kernel, scale), whole)(total, smooth, slope, *opposing)
+    arrived = local(
+        gather_kernel,
+        array(stations, capacity, 4, BLOCK),
+        in_specs=[smem] + [vmem] * stations,
+        out_specs=pl.BlockSpec(memory_space=pltpu.HBM),
+        scratch_shapes=[pltpu.SemaphoreType.DMA((stations,))],
+    )(me, *parts)
     return (arrived[None, None], opposing[None, None])
 
 

time: 92.9 us -> 88.4 us (0.952)
  waiting for transfers between devices: 38.5 us -> 32.7 us
  Pallas kernels: 25.4 us -> 26.9 us
    ppermute x6, waiting for transfers between devices: 14.9 us -> 8.78 us  [shifted(): return lax.ppermute(value, axis, pairs)]
    ppermute x0 -> x3, starting transfers between devices: none -> 4.19 us  [shards(): lax.ppermute(part, 'station', [(source, source ^ distance) for source in...]
    all_to_all x1 -> x0, starting transfers between devices: 3.41 us -> none  [shards(): lax.all_to_all(outgoing, 'station', split_axis=0, concat_axis=0, tiled=True)]
    ppermute x0 -> x3, waiting for transfers between devices: none -> 1.62 us  [shards(): lax.ppermute(part, 'station', [(source, source ^ distance) for source in...]
    pallas_call x8 -> x9, Pallas kernels: 17.5 us -> 18.9 us  [the longest x3 7.69 us: shards(): local(functools.partial(resident_kernel, scale), (whole, density))]
    ppermute x12, waiting for transfers between devices: 23.7 us -> 22.4 us  [summed(): other = lax.ppermute(value.astype(jnp.bfloat16), axis, pairs)]
    ppermute x6, starting transfers between devices: 4.66 us -> 3.66 us  [shifted(): return lax.ppermute(value, axis, pairs)]
  transfers between devices with their start and end apart: 19 -> 21, of which waited for: 18 -> 18; matrix products, arithmetic and copies ran while one was open for 0% -> 0% of each run, Pallas kernels for 12% -> 17%
where the time goes in v3:
time: 88.4 us; the launch traced here: 88.2 us
  waiting for transfers between devices  32.7 us (37%)
  Pallas kernels  26.9 us (30%)
  starting transfers between devices  26.5 us (30%)
  between operations  1.03 us (1%)
    ppermute x12, waiting for transfers between devices, summed(): other = lax.ppermute(value.astype(jnp.bfloat16), axis, pairs)  22.4 us
    ppermute x12, starting transfers between devices, summed(): other = lax.ppermute(value.astype(jnp.bfloat16), axis, pairs)  18.7 us
    ppermute x6, waiting for transfers between devices, shifted(): return lax.ppermute(value, axis, pairs)  8.78 us
    pallas_call x3, Pallas kernels, shards(): local(functools.partial(resident_kernel, scale), (whole, density))  7.69 us
    pallas_call x3, Pallas kernels, shards(): local(functools.partial(opposing_kernel, scale), (half, half))  5.53 us
    ppermute x3, starting transfers between devices, shards(): lax.ppermute(part, 'station', [(source, source ^ distance) for source in...  4.19 us
    ppermute x6, starting transfers between devices, shifted(): return lax.ppermute(value, axis, pairs)  3.66 us
    pallas_call x1, Pallas kernels, shards(): local(first_kernel, (whole, whole, densities), in_specs=[pl.BlockSpec(mem...  3.4 us
  transfers between devices with their start and end apart: 21, of which 18 were waited for; matrix products, arithmetic and copies ran while one was open for 0% of the time, Pallas kernels for 17%

profile of v3, /device:TPU:0, one launch (start us, length us, event | category | flops | bytes accessed | tf_op | source)
XLA Modules:
  0.0 88.2 jit_solution(4550413202957125952)
XLA Ops:
  0.6 3.4 %shard_map.69 = (f32[4,8192]{1,0:T(4,128)S(1)}, f32[4,8192]{1,0:T(4,128)S(1)}, f32[2,128,128]{2,1,0:T(8,128)S(1)}) custom-call(f32[4,8192]{1,0:T(4,128)} %bitcast.8, f32[4,8192]{1,0:T(4,128)} %bitcast.9), custom_call_target="tpu_custom_call" | custom-call | tf_op jit(solution)/shard_map/pallas_call | solution.py:279
  4.1 0.6 collective-permute-start
  4.6 0.9 %collective-permute-done = bf16[2,128,128]{2,1,0:T(8,128)(2,1)S(1)} collective-permute-done((bf16[2,128,128]{2,1,0:T(8,128)(2,1)S(1)}, bf16[2,128,128]{2,1,0:T(8,128)(2,1)S(1)}, u32[]{:S(2)}, u32[]{:S(2)}) %collective-permute-start) | collective-permute-done | bytes 65568 | tf_op jit(solution)/shard_map/ppermute | solution.py:36
  5.6 3.0 %collective-permute-start.1 = (bf16[2,128,128]{2,1,0:T(8,128)(2,1)S(1)}, bf16[2,128,128]{2,1,0:T(8,128)(2,1)S(1)}, u32[]{:S(2)}, u32[]{:S(2)}) collective-permute-start(bf16[2,128,128]{2,1,0:T(8,128)(2,1)S(1)} %fusion), channel_id=1, source_target_pairs={{0,2},{1,3},{2,0},{3,1},{4,6},{5,7},{6,4},{7,5},{8,10},{9,11},{10,... | collective-permute-start | bytes 196616 | tf_op jit(solution)/shard_map/ppermute | solution.py:36
  8.5 2.4 %collective-permute-done.1 = bf16[2,128,128]{2,1,0:T(8,128)(2,1)S(1)} collective-permute-done((bf16[2,128,128]{2,1,0:T(8,128)(2,1)S(1)}, bf16[2,128,128]{2,1,0:T(8,128)(2,1)S(1)}, u32[]{:S(2)}, u32[]{:S(2)}) %collective-permute-start.1) | collective-permute-done | bytes 65568 | tf_op jit(solution)/shard_map/ppermute | solution.py:36
  11.0 2.9 %collective-permute-start.2 = (bf16[2,128,128]{2,1,0:T(8,128)(2,1)S(1)}, bf16[2,128,128]{2,1,0:T(8,128)(2,1)S(1)}, u32[]{:S(2)}, u32[]{:S(2)}) collective-permute-start(bf16[2,128,128]{2,1,0:T(8,128)(2,1)S(1)} %fusion.4), channel_id=1, source_target_pairs={{0,4},{1,5},{2,6},{3,7},{4,0},{5,1},{6,2},{7,3},{8,12},{9,13},{10,... | collective-permute-start | bytes 196616 | tf_op jit(solution)/shard_map/ppermute | solution.py:36
  13.9 0.7 shard_map.70
  14.6 1.6 %collective-permute-done.2 = bf16[2,128,128]{2,1,0:T(8,128)(2,1)S(1)} collective-permute-done((bf16[2,128,128]{2,1,0:T(8,128)(2,1)S(1)}, bf16[2,128,128]{2,1,0:T(8,128)(2,1)S(1)}, u32[]{:S(2)}, u32[]{:S(2)}) %collective-permute-start.2) | collective-permute-done | bytes 65568 | tf_op jit(solution)/shard_map/ppermute | solution.py:36
  16.3 1.8 %shard_map.71 = (f32[2,8192]{1,0:T(2,128)S(1)}, f32[2,8192]{1,0:T(2,128)S(1)}) custom-call(f32[2,128,128]{2,1,0:T(8,128)S(1)} %convert_add_fusion.9.density_ref, bf16[128,384]{1,0:T(8,128)(2,1)S(1)} %get-tuple-element.24.smooth_ref, bf16[128,384]{1,0:T(8,128)(2,1)S(1)} %get-tuple-element.25.slope_ref, f32[4,8192]{1,0:T(4,128)S(1)} %get-tuple-element.26.refs_0_), custom_call_target="tpu_custom_call" | custom-call | tf_op jit(solution)/shard_map/pallas_call | solution.py:290
  18.1 1.8 %collective-permute-start.3 = (f32[2,8192]{1,0:T(2,128)S(1)}, f32[2,8192]{1,0:T(2,128)S(1)}, u32[]{:S(2)}, u32[]{:S(2)}) collective-permute-start(f32[2,8192]{1,0:T(2,128)S(1)} %get-tuple-element.27), channel_id=1, source_target_pairs={{0,8},{8,16},{16,24},{24,0},{1,9},{9,17},{17,25},{25,1},{2,10},{10... | collective-permute-start | bytes 196616 | tf_op jit(solution)/shard_map/ppermute | solution.py:28
  19.9 2.6 %shard_map.72 = (f32[4,8192]{1,0:T(4,128)S(1)}, f32[128,128]{1,0:T(8,128)S(1)}) custom-call(f32[2,128,128]{2,1,0:T(8,128)S(1)} %convert_add_fusion.9.density_ref, bf16[128,384]{1,0:T(8,128)(2,1)S(1)} %get-tuple-element.24.smooth_ref, bf16[128,384]{1,0:T(8,128)(2,1)S(1)} %get-tuple-element.25.slope_ref, f32[4,8192]{1,0:T(4,128)S(1)} %get-tuple-element.28.beam_ref), custom_call_target="tpu_custom_call" | custom-call | tf_op jit(solution)/shard_map/pallas_call | solution.py:296
  22.5 0.9 collective-permute-done.3.place_ref.refs_0_
  23.3 0.7 shard_map.73
  24.2 1.2 %collective-permute-done.4 = bf16[2,128,128]{2,1,0:T(8,128)(2,1)S(1)} collective-permute-done((bf16[2,128,128]{2,1,0:T(8,128)(2,1)S(1)}, bf16[2,128,128]{2,1,0:T(8,128)(2,1)S(1)}, u32[]{:S(2)}, u32[]{:S(2)}) %collective-permute-start.4) | collective-permute-done | bytes 65568 | tf_op jit(solution)/shard_map/ppermute | solution.py:36
  25.4 1.9 %collective-permute-start.5 = (bf16[2,128,128]{2,1,0:T(8,128)(2,1)S(1)}, bf16[2,128,128]{2,1,0:T(8,128)(2,1)S(1)}, u32[]{:S(2)}, u32[]{:S(2)}) collective-permute-start(bf16[2,128,128]{2,1,0:T(8,128)(2,1)S(1)} %fusion.1), channel_id=1, source_target_pairs={{0,2},{1,3},{2,0},{3,1},{4,6},{5,7},{6,4},{7,5},{8,10},{9,11},{10,... | collective-permute-start | bytes 196616 | tf_op jit(solution)/shard_map/ppermute | solution.py:36
  27.3 2.4 %collective-permute-done.5 = bf16[2,128,128]{2,1,0:T(8,128)(2,1)S(1)} collective-permute-done((bf16[2,128,128]{2,1,0:T(8,128)(2,1)S(1)}, bf16[2,128,128]{2,1,0:T(8,128)(2,1)S(1)}, u32[]{:S(2)}, u32[]{:S(2)}) %collective-permute-start.5) | collective-permute-done | bytes 65568 | tf_op jit(solution)/shard_map/ppermute | solution.py:36
  29.8 3.2 %collective-permute-start.6 = (bf16[2,128,128]{2,1,0:T(8,128)(2,1)S(1)}, bf16[2,128,128]{2,1,0:T(8,128)(2,1)S(1)}, u32[]{:S(2)}, u32[]{:S(2)}) collective-permute-start(bf16[2,128,128]{2,1,0:T(8,128)(2,1)S(1)} %fusion.5), channel_id=1, source_target_pairs={{0,4},{1,5},{2,6},{3,7},{4,0},{5,1},{6,2},{7,3},{8,12},{9,13},{10,... | collective-permute-start | bytes 196616 | tf_op jit(solution)/shard_map/ppermute | solution.py:36
  33.0 0.6 collective-permute-start.7
  33.6 2.0 %collective-permute-done.6 = bf16[2,128,128]{2,1,0:T(8,128)(2,1)S(1)} collective-permute-done((bf16[2,128,128]{2,1,0:T(8,128)(2,1)S(1)}, bf16[2,128,128]{2,1,0:T(8,128)(2,1)S(1)}, u32[]{:S(2)}, u32[]{:S(2)}) %collective-permute-start.6) | collective-permute-done | bytes 65568 | tf_op jit(solution)/shard_map/ppermute | solution.py:36
  35.6 2.6 %collective-permute-done.7.refs_1_ = f32[2,8192]{1,0:T(2,128)S(1)} collective-permute-done((f32[2,8192]{1,0:T(2,128)S(1)}, f32[2,8192]{1,0:T(2,128)S(1)}, u32[]{:S(2)}, u32[]{:S(2)}) %collective-permute-start.7) | collective-permute-done | bytes 65568 | tf_op jit(solution)/shard_map/ppermute | solution.py:28
  38.2 1.8 %shard_map.74 = (f32[2,8192]{1,0:T(2,128)S(1)}, f32[2,8192]{1,0:T(2,128)S(1)}) custom-call(f32[2,128,128]{2,1,0:T(8,128)S(1)} %convert_add_fusion.6.density_ref, bf16[128,384]{1,0:T(8,128)(2,1)S(1)} %get-tuple-element.24.smooth_ref, bf16[128,384]{1,0:T(8,128)(2,1)S(1)} %get-tuple-element.25.slope_ref, ...), custom_call_target="tpu_custom_call" | custom-call | tf_op jit(solution)/shard_map/pallas_call | solution.py:290
  40.3 2.6 %shard_map.75 = (f32[4,8192]{1,0:T(4,128)S(1)}, f32[128,128]{1,0:T(8,128)S(1)}) custom-call(f32[2,128,128]{2,1,0:T(8,128)S(1)} %convert_add_fusion.6.density_ref, bf16[128,384]{1,0:T(8,128)(2,1)S(1)} %get-tuple-element.24.smooth_ref, bf16[128,384]{1,0:T(8,128)(2,1)S(1)} %get-tuple-element.25.slope_ref, f32[4,8192]{1,0:T(4,128)S(1)} %get-tuple-element.32.beam_ref), custom_call_target="tpu_custom_call" | custom-call | tf_op jit(solution)/shard_map/pallas_call | solution.py:296
  42.8 2.6 %collective-permute-done.8.place_ref.refs_0_ = f32[2,8192]{1,0:T(2,128)S(1)} collective-permute-done((f32[2,8192]{1,0:T(2,128)S(1)}, f32[2,8192]{1,0:T(2,128)S(1)}, u32[]{:S(2)}, u32[]{:S(2)}) %collective-permute-start.8) | collective-permute-done | bytes 65568 | tf_op jit(solution)/shard_map/ppermute | solution.py:28
  45.4 0.7 shard_map.76
  46.2 1.2 %collective-permute-done.9 = bf16[2,128,128]{2,1,0:T(8,128)(2,1)S(1)} collective-permute-done((bf16[2,128,128]{2,1,0:T(8,128)(2,1)S(1)}, bf16[2,128,128]{2,1,0:T(8,128)(2,1)S(1)}, u32[]{:S(2)}, u32[]{:S(2)}) %collective-permute-start.9) | collective-permute-done | bytes 65568 | tf_op jit(solution)/shard_map/ppermute | solution.py:36
  47.5 1.9 %collective-permute-start.10 = (bf16[2,128,128]{2,1,0:T(8,128)(2,1)S(1)}, bf16[2,128,128]{2,1,0:T(8,128)(2,1)S(1)}, u32[]{:S(2)}, u32[]{:S(2)}) collective-permute-start(bf16[2,128,128]{2,1,0:T(8,128)(2,1)S(1)} %fusion.2), channel_id=1, source_target_pairs={{0,2},{1,3},{2,0},{3,1},{4,6},{5,7},{6,4},{7,5},{8,10},{9,11},{10,... | collective-permute-start | bytes 196616 | tf_op jit(solution)/shard_map/ppermute | solution.py:36
  49.4 2.4 %collective-permute-done.10 = bf16[2,128,128]{2,1,0:T(8,128)(2,1)S(1)} collective-permute-done((bf16[2,128,128]{2,1,0:T(8,128)(2,1)S(1)}, bf16[2,128,128]{2,1,0:T(8,128)(2,1)S(1)}, u32[]{:S(2)}, u32[]{:S(2)}) %collective-permute-start.10) | collective-permute-done | bytes 65568 | tf_op jit(solution)/shard_map/ppermute | solution.py:36
  51.9 0.4 collective-permute-start.11
  52.3 0.4 collective-permute-start.12
  52.7 4.4 %collective-permute-done.11 = bf16[2,128,128]{2,1,0:T(8,128)(2,1)S(1)} collective-permute-done((bf16[2,128,128]{2,1,0:T(8,128)(2,1)S(1)}, bf16[2,128,128]{2,1,0:T(8,128)(2,1)S(1)}, u32[]{:S(2)}, u32[]{:S(2)}) %collective-permute-start.11) | collective-permute-done | bytes 65568 | tf_op jit(solution)/shard_map/ppermute | solution.py:36
  57.5 1.8 %shard_map.77 = (f32[2,8192]{1,0:T(2,128)S(1)}, f32[2,8192]{1,0:T(2,128)S(1)}) custom-call(f32[2,128,128]{2,1,0:T(8,128)S(1)} %convert_add_fusion.3.density_ref, bf16[128,384]{1,0:T(8,128)(2,1)S(1)} %get-tuple-element.24.smooth_ref, bf16[128,384]{1,0:T(8,128)(2,1)S(1)} %get-tuple-element.25.slope_ref, ...), custom_call_target="tpu_custom_call" | custom-call | tf_op jit(solution)/shard_map/pallas_call | solution.py:290
  59.5 2.6 %shard_map.78 = (f32[4,8192]{1,0:T(4,128)S(1)}, f32[128,128]{1,0:T(8,128)S(1)}) custom-call(f32[2,128,128]{2,1,0:T(8,128)S(1)} %convert_add_fusion.3.density_ref, bf16[128,384]{1,0:T(8,128)(2,1)S(1)} %get-tuple-element.24.smooth_ref, bf16[128,384]{1,0:T(8,128)(2,1)S(1)} %get-tuple-element.25.slope_ref, f32[4,8192]{1,0:T(4,128)S(1)} %get-tuple-element.36.beam_ref), custom_call_target="tpu_custom_call" | custom-call | tf_op jit(solution)/shard_map/pallas_call | solution.py:296
  62.1 2.5 %collective-permute-done.13.place_ref = f32[2,8192]{1,0:T(2,128)S(1)} collective-permute-done((f32[2,8192]{1,0:T(2,128)S(1)}, f32[2,8192]{1,0:T(2,128)S(1)}, u32[]{:S(2)}, u32[]{:S(2)}) %collective-permute-start.13) | collective-permute-done | bytes 65568 | tf_op jit(solution)/shard_map/ppermute | solution.py:28
  64.5 0.7 shard_map.79
  65.4 1.2 %collective-permute-done.14 = bf16[2,128,128]{2,1,0:T(8,128)(2,1)S(1)} collective-permute-done((bf16[2,128,128]{2,1,0:T(8,128)(2,1)S(1)}, bf16[2,128,128]{2,1,0:T(8,128)(2,1)S(1)}, u32[]{:S(2)}, u32[]{:S(2)}) %collective-permute-start.14) | collective-permute-done | bytes 65568 | tf_op jit(solution)/shard_map/ppermute | solution.py:36
  66.6 1.9 %collective-permute-start.15 = (bf16[2,128,128]{2,1,0:T(8,128)(2,1)S(1)}, bf16[2,128,128]{2,1,0:T(8,128)(2,1)S(1)}, u32[]{:S(2)}, u32[]{:S(2)}) collective-permute-start(bf16[2,128,128]{2,1,0:T(8,128)(2,1)S(1)} %fusion.3), channel_id=1, source_target_pairs={{0,2},{1,3},{2,0},{3,1},{4,6},{5,7},{6,4},{7,5},{8,10},{9,11},{10,... | collective-permute-start | bytes 196616 | tf_op jit(solution)/shard_map/ppermute | solution.py:36
  68.5 2.4 %collective-permute-done.15 = bf16[2,128,128]{2,1,0:T(8,128)(2,1)S(1)} collective-permute-done((bf16[2,128,128]{2,1,0:T(8,128)(2,1)S(1)}, bf16[2,128,128]{2,1,0:T(8,128)(2,1)S(1)}, u32[]{:S(2)}, u32[]{:S(2)}) %collective-permute-start.15) | collective-permute-done | bytes 65568 | tf_op jit(solution)/shard_map/ppermute | solution.py:36
  71.0 2.6 %collective-permute-start.16 = (bf16[2,128,128]{2,1,0:T(8,128)(2,1)S(1)}, bf16[2,128,128]{2,1,0:T(8,128)(2,1)S(1)}, u32[]{:S(2)}, u32[]{:S(2)}) collective-permute-start(bf16[2,128,128]{2,1,0:T(8,128)(2,1)S(1)} %fusion.7), channel_id=1, source_target_pairs={{0,4},{1,5},{2,6},{3,7},{4,0},{5,1},{6,2},{7,3},{8,12},{9,13},{10,... | collective-permute-start | bytes 196616 | tf_op jit(solution)/shard_map/ppermute | solution.py:36
  73.6 0.7 copy-done.2
  74.3 1.8 %shard_map.68.slots_ref = s32[64]{0:T(128)S(1)} custom-call(s32[1]{0:T(128)} %bitcast.me_ref, s32[64]{0:T(128)S(1)} %bitcast.6), custom_call_target="tpu_custom_call" | custom-call | tf_op jit(solution)/shard_map/pallas_call | solution.py:271
  76.1 0.5 collective-permute-start.20
  76.6 2.5 %shard_map.80 = (f32[32,4,128]{2,1,0:T(4,128)S(1)}, f32[32,4,128]{2,1,0:T(4,128)S(1)}, f32[32,4,128]{2,1,0:T(4,128)S(1)}, f32[32,4,128]{2,1,0:T(4,128)S(1)}) custom-call(s32[64]{0:T(128)S(1)} %shard_map.68.slots_ref, f32[2,128,128]{2,1,0:T(8,128)S(1)} %convert_add_fusion.density_ref, bf16[128,384]{1,0:T(8,128)(2,1)S(1)} %get-tuple-element.24.smooth_ref, ...), custom_call_target="tpu_custom_call" | custom-call | tf_op jit(solution)/shard_map/pallas_call | solution.py:302
  79.0 2.6 %collective-permute-start.17 = (f32[32,4,128]{2,1,0:T(4,128)S(1)}, f32[32,4,128]{2,1,0:T(4,128)S(1)}, u32[]{:S(2)}, u32[]{:S(2)}) collective-permute-start(f32[32,4,128]{2,1,0:T(4,128)S(1)} %get-tuple-element.40), channel_id=1, source_target_pairs={{0,8},{8,0},{16,24},{24,16},{1,9},{9,1},{17,25},{25,17},{2,10},{10... | collective-permute-start | bytes 196616 | tf_op jit(solution)/shard_map/ppermute | solution.py:313
  81.7 0.5 collective-permute-start.18
  82.2 1.0 %collective-permute-start.19 = (f32[32,4,128]{2,1,0:T(4,128)S(1)}, f32[32,4,128]{2,1,0:T(4,128)S(1)}, u32[]{:S(2)}, u32[]{:S(2)}) collective-permute-start(f32[32,4,128]{2,1,0:T(4,128)S(1)} %get-tuple-element.42), channel_id=1, source_target_pairs={{0,24},{8,16},{16,8},{24,0},{1,25},{9,17},{17,9},{25,1},{2,26},{10... | collective-permute-start | bytes 196616 | tf_op jit(solution)/shard_map/ppermute | solution.py:313
  83.2 2.5 %shard_map.82 = f32[4,8192]{1,0:T(4,128)} custom-call(f32[2,128,128]{2,1,0:T(8,128)S(1)} %convert_add_fusion.density_ref, bf16[128,384]{1,0:T(8,128)(2,1)S(1)} %get-tuple-element.24.smooth_ref, bf16[128,384]{1,0:T(8,128)(2,1)S(1)} %get-tuple-element.25.slope_ref, f32[2,8192]{1,0:T(2,128)S(1)} %collective-permute-done.13.place_ref, ...), custom_call_target="tpu_custom_call" | custom-call | tf_op jit(solution)/shard_map/pallas_call | solution.py:318
  86.0 1.4 %collective-permute-done.19.refs_3_ = f32[32,4,128]{2,1,0:T(4,128)S(1)} collective-permute-done((f32[32,4,128]{2,1,0:T(4,128)S(1)}, f32[32,4,128]{2,1,0:T(4,128)S(1)}, u32[]{:S(2)}, u32[]{:S(2)}) %collective-permute-start.19) | collective-permute-done | bytes 65568 | tf_op jit(solution)/shard_map/ppermute | solution.py:313
  87.4 0.7 shard_map.81
  (31 shorter events, 1.5 us)
Async XLA Ops:
  4.1 1.5 %collective-permute-start = (bf16[2,128,128]{2,1,0:T(8,128)(2,1)S(1)}, bf16[2,128,128]{2,1,0:T(8,128)(2,1)S(1)}, u32[]{:S(2)}, u32[]{:S(2)}) collective-permute-start(bf16[2,128,128]{2,1,0:T(8,128)(2,1)S(1)} %convert_element_type.72), channel_id=1, source_target_pairs={{0,1},{1,0},{2,3},{3,2},{4,5},{5,4},{6,7},{7,6},{8,9},{9,8},{10,11... | collective-permute-start | bytes 196616 | tf_op jit(solution)/shard_map/ppermute | solution.py:36
  5.5 8.4 %copy-start = (f32[128,128]{1,0:T(8,128)S(1)}, f32[128,128]{1,0:T(8,128)}, u32[]{:S(2)}) copy-start(f32[128,128]{1,0:T(8,128)} %smooth_ref.1) | copy-start | bytes 196612
  5.5 8.4 %copy-start.1 = (f32[128,128]{1,0:T(8,128)S(1)}, f32[128,128]{1,0:T(8,128)}, u32[]{:S(2)}) copy-start(f32[128,128]{1,0:T(8,128)} %slope_ref.1) | copy-start | bytes 196612
  5.6 5.4 %collective-permute-start.1 = (bf16[2,128,128]{2,1,0:T(8,128)(2,1)S(1)}, bf16[2,128,128]{2,1,0:T(8,128)(2,1)S(1)}, u32[]{:S(2)}, u32[]{:S(2)}) collective-permute-start(bf16[2,128,128]{2,1,0:T(8,128)(2,1)S(1)} %fusion), channel_id=1, source_target_pairs={{0,2},{1,3},{2,0},{3,1},{4,6},{5,7},{6,4},{7,5},{8,10},{9,11},{10,... | collective-permute-start | bytes 196616 | tf_op jit(solution)/shard_map/ppermute | solution.py:36
  11.0 5.3 %collective-permute-start.2 = (bf16[2,128,128]{2,1,0:T(8,128)(2,1)S(1)}, bf16[2,128,128]{2,1,0:T(8,128)(2,1)S(1)}, u32[]{:S(2)}, u32[]{:S(2)}) collective-permute-start(bf16[2,128,128]{2,1,0:T(8,128)(2,1)S(1)} %fusion.4), channel_id=1, source_target_pairs={{0,4},{1,5},{2,6},{3,7},{4,0},{5,1},{6,2},{7,3},{8,12},{9,13},{10,... | collective-permute-start | bytes 196616 | tf_op jit(solution)/shard_map/ppermute | solution.py:36
  18.1 5.2 %collective-permute-start.3 = (f32[2,8192]{1,0:T(2,128)S(1)}, f32[2,8192]{1,0:T(2,128)S(1)}, u32[]{:S(2)}, u32[]{:S(2)}) collective-permute-start(f32[2,8192]{1,0:T(2,128)S(1)} %get-tuple-element.27), channel_id=1, source_target_pairs={{0,8},{8,16},{16,24},{24,0},{1,9},{9,17},{17,25},{25,1},{2,10},{10... | collective-permute-start | bytes 196616 | tf_op jit(solution)/shard_map/ppermute | solution.py:28
  24.1 1.3 %collective-permute-start.4 = (bf16[2,128,128]{2,1,0:T(8,128)(2,1)S(1)}, bf16[2,128,128]{2,1,0:T(8,128)(2,1)S(1)}, u32[]{:S(2)}, u32[]{:S(2)}) collective-permute-start(bf16[2,128,128]{2,1,0:T(8,128)(2,1)S(1)} %convert_element_type.78), channel_id=1, source_target_pairs={{0,1},{1,0},{2,3},{3,2},{4,5},{5,4},{6,7},{7,6},{8,9},{9,8},{10,11... | collective-permute-start | bytes 196616 | tf_op jit(solution)/shard_map/ppermute | solution.py:36
  25.4 4.3 %collective-permute-start.5 = (bf16[2,128,128]{2,1,0:T(8,128)(2,1)S(1)}, bf16[2,128,128]{2,1,0:T(8,128)(2,1)S(1)}, u32[]{:S(2)}, u32[]{:S(2)}) collective-permute-start(bf16[2,128,128]{2,1,0:T(8,128)(2,1)S(1)} %fusion.1), channel_id=1, source_target_pairs={{0,2},{1,3},{2,0},{3,1},{4,6},{5,7},{6,4},{7,5},{8,10},{9,11},{10,... | collective-permute-start | bytes 196616 | tf_op jit(solution)/shard_map/ppermute | solution.py:36
  29.8 5.8 %collective-permute-start.6 = (bf16[2,128,128]{2,1,0:T(8,128)(2,1)S(1)}, bf16[2,128,128]{2,1,0:T(8,128)(2,1)S(1)}, u32[]{:S(2)}, u32[]{:S(2)}) collective-permute-start(bf16[2,128,128]{2,1,0:T(8,128)(2,1)S(1)} %fusion.5), channel_id=1, source_target_pairs={{0,4},{1,5},{2,6},{3,7},{4,0},{5,1},{6,2},{7,3},{8,12},{9,13},{10,... | collective-permute-start | bytes 196616 | tf_op jit(solution)/shard_map/ppermute | solution.py:36
  33.0 5.2 %collective-permute-start.7 = (f32[2,8192]{1,0:T(2,128)S(1)}, f32[2,8192]{1,0:T(2,128)S(1)}, u32[]{:S(2)}, u32[]{:S(2)}) collective-permute-start(f32[2,8192]{1,0:T(2,128)S(1)} %get-tuple-element.30), channel_id=1, source_target_pairs={{0,8},{8,16},{16,24},{24,0},{1,9},{9,17},{17,25},{25,1},{2,10},{10... | collective-permute-start | bytes 196616 | tf_op jit(solution)/shard_map/ppermute | solution.py:28
  40.0 5.4 %collective-permute-start.8 = (f32[2,8192]{1,0:T(2,128)S(1)}, f32[2,8192]{1,0:T(2,128)S(1)}, u32[]{:S(2)}, u32[]{:S(2)}) collective-permute-start(f32[2,8192]{1,0:T(2,128)S(1)} %get-tuple-element.31), channel_id=1, source_target_pairs={{0,8},{8,16},{16,24},{24,0},{1,9},{9,17},{17,25},{25,1},{2,10},{10... | collective-permute-start | bytes 196616 | tf_op jit(solution)/shard_map/ppermute | solution.py:28
  46.2 1.3 %collective-permute-start.9 = (bf16[2,128,128]{2,1,0:T(8,128)(2,1)S(1)}, bf16[2,128,128]{2,1,0:T(8,128)(2,1)S(1)}, u32[]{:S(2)}, u32[]{:S(2)}) collective-permute-start(bf16[2,128,128]{2,1,0:T(8,128)(2,1)S(1)} %convert_element_type.84), channel_id=1, source_target_pairs={{0,1},{1,0},{2,3},{3,2},{4,5},{5,4},{6,7},{7,6},{8,9},{9,8},{10,11... | collective-permute-start | bytes 196616 | tf_op jit(solution)/shard_map/ppermute | solution.py:36
  47.5 4.3 %collective-permute-start.10 = (bf16[2,128,128]{2,1,0:T(8,128)(2,1)S(1)}, bf16[2,128,128]{2,1,0:T(8,128)(2,1)S(1)}, u32[]{:S(2)}, u32[]{:S(2)}) collective-permute-start(bf16[2,128,128]{2,1,0:T(8,128)(2,1)S(1)} %fusion.2), channel_id=1, source_target_pairs={{0,2},{1,3},{2,0},{3,1},{4,6},{5,7},{6,4},{7,5},{8,10},{9,11},{10,... | collective-permute-start | bytes 196616 | tf_op jit(solution)/shard_map/ppermute | solution.py:36
  51.9 5.3 %collective-permute-start.11 = (bf16[2,128,128]{2,1,0:T(8,128)(2,1)S(1)}, bf16[2,128,128]{2,1,0:T(8,128)(2,1)S(1)}, u32[]{:S(2)}, u32[]{:S(2)}) collective-permute-start(bf16[2,128,128]{2,1,0:T(8,128)(2,1)S(1)} %fusion.6), channel_id=1, source_target_pairs={{0,4},{1,5},{2,6},{3,7},{4,0},{5,1},{6,2},{7,3},{8,12},{9,13},{10,... | collective-permute-start | bytes 196616 | tf_op jit(solution)/shard_map/ppermute | solution.py:36
  52.3 5.2 %collective-permute-start.12 = (f32[2,8192]{1,0:T(2,128)S(1)}, f32[2,8192]{1,0:T(2,128)S(1)}, u32[]{:S(2)}, u32[]{:S(2)}) collective-permute-start(f32[2,8192]{1,0:T(2,128)S(1)} %get-tuple-element.34), channel_id=1, source_target_pairs={{0,8},{8,16},{16,24},{24,0},{1,9},{9,17},{17,25},{25,1},{2,10},{10... | collective-permute-start | bytes 196616 | tf_op jit(solution)/shard_map/ppermute | solution.py:28
  59.3 5.2 %collective-permute-start.13 = (f32[2,8192]{1,0:T(2,128)S(1)}, f32[2,8192]{1,0:T(2,128)S(1)}, u32[]{:S(2)}, u32[]{:S(2)}) collective-permute-start(f32[2,8192]{1,0:T(2,128)S(1)} %get-tuple-element.35), channel_id=1, source_target_pairs={{0,8},{8,16},{16,24},{24,0},{1,9},{9,17},{17,25},{25,1},{2,10},{10... | collective-permute-start | bytes 196616 | tf_op jit(solution)/shard_map/ppermute | solution.py:28
  65.3 1.3 %collective-permute-start.14 = (bf16[2,128,128]{2,1,0:T(8,128)(2,1)S(1)}, bf16[2,128,128]{2,1,0:T(8,128)(2,1)S(1)}, u32[]{:S(2)}, u32[]{:S(2)}) collective-permute-start(bf16[2,128,128]{2,1,0:T(8,128)(2,1)S(1)} %convert_element_type.90), channel_id=1, source_target_pairs={{0,1},{1,0},{2,3},{3,2},{4,5},{5,4},{6,7},{7,6},{8,9},{9,8},{10,11... | collective-permute-start | bytes 196616 | tf_op jit(solution)/shard_map/ppermute | solution.py:36
  66.6 4.3 %collective-permute-start.15 = (bf16[2,128,128]{2,1,0:T(8,128)(2,1)S(1)}, bf16[2,128,128]{2,1,0:T(8,128)(2,1)S(1)}, u32[]{:S(2)}, u32[]{:S(2)}) collective-permute-start(bf16[2,128,128]{2,1,0:T(8,128)(2,1)S(1)} %fusion.3), channel_id=1, source_target_pairs={{0,2},{1,3},{2,0},{3,1},{4,6},{5,7},{6,4},{7,5},{8,10},{9,11},{10,... | collective-permute-start | bytes 196616 | tf_op jit(solution)/shard_map/ppermute | solution.py:36
  71.0 5.5 %collective-permute-start.16 = (bf16[2,128,128]{2,1,0:T(8,128)(2,1)S(1)}, bf16[2,128,128]{2,1,0:T(8,128)(2,1)S(1)}, u32[]{:S(2)}, u32[]{:S(2)}) collective-permute-start(bf16[2,128,128]{2,1,0:T(8,128)(2,1)S(1)} %fusion.7), channel_id=1, source_target_pairs={{0,4},{1,5},{2,6},{3,7},{4,0},{5,1},{6,2},{7,3},{8,12},{9,13},{10,... | collective-permute-start | bytes 196616 | tf_op jit(solution)/shard_map/ppermute | solution.py:36
  73.6 0.7 copy-start.2
  76.1 7.2 %collective-permute-start.20 = (f32[2,8192]{1,0:T(2,128)S(1)}, f32[2,8192]{1,0:T(2,128)S(1)}, u32[]{:S(2)}, u32[]{:S(2)}) collective-permute-start(f32[2,8192]{1,0:T(2,128)S(1)} %get-tuple-element.43), channel_id=1, source_target_pairs={{0,8},{8,16},{16,24},{24,0},{1,9},{9,17},{17,25},{25,1},{2,10},{10... | collective-permute-start | bytes 196616 | tf_op jit(solution)/shard_map/ppermute | solution.py:28
  79.0 6.7 %collective-permute-start.17 = (f32[32,4,128]{2,1,0:T(4,128)S(1)}, f32[32,4,128]{2,1,0:T(4,128)S(1)}, u32[]{:S(2)}, u32[]{:S(2)}) collective-permute-start(f32[32,4,128]{2,1,0:T(4,128)S(1)} %get-tuple-element.40), channel_id=1, source_target_pairs={{0,8},{8,0},{16,24},{24,16},{1,9},{9,1},{17,25},{25,17},{2,10},{10... | collective-permute-start | bytes 196616 | tf_op jit(solution)/shard_map/ppermute | solution.py:313
  81.7 4.3 %collective-permute-start.18 = (f32[32,4,128]{2,1,0:T(4,128)S(1)}, f32[32,4,128]{2,1,0:T(4,128)S(1)}, u32[]{:S(2)}, u32[]{:S(2)}) collective-permute-start(f32[32,4,128]{2,1,0:T(4,128)S(1)} %get-tuple-element.41), channel_id=1, source_target_pairs={{0,16},{8,24},{16,0},{24,8},{1,17},{9,25},{17,1},{25,9},{2,18},{10... | collective-permute-start | bytes 196616 | tf_op jit(solution)/shard_map/ppermute | solution.py:313
  82.2 5.2 %collective-permute-start.19 = (f32[32,4,128]{2,1,0:T(4,128)S(1)}, f32[32,4,128]{2,1,0:T(4,128)S(1)}, u32[]{:S(2)}, u32[]{:S(2)}) collective-permute-start(f32[32,4,128]{2,1,0:T(4,128)S(1)} %get-tuple-element.42), channel_id=1, source_target_pairs={{0,24},{8,16},{16,8},{24,0},{1,25},{9,17},{17,9},{25,1},{2,26},{10... | collective-permute-start | bytes 196616 | tf_op jit(solution)/shard_map/ppermute | solution.py:313

commit v4 on v3

--- a/solution.py
+++ b/solution.py
@@ -28,15 +28,16 @@
     return lax.ppermute(value, axis, pairs)
 
 
-def summed(value, axis):
-    count = lax.axis_size(axis)
-    step = 1
-    while step < count:
-        pairs = [(source, source ^ step) for source in range(count)]
-        other = lax.ppermute(value.astype(jnp.bfloat16), axis, pairs)
-        value = value + other.astype(jnp.float32)
-        step *= 2
-    return value
+def paired(value, axis, distance):
+    pairs = [(source, source ^ distance) for source in range(lax.axis_size(axis))]
+    return lax.ppermute(value, axis, pairs)
+
+
+def summed(kept, sent, axis):
+    value = kept + paired(sent, axis, 1).astype(jnp.float32)
+    sent = value.astype(jnp.bfloat16)
+    far = [paired(sent, axis, distance) for distance in range(2, lax.axis_size(axis), 2)]
+    return value + sum(part.astype(jnp.float32) for part in reversed(far))
 
 
 def cells(coordinate):
@@ -138,7 +139,18 @@
     return [pl.ds(start, width) for start in range(0, count, width)]
 
 
-def first_kernel(resident_hbm, opposing_hbm, resident_ref, opposing_ref, density_ref, landed):
+def share(resident, opposing, kept_ref, sent_ref):
+    even = lax.rem(lax.axis_index("dom"), 2) == 0
+    kept_ref[...] = jnp.where(even, resident, opposing)
+    sent_ref[...] = jnp.where(even, opposing, resident).astype(jnp.bfloat16)
+
+
+def chosen(which, own_ref, other_ref):
+    own = lax.rem(lax.axis_index("dom"), 2) == which
+    return jnp.where(own, own_ref[...], other_ref[...])
+
+
+def first_kernel(resident_hbm, opposing_hbm, resident_ref, opposing_ref, kept_ref, sent_ref, landed):
     held = (resident_ref, opposing_ref)
     copies = [
         pltpu.make_async_copy(source, place, landed.at[which])
@@ -146,12 +158,14 @@
     ]
     for copy in copies:
         copy.start()
-    for which, copy in enumerate(copies):
+    densities = []
+    for copy in copies:
         copy.wait()
-        beam = held[which]
-        density_ref[which] = sum(
-            deposit(line(beam, 0, tile), line(beam, 2, tile)) for tile in columns(beam.shape[1])
+    for beam in held:
+        densities.append(
+            sum(deposit(line(beam, 0, tile), line(beam, 2, tile)) for tile in columns(beam.shape[1]))
         )
+    share(*densities, kept_ref, sent_ref)
 
 
 def line(ref, row, tile):
@@ -164,8 +178,12 @@
     return [line(sources[row % 2], row // 2, tile) for row in range(4)]
 
 
-def opposing_kernel(scale, density_ref, smooth_ref, slope_ref, *refs):
-    table = table_of(density_ref[0], smooth_ref[...], slope_ref[...], scale)
+def table_kernel(scale, density_ref, smooth_ref, slope_ref, table_ref):
+    table_ref[...] = table_of(density_ref[...], smooth_ref[...], slope_ref[...], scale)
+
+
+def opposing_kernel(own_ref, other_ref, *refs):
+    table = chosen(0, own_ref, other_ref)
     *sources, place_ref, moment_ref = refs
     for tile in columns(place_ref.shape[1]):
         x, moment_x, y, moment_y = kick(*rows(sources, tile), table)
@@ -175,8 +193,8 @@
         moment_ref[1:2, tile] = moment_y[:1]
 
 
-def resident_kernel(scale, density_ref, smooth_ref, slope_ref, beam_ref, moved_ref, part_ref):
-    table = table_of(density_ref[1], smooth_ref[...], slope_ref[...], scale)
+def resident_kernel(own_ref, other_ref, beam_ref, moved_ref, part_ref):
+    table = chosen(1, own_ref, other_ref)
     total = 0.0
     for tile in columns(beam_ref.shape[1]):
         new = kick(*rows([beam_ref], tile), table)
@@ -186,16 +204,16 @@
     part_ref[...] = total
 
 
-def arrival_kernel(place_ref, resident_ref, density_ref):
-    density_ref[0] = resident_ref[...]
-    density_ref[1] = sum(
+def arrival_kernel(place_ref, resident_ref, kept_ref, sent_ref):
+    total = sum(
         deposit(line(place_ref, 0, tile), line(place_ref, 1, tile)) for tile in columns(place_ref.shape[1])
     )
-
-
-def last_kernel(scale, slots_ref, density_ref, smooth_ref, slope_ref, beam_ref, *refs):
+    share(resident_ref[...], total, kept_ref, sent_ref)
+
+
+def last_kernel(slots_ref, own_ref, other_ref, beam_ref, *refs):
     *packed, moved_ref, slots_out = refs
-    table = table_of(density_ref[1], smooth_ref[...], slope_ref[...], scale)
+    table = chosen(1, own_ref, other_ref)
     slots_out[...] = jnp.zeros_like(slots_out)
     for tile in columns(beam_ref.shape[1]):
         new = kick(*rows([beam_ref], tile), table)
@@ -208,18 +226,19 @@
         ref[...] = slots_out[distance * capacity : (distance + 1) * capacity]
 
 
-def final_kernel(scale, density_ref, smooth_ref, slope_ref, place_ref, moment_ref, out_ref):
-    table = table_of(density_ref[0], smooth_ref[...], slope_ref[...], scale)
+def final_kernel(own_ref, other_ref, place_ref, moment_ref, out_ref):
+    table = chosen(0, own_ref, other_ref)
     for tile in columns(place_ref.shape[1]):
         new = kick(*rows([place_ref, moment_ref], tile), table)
         for row in range(4):
             out_ref[row : row + 1, tile] = new[row][:1]
 
 
-def gather_kernel(me_ref, *refs):
+def gather_kernel(*refs):
     *parts, out_hbm, landed = refs
+    me = lax.axis_index("station")
     copies = [
-        pltpu.make_async_copy(part, out_hbm.at[me_ref[0] ^ distance], landed.at[distance])
+        pltpu.make_async_copy(part, out_hbm.at[me ^ distance], landed.at[distance])
         for distance, part in enumerate(parts)
     ]
     for copy in copies:
@@ -241,12 +260,13 @@
     return jax.ShapeDtypeStruct(shape, dtype)
 
 
-def slots_kernel(capacity, me_ref, routes_ref, slots_ref, taken_ref):
+def slots_kernel(capacity, routes_ref, slots_ref, taken_ref):
+    me = lax.axis_index("station")
     for station in range(taken_ref.shape[0]):
         taken_ref[station] = 0
 
     def place(block, carry):
-        distance = routes_ref[block] ^ me_ref[0]
+        distance = routes_ref[block] ^ me
         taken = taken_ref[distance]
         slots_ref[block] = distance * capacity + jnp.minimum(taken, capacity - 1)
         taken_ref[distance] = taken + 1
@@ -265,64 +285,66 @@
     capacity = max(2, 2 * block_count // stations)
     scale = STRENGTH * GRID * GRID / (count * groups)
     half, whole = array(2, count), array(4, count)
-    density, densities = array(GRID, GRID), array(2, GRID, GRID)
-    me = jnp.full((1,), lax.axis_index("station"), jnp.int32)
+    density = array(GRID, GRID)
+    shares = (density, array(GRID, GRID, dtype=jnp.bfloat16))
+    table = array(2 * GRID, GRID, dtype=jnp.bfloat16)
     vmem, smem = (pl.BlockSpec(memory_space=space) for space in (pltpu.VMEM, pltpu.SMEM))
-    place = local(
-        functools.partial(slots_kernel, capacity),
-        array(block_count, dtype=jnp.int32),
-        in_specs=[smem] * 2,
-        out_specs=smem,
-        scratch_shapes=[pltpu.SMEM((stations,), jnp.int32)],
-    )(me, destination[0, :, 0])
-
-    resident, *opposing, total = local(
+    resident, *opposing, kept, sent = local(
         first_kernel,
-        (whole, whole, densities),
+        (whole, whole, *shares),
         in_specs=[pl.BlockSpec(memory_space=pltpu.HBM)] * 2,
-        out_specs=(vmem,) * 3,
+        out_specs=(vmem,) * 4,
         scratch_shapes=[pltpu.SemaphoreType.DMA((2,))],
     )(*(pltpu.with_memory_space_constraint(value, pltpu.HBM) for value in (resident, opposing[0])))
     wide = array(GRID, 3 * GRID, dtype=jnp.bfloat16)
     smooth, slope = local(greens_kernel, (wide, wide))(green_smooth, green_slope)
-    total = summed(total, "dom")
+
+    def both_tables(kept, sent):
+        total = summed(kept, sent, "dom")
+        own = local(functools.partial(table_kernel, scale), table)(total, smooth, slope)
+        return own, paired(own, "dom", 1)
+
+    place = local(
+        functools.partial(slots_kernel, capacity),
+        array(block_count, dtype=jnp.int32),
+        in_specs=[smem],
+        out_specs=smem,
+        scratch_shapes=[pltpu.SMEM((stations,), jnp.int32)],
+    )(destination[0, :, 0])
+    pair = both_tables(kept, sent)
     for _ in range(FRONTS - 1):
-        positions, moments = local(functools.partial(opposing_kernel, scale), (half, half))(
-            total, smooth, slope, *opposing
-        )
+        positions, moments = local(opposing_kernel, (half, half))(*pair, *opposing)
         positions = shifted(positions, "station", 1)
         moments = shifted(moments, "station", 1)
         opposing = (positions, moments)
-        resident, part = local(
-            functools.partial(resident_kernel, scale), (whole, density)
-        )(total, smooth, slope, resident)
-        total = local(arrival_kernel, densities)(positions, part)
-        total = summed(total, "dom")
+        resident, part = local(resident_kernel, (whole, density))(*pair, resident)
+        kept, sent = local(arrival_kernel, shares)(positions, part)
+        pair = both_tables(kept, sent)
     blocks = array(capacity, 4, BLOCK)
     parts = local(
-        functools.partial(last_kernel, scale),
+        last_kernel,
         (blocks,) * stations,
-        in_specs=[smem] + [vmem] * 4,
+        in_specs=[smem] + [vmem] * 3,
         out_specs=(vmem,) * stations,
         scratch_shapes=[
             pltpu.VMEM((4, count), jnp.float32),
             pltpu.VMEM((stations * capacity, 4, BLOCK), jnp.float32),
         ],
-    )(place, total, smooth, slope, resident)
+    )(place, *pair, resident)
     parts = [
         lax.ppermute(part, "station", [(source, source ^ distance) for source in range(stations)])
         if distance
         else part
         for distance, part in enumerate(parts)
     ]
-    opposing = local(functools.partial(final_kernel, scale), whole)(total, smooth, slope, *opposing)
+    opposing = local(final_kernel, whole)(*pair, *opposing)
     arrived = local(
         gather_kernel,
         array(stations, capacity, 4, BLOCK),
-        in_specs=[smem] + [vmem] * stations,
+        in_specs=[vmem] * stations,
         out_specs=pl.BlockSpec(memory_space=pltpu.HBM),
         scratch_shapes=[pltpu.SemaphoreType.DMA((stations,))],
-    )(me, *parts)
+    )(*parts)
     return (arrived[None, None], opposing[None, None])
 
 

time: 88.4 us -> 82.8 us (0.937)
  waiting for transfers between devices: 32.7 us -> 29.8 us
  Pallas kernels: 26.9 us -> 24.1 us
    ppermute x12 -> x20, waiting for transfers between devices: 22.4 us -> 15.8 us  [paired(): return lax.ppermute(value, axis, pairs)]
    ppermute x6, waiting for transfers between devices: 8.78 us -> 11.9 us  [shifted(): return lax.ppermute(value, axis, pairs)]
    pallas_call x13 -> x17, Pallas kernels: 24.5 us -> 21.7 us  [the longest x3 6.44 us: shards(): resident, part = local(resident_kernel, (whole, density))(*pair, resident)]
    ppermute x12 -> x20, starting transfers between devices: 18.7 us -> 20 us  [paired(): return lax.ppermute(value, axis, pairs)]
    ppermute x6, starting transfers between devices: 3.66 us -> 2.33 us  [shifted(): return lax.ppermute(value, axis, pairs)]
  transfers between devices with their start and end apart: 21 -> 29, of which waited for: 18 -> 23; matrix products, arithmetic and copies ran while one was open for 0% -> 0% of each run, Pallas kernels for 17% -> 17%
where the time goes in v4:
time: 82.8 us; the launch traced here: 82.6 us
  waiting for transfers between devices  29.8 us (36%)
  starting transfers between devices  26.9 us (32%)
  Pallas kernels  24.1 us (29%)
  between operations  1.06 us (1%)
    ppermute x20, starting transfers between devices, paired(): return lax.ppermute(value, axis, pairs)  20 us
    ppermute x20, waiting for transfers between devices, paired(): return lax.ppermute(value, axis, pairs)  15.8 us
    ppermute x6, waiting for transfers between devices, shifted(): return lax.ppermute(value, axis, pairs)  11.9 us
    pallas_call x3, Pallas kernels, shards(): resident, part = local(resident_kernel, (whole, density))(*pair, resident)  6.44 us
    ppermute x3, starting transfers between devices, shards(): lax.ppermute(part, 'station', [(source, source ^ distance) for source in...  4.57 us
    pallas_call x3, Pallas kernels, shards(): positions, moments = local(opposing_kernel, (half, half))(*pair, *opposing)  4.12 us
    ppermute x6, starting transfers between devices, shifted(): return lax.ppermute(value, axis, pairs)  2.33 us
    pallas_call x1, Pallas kernels, shards(): local(first_kernel, (whole, whole, *shares), in_specs=[pl.BlockSpec(memor...  2.27 us
  transfers between devices with their start and end apart: 29, of which 23 were waited for; matrix products, arithmetic and copies ran while one was open for 0% of the time, Pallas kernels for 17%

profile of v4, /device:TPU:0, one launch (start us, length us, event | category | flops | bytes accessed | tf_op | source)
XLA Modules:
  0.0 82.6 jit_solution(11388819237911730814)
XLA Ops:
  0.6 2.3 %shard_map.69 = (f32[4,8192]{1,0:T(4,128)S(1)}, f32[4,8192]{1,0:T(4,128)S(1)}, f32[128,128]{1,0:T(8,128)S(1)}, bf16[128,128]{1,0:T(8,128)(2,1)S(1)}) custom-call(f32[4,8192]{1,0:T(4,128)} %bitcast.8, f32[4,8192]{1,0:T(4,128)} %bitcast.9), custom_call_target="tpu_custom_call" | custom-call | tf_op jit(solution)/shard_map/pallas_call | solution.py:292
  3.5 0.9 %collective-permute-done = bf16[128,128]{1,0:T(8,128)(2,1)S(1)} collective-permute-done((bf16[128,128]{1,0:T(8,128)(2,1)S(1)}, bf16[128,128]{1,0:T(8,128)(2,1)S(1)}, u32[]{:S(2)}, u32[]{:S(2)}) %collective-permute-start) | collective-permute-done | bytes 32800 | tf_op jit(solution)/shard_map/ppermute | solution.py:33
  4.3 5.0 %collective-permute-start.1 = (bf16[128,128]{1,0:T(8,128)(2,1)S(1)}, bf16[128,128]{1,0:T(8,128)(2,1)S(1)}, u32[]{:S(2)}, u32[]{:S(2)}) collective-permute-start(bf16[128,128]{1,0:T(8,128)(2,1)S(1)} %fusion), channel_id=1, source_target_pairs={{0,6},{1,7},{2,4},{3,5},{4,2},{5,3},{6,0},{7,1},{8,14},{9,15},{10,... | collective-permute-start | bytes 98312 | tf_op jit(solution)/shard_map/ppermute | solution.py:33
  9.3 0.6 collective-permute-start.3
  10.0 0.7 shard_map.70
  10.7 0.6 collective-permute-done.1
  11.2 2.9 %collective-permute-done.2 = bf16[128,128]{1,0:T(8,128)(2,1)S(1)} collective-permute-done((bf16[128,128]{1,0:T(8,128)(2,1)S(1)}, bf16[128,128]{1,0:T(8,128)(2,1)S(1)}, u32[]{:S(2)}, u32[]{:S(2)}) %collective-permute-start.2) | collective-permute-done | bytes 32800 | tf_op jit(solution)/shard_map/ppermute | solution.py:33
  14.7 1.2 %collective-permute-done.4.other_ref = bf16[256,128]{1,0:T(8,128)(2,1)S(1)} collective-permute-done((bf16[256,128]{1,0:T(8,128)(2,1)S(1)}, bf16[256,128]{1,0:T(8,128)(2,1)S(1)}, u32[]{:S(2)}, u32[]{:S(2)}) %collective-permute-start.4) | collective-permute-done | bytes 65568 | tf_op jit(solution)/shard_map/ppermute | solution.py:33
  16.0 1.4 %shard_map.72 = (f32[2,8192]{1,0:T(2,128)S(1)}, f32[2,8192]{1,0:T(2,128)S(1)}) custom-call(bf16[256,128]{1,0:T(8,128)(2,1)S(1)} %shard_map.71.own_ref, bf16[256,128]{1,0:T(8,128)(2,1)S(1)} %collective-permute-done.4.other_ref, f32[4,8192]{1,0:T(4,128)S(1)} %get-tuple-element.34.refs_0_), custom_call_target="tpu_custom_call" | custom-call | tf_op jit(solution)/shard_map/pallas_call | solution.py:316
  17.3 1.6 %collective-permute-start.5 = (f32[2,8192]{1,0:T(2,128)S(1)}, f32[2,8192]{1,0:T(2,128)S(1)}, u32[]{:S(2)}, u32[]{:S(2)}) collective-permute-start(f32[2,8192]{1,0:T(2,128)S(1)} %get-tuple-element.35), channel_id=1, source_target_pairs={{0,8},{8,16},{16,24},{24,0},{1,9},{9,17},{17,25},{25,1},{2,10},{10... | collective-permute-start | bytes 196616 | tf_op jit(solution)/shard_map/ppermute | solution.py:28
  18.9 2.1 %shard_map.73 = (f32[4,8192]{1,0:T(4,128)S(1)}, f32[128,128]{1,0:T(8,128)S(1)}) custom-call(bf16[256,128]{1,0:T(8,128)(2,1)S(1)} %shard_map.71.own_ref, bf16[256,128]{1,0:T(8,128)(2,1)S(1)} %collective-permute-done.4.other_ref, f32[4,8192]{1,0:T(4,128)S(1)} %get-tuple-element.36.beam_ref), custom_call_target="tpu_custom_call" | custom-call | tf_op jit(solution)/shard_map/pallas_call | solution.py:320
  21.1 1.5 %collective-permute-done.5.place_ref.refs_0_ = f32[2,8192]{1,0:T(2,128)S(1)} collective-permute-done((f32[2,8192]{1,0:T(2,128)S(1)}, f32[2,8192]{1,0:T(2,128)S(1)}, u32[]{:S(2)}, u32[]{:S(2)}) %collective-permute-start.5) | collective-permute-done | bytes 65568 | tf_op jit(solution)/shard_map/ppermute | solution.py:28
  22.6 0.7 shard_map.74
  23.4 1.2 %collective-permute-done.6 = bf16[128,128]{1,0:T(8,128)(2,1)S(1)} collective-permute-done((bf16[128,128]{1,0:T(8,128)(2,1)S(1)}, bf16[128,128]{1,0:T(8,128)(2,1)S(1)}, u32[]{:S(2)}, u32[]{:S(2)}) %collective-permute-start.6) | collective-permute-done | bytes 32800 | tf_op jit(solution)/shard_map/ppermute | solution.py:33
  24.6 1.5 %collective-permute-start.7 = (bf16[128,128]{1,0:T(8,128)(2,1)S(1)}, bf16[128,128]{1,0:T(8,128)(2,1)S(1)}, u32[]{:S(2)}, u32[]{:S(2)}) collective-permute-start(bf16[128,128]{1,0:T(8,128)(2,1)S(1)} %fusion.1), channel_id=1, source_target_pairs={{0,6},{1,7},{2,4},{3,5},{4,2},{5,3},{6,0},{7,1},{8,14},{9,15},{10,... | collective-permute-start | bytes 98312 | tf_op jit(solution)/shard_map/ppermute | solution.py:33
  26.1 0.6 collective-permute-start.8
  26.8 2.3 %collective-permute-start.9 = (bf16[128,128]{1,0:T(8,128)(2,1)S(1)}, bf16[128,128]{1,0:T(8,128)(2,1)S(1)}, u32[]{:S(2)}, u32[]{:S(2)}) collective-permute-start(bf16[128,128]{1,0:T(8,128)(2,1)S(1)} %fusion.1), channel_id=1, source_target_pairs={{0,2},{1,3},{2,0},{3,1},{4,6},{5,7},{6,4},{7,5},{8,10},{9,11},{10,... | collective-permute-start | bytes 98312 | tf_op jit(solution)/shard_map/ppermute | solution.py:33
  29.0 0.6 collective-permute-start.11
  29.6 1.0 %collective-permute-done.7 = bf16[128,128]{1,0:T(8,128)(2,1)S(1)} collective-permute-done((bf16[128,128]{1,0:T(8,128)(2,1)S(1)}, bf16[128,128]{1,0:T(8,128)(2,1)S(1)}, u32[]{:S(2)}, u32[]{:S(2)}) %collective-permute-start.7) | collective-permute-done | bytes 32800 | tf_op jit(solution)/shard_map/ppermute | solution.py:33
  31.9 2.3 %collective-permute-done.11.refs_1_ = f32[2,8192]{1,0:T(2,128)S(1)} collective-permute-done((f32[2,8192]{1,0:T(2,128)S(1)}, f32[2,8192]{1,0:T(2,128)S(1)}, u32[]{:S(2)}, u32[]{:S(2)}) %collective-permute-start.11) | collective-permute-done | bytes 65568 | tf_op jit(solution)/shard_map/ppermute | solution.py:28
  34.2 1.4 %shard_map.76 = (f32[2,8192]{1,0:T(2,128)S(1)}, f32[2,8192]{1,0:T(2,128)S(1)}) custom-call(bf16[256,128]{1,0:T(8,128)(2,1)S(1)} %shard_map.75.own_ref, bf16[256,128]{1,0:T(8,128)(2,1)S(1)} %collective-permute-done.10.other_ref, f32[2,8192]{1,0:T(2,128)S(1)} %collective-permute-done.5.place_ref.refs_0_, f32[2,8192]{1,0:T(2,128)S(1)} %collective-permute-done.11.refs_1_), custom_call_target="tpu_custom_call" | custom-call | tf_op jit(solution)/shard_map/pallas_call | solution.py:316
  35.7 2.1 %shard_map.77 = (f32[4,8192]{1,0:T(4,128)S(1)}, f32[128,128]{1,0:T(8,128)S(1)}) custom-call(bf16[256,128]{1,0:T(8,128)(2,1)S(1)} %shard_map.75.own_ref, bf16[256,128]{1,0:T(8,128)(2,1)S(1)} %collective-permute-done.10.other_ref, f32[4,8192]{1,0:T(4,128)S(1)} %get-tuple-element.42.beam_ref), custom_call_target="tpu_custom_call" | custom-call | tf_op jit(solution)/shard_map/pallas_call | solution.py:320
  37.8 3.0 %collective-permute-done.12.place_ref.refs_0_ = f32[2,8192]{1,0:T(2,128)S(1)} collective-permute-done((f32[2,8192]{1,0:T(2,128)S(1)}, f32[2,8192]{1,0:T(2,128)S(1)}, u32[]{:S(2)}, u32[]{:S(2)}) %collective-permute-start.12) | collective-permute-done | bytes 65568 | tf_op jit(solution)/shard_map/ppermute | solution.py:28
  40.8 0.7 shard_map.78
  41.6 1.2 %collective-permute-done.13 = bf16[128,128]{1,0:T(8,128)(2,1)S(1)} collective-permute-done((bf16[128,128]{1,0:T(8,128)(2,1)S(1)}, bf16[128,128]{1,0:T(8,128)(2,1)S(1)}, u32[]{:S(2)}, u32[]{:S(2)}) %collective-permute-start.13) | collective-permute-done | bytes 32800 | tf_op jit(solution)/shard_map/ppermute | solution.py:33
  42.8 1.5 %collective-permute-start.14 = (bf16[128,128]{1,0:T(8,128)(2,1)S(1)}, bf16[128,128]{1,0:T(8,128)(2,1)S(1)}, u32[]{:S(2)}, u32[]{:S(2)}) collective-permute-start(bf16[128,128]{1,0:T(8,128)(2,1)S(1)} %fusion.2), channel_id=1, source_target_pairs={{0,6},{1,7},{2,4},{3,5},{4,2},{5,3},{6,0},{7,1},{8,14},{9,15},{10,... | collective-permute-start | bytes 98312 | tf_op jit(solution)/shard_map/ppermute | solution.py:33
  44.9 2.4 %collective-permute-start.16 = (bf16[128,128]{1,0:T(8,128)(2,1)S(1)}, bf16[128,128]{1,0:T(8,128)(2,1)S(1)}, u32[]{:S(2)}, u32[]{:S(2)}) collective-permute-start(bf16[128,128]{1,0:T(8,128)(2,1)S(1)} %fusion.2), channel_id=1, source_target_pairs={{0,2},{1,3},{2,0},{3,1},{4,6},{5,7},{6,4},{7,5},{8,10},{9,11},{10,... | collective-permute-start | bytes 98312 | tf_op jit(solution)/shard_map/ppermute | solution.py:33
  47.3 1.3 %collective-permute-done.14 = bf16[128,128]{1,0:T(8,128)(2,1)S(1)} collective-permute-done((bf16[128,128]{1,0:T(8,128)(2,1)S(1)}, bf16[128,128]{1,0:T(8,128)(2,1)S(1)}, u32[]{:S(2)}, u32[]{:S(2)}) %collective-permute-start.14) | collective-permute-done | bytes 32800 | tf_op jit(solution)/shard_map/ppermute | solution.py:33
  48.6 0.9 %collective-permute-done.15 = bf16[128,128]{1,0:T(8,128)(2,1)S(1)} collective-permute-done((bf16[128,128]{1,0:T(8,128)(2,1)S(1)}, bf16[128,128]{1,0:T(8,128)(2,1)S(1)}, u32[]{:S(2)}, u32[]{:S(2)}) %collective-permute-start.15) | collective-permute-done | bytes 32800 | tf_op jit(solution)/shard_map/ppermute | solution.py:33
  50.4 2.1 %collective-permute-done.18.refs_1_ = f32[2,8192]{1,0:T(2,128)S(1)} collective-permute-done((f32[2,8192]{1,0:T(2,128)S(1)}, f32[2,8192]{1,0:T(2,128)S(1)}, u32[]{:S(2)}, u32[]{:S(2)}) %collective-permute-start.18) | collective-permute-done | bytes 65568 | tf_op jit(solution)/shard_map/ppermute | solution.py:28
  52.5 1.4 %shard_map.80 = (f32[2,8192]{1,0:T(2,128)S(1)}, f32[2,8192]{1,0:T(2,128)S(1)}) custom-call(bf16[256,128]{1,0:T(8,128)(2,1)S(1)} %shard_map.79.own_ref, bf16[256,128]{1,0:T(8,128)(2,1)S(1)} %collective-permute-done.17.other_ref, f32[2,8192]{1,0:T(2,128)S(1)} %collective-permute-done.12.place_ref.refs_0_, f32[2,8192]{1,0:T(2,128)S(1)} %collective-permute-done.18.refs_1_), custom_call_target="tpu_custom_call" | custom-call | tf_op jit(solution)/shard_map/pallas_call | solution.py:316
  53.9 2.1 %shard_map.81 = (f32[4,8192]{1,0:T(4,128)S(1)}, f32[128,128]{1,0:T(8,128)S(1)}) custom-call(bf16[256,128]{1,0:T(8,128)(2,1)S(1)} %shard_map.79.own_ref, bf16[256,128]{1,0:T(8,128)(2,1)S(1)} %collective-permute-done.17.other_ref, f32[4,8192]{1,0:T(4,128)S(1)} %get-tuple-element.48.beam_ref), custom_call_target="tpu_custom_call" | custom-call | tf_op jit(solution)/shard_map/pallas_call | solution.py:320
  56.1 3.0 %collective-permute-done.19.place_ref = f32[2,8192]{1,0:T(2,128)S(1)} collective-permute-done((f32[2,8192]{1,0:T(2,128)S(1)}, f32[2,8192]{1,0:T(2,128)S(1)}, u32[]{:S(2)}, u32[]{:S(2)}) %collective-permute-start.19) | collective-permute-done | bytes 65568 | tf_op jit(solution)/shard_map/ppermute | solution.py:28
  59.1 0.7 shard_map.82
  59.9 1.2 %collective-permute-done.20 = bf16[128,128]{1,0:T(8,128)(2,1)S(1)} collective-permute-done((bf16[128,128]{1,0:T(8,128)(2,1)S(1)}, bf16[128,128]{1,0:T(8,128)(2,1)S(1)}, u32[]{:S(2)}, u32[]{:S(2)}) %collective-permute-start.20) | collective-permute-done | bytes 32800 | tf_op jit(solution)/shard_map/ppermute | solution.py:33
  61.1 1.6 %collective-permute-start.21 = (bf16[128,128]{1,0:T(8,128)(2,1)S(1)}, bf16[128,128]{1,0:T(8,128)(2,1)S(1)}, u32[]{:S(2)}, u32[]{:S(2)}) collective-permute-start(bf16[128,128]{1,0:T(8,128)(2,1)S(1)} %fusion.3), channel_id=1, source_target_pairs={{0,6},{1,7},{2,4},{3,5},{4,2},{5,3},{6,0},{7,1},{8,14},{9,15},{10,... | collective-permute-start | bytes 98312 | tf_op jit(solution)/shard_map/ppermute | solution.py:33
  63.2 2.4 %collective-permute-start.23 = (bf16[128,128]{1,0:T(8,128)(2,1)S(1)}, bf16[128,128]{1,0:T(8,128)(2,1)S(1)}, u32[]{:S(2)}, u32[]{:S(2)}) collective-permute-start(bf16[128,128]{1,0:T(8,128)(2,1)S(1)} %fusion.3), channel_id=1, source_target_pairs={{0,2},{1,3},{2,0},{3,1},{4,6},{5,7},{6,4},{7,5},{8,10},{9,11},{10,... | collective-permute-start | bytes 98312 | tf_op jit(solution)/shard_map/ppermute | solution.py:33
  65.5 1.3 %collective-permute-done.21 = bf16[128,128]{1,0:T(8,128)(2,1)S(1)} collective-permute-done((bf16[128,128]{1,0:T(8,128)(2,1)S(1)}, bf16[128,128]{1,0:T(8,128)(2,1)S(1)}, u32[]{:S(2)}, u32[]{:S(2)}) %collective-permute-start.21) | collective-permute-done | bytes 32800 | tf_op jit(solution)/shard_map/ppermute | solution.py:33
  66.9 0.9 %collective-permute-done.22 = bf16[128,128]{1,0:T(8,128)(2,1)S(1)} collective-permute-done((bf16[128,128]{1,0:T(8,128)(2,1)S(1)}, bf16[128,128]{1,0:T(8,128)(2,1)S(1)}, u32[]{:S(2)}, u32[]{:S(2)}) %collective-permute-start.22) | collective-permute-done | bytes 32800 | tf_op jit(solution)/shard_map/ppermute | solution.py:33
  68.6 0.6 copy-done.2
  69.2 1.7 %shard_map.68.slots_ref = s32[64]{0:T(128)S(1)} custom-call(s32[64]{0:T(128)S(1)} %bitcast.5), custom_call_target="tpu_custom_call" | custom-call | tf_op jit(solution)/shard_map/pallas_call | solution.py:307
  71.0 2.0 %shard_map.84 = (f32[32,4,128]{2,1,0:T(4,128)S(1)}, f32[32,4,128]{2,1,0:T(4,128)S(1)}, f32[32,4,128]{2,1,0:T(4,128)S(1)}, f32[32,4,128]{2,1,0:T(4,128)S(1)}) custom-call(s32[64]{0:T(128)S(1)} %shard_map.68.slots_ref, bf16[256,128]{1,0:T(8,128)(2,1)S(1)} %shard_map.83.own_ref, bf16[256,128]{1,0:T(8,128)(2,1)S(1)} %collective-permute-done.24.other_ref, ...), custom_call_target="tpu_custom_call" | custom-call | tf_op jit(solution)/shard_map/pallas_call | solution.py:324
  73.0 3.0 %collective-permute-start.25 = (f32[32,4,128]{2,1,0:T(4,128)S(1)}, f32[32,4,128]{2,1,0:T(4,128)S(1)}, u32[]{:S(2)}, u32[]{:S(2)}) collective-permute-start(f32[32,4,128]{2,1,0:T(4,128)S(1)} %get-tuple-element.54), channel_id=1, source_target_pairs={{0,8},{8,0},{16,24},{24,16},{1,9},{9,1},{17,25},{25,17},{2,10},{10... | collective-permute-start | bytes 196616 | tf_op jit(solution)/shard_map/ppermute | solution.py:335
  76.6 1.0 %collective-permute-start.27 = (f32[32,4,128]{2,1,0:T(4,128)S(1)}, f32[32,4,128]{2,1,0:T(4,128)S(1)}, u32[]{:S(2)}, u32[]{:S(2)}) collective-permute-start(f32[32,4,128]{2,1,0:T(4,128)S(1)} %get-tuple-element.56), channel_id=1, source_target_pairs={{0,24},{8,16},{16,8},{24,0},{1,25},{9,17},{17,9},{25,1},{2,26},{10... | collective-permute-start | bytes 196616 | tf_op jit(solution)/shard_map/ppermute | solution.py:335
  77.6 2.1 %shard_map.86 = f32[4,8192]{1,0:T(4,128)} custom-call(bf16[256,128]{1,0:T(8,128)(2,1)S(1)} %shard_map.83.own_ref, bf16[256,128]{1,0:T(8,128)(2,1)S(1)} %collective-permute-done.24.other_ref, f32[2,8192]{1,0:T(2,128)S(1)} %collective-permute-done.19.place_ref, f32[2,8192]{1,0:T(2,128)S(1)} %collective-permute-done.28.moment_ref), custom_call_target="tpu_custom_call" | custom-call | tf_op jit(solution)/shard_map/pallas_call | solution.py:340
  79.7 0.9 %collective-permute-done.26.refs_2_ = f32[32,4,128]{2,1,0:T(4,128)S(1)} collective-permute-done((f32[32,4,128]{2,1,0:T(4,128)S(1)}, f32[32,4,128]{2,1,0:T(4,128)S(1)}, u32[]{:S(2)}, u32[]{:S(2)}) %collective-permute-start.26) | collective-permute-done | bytes 65568 | tf_op jit(solution)/shard_map/ppermute | solution.py:335
  80.6 1.2 %collective-permute-done.27.refs_3_ = f32[32,4,128]{2,1,0:T(4,128)S(1)} collective-permute-done((f32[32,4,128]{2,1,0:T(4,128)S(1)}, f32[32,4,128]{2,1,0:T(4,128)S(1)}, u32[]{:S(2)}, u32[]{:S(2)}) %collective-permute-start.27) | collective-permute-done | bytes 65568 | tf_op jit(solution)/shard_map/ppermute | solution.py:335
  81.7 0.7 shard_map.85
  (43 shorter events, 5.9 us)
Async XLA Ops:
  2.9 1.4 %collective-permute-start = (bf16[128,128]{1,0:T(8,128)(2,1)S(1)}, bf16[128,128]{1,0:T(8,128)(2,1)S(1)}, u32[]{:S(2)}, u32[]{:S(2)}) collective-permute-start(bf16[128,128]{1,0:T(8,128)(2,1)S(1)} %get-tuple-element.31), channel_id=1, source_target_pairs={{0,1},{1,0},{2,3},{3,2},{4,5},{5,4},{6,7},{7,6},{8,9},{9,8},{10,11... | collective-permute-start | bytes 98312 | tf_op jit(solution)/shard_map/ppermute | solution.py:33
  4.3 5.7 %copy-start = (f32[128,128]{1,0:T(8,128)S(1)}, f32[128,128]{1,0:T(8,128)}, u32[]{:S(2)}) copy-start(f32[128,128]{1,0:T(8,128)} %smooth_ref.1) | copy-start | bytes 196612
  4.3 5.7 %copy-start.1 = (f32[128,128]{1,0:T(8,128)S(1)}, f32[128,128]{1,0:T(8,128)}, u32[]{:S(2)}) copy-start(f32[128,128]{1,0:T(8,128)} %slope_ref.1) | copy-start | bytes 196612
  4.3 6.9 %collective-permute-start.1 = (bf16[128,128]{1,0:T(8,128)(2,1)S(1)}, bf16[128,128]{1,0:T(8,128)(2,1)S(1)}, u32[]{:S(2)}, u32[]{:S(2)}) collective-permute-start(bf16[128,128]{1,0:T(8,128)(2,1)S(1)} %fusion), channel_id=1, source_target_pairs={{0,6},{1,7},{2,4},{3,5},{4,2},{5,3},{6,0},{7,1},{8,14},{9,15},{10,... | collective-permute-start | bytes 98312 | tf_op jit(solution)/shard_map/ppermute | solution.py:33
  9.3 4.8 %collective-permute-start.2 = (bf16[128,128]{1,0:T(8,128)(2,1)S(1)}, bf16[128,128]{1,0:T(8,128)(2,1)S(1)}, u32[]{:S(2)}, u32[]{:S(2)}) collective-permute-start(bf16[128,128]{1,0:T(8,128)(2,1)S(1)} %fusion), channel_id=1, source_target_pairs={{0,4},{1,5},{2,6},{3,7},{4,0},{5,1},{6,2},{7,3},{8,12},{9,13},{10,... | collective-permute-start | bytes 98312 | tf_op jit(solution)/shard_map/ppermute | solution.py:33
  9.3 4.8 %collective-permute-start.3 = (bf16[128,128]{1,0:T(8,128)(2,1)S(1)}, bf16[128,128]{1,0:T(8,128)(2,1)S(1)}, u32[]{:S(2)}, u32[]{:S(2)}) collective-permute-start(bf16[128,128]{1,0:T(8,128)(2,1)S(1)} %fusion), channel_id=1, source_target_pairs={{0,2},{1,3},{2,0},{3,1},{4,6},{5,7},{6,4},{7,5},{8,10},{9,11},{10,... | collective-permute-start | bytes 98312 | tf_op jit(solution)/shard_map/ppermute | solution.py:33
  14.7 1.3 %collective-permute-start.4 = (bf16[256,128]{1,0:T(8,128)(2,1)S(1)}, bf16[256,128]{1,0:T(8,128)(2,1)S(1)}, u32[]{:S(2)}, u32[]{:S(2)}) collective-permute-start(bf16[256,128]{1,0:T(8,128)(2,1)S(1)} %shard_map.71.own_ref), channel_id=1, source_target_pairs={{0,1},{1,0},{2,3},{3,2},{4,5},{5,4},{6,7},{7,6},{8,9},{9,8},{10,11... | collective-permute-start | bytes 196616 | tf_op jit(solution)/shard_map/ppermute | solution.py:33
  17.3 5.2 %collective-permute-start.5 = (f32[2,8192]{1,0:T(2,128)S(1)}, f32[2,8192]{1,0:T(2,128)S(1)}, u32[]{:S(2)}, u32[]{:S(2)}) collective-permute-start(f32[2,8192]{1,0:T(2,128)S(1)} %get-tuple-element.35), channel_id=1, source_target_pairs={{0,8},{8,16},{16,24},{24,0},{1,9},{9,17},{17,25},{25,1},{2,10},{10... | collective-permute-start | bytes 196616 | tf_op jit(solution)/shard_map/ppermute | solution.py:28
  23.3 1.3 %collective-permute-start.6 = (bf16[128,128]{1,0:T(8,128)(2,1)S(1)}, bf16[128,128]{1,0:T(8,128)(2,1)S(1)}, u32[]{:S(2)}, u32[]{:S(2)}) collective-permute-start(bf16[128,128]{1,0:T(8,128)(2,1)S(1)} %get-tuple-element.39), channel_id=1, source_target_pairs={{0,1},{1,0},{2,3},{3,2},{4,5},{5,4},{6,7},{7,6},{8,9},{9,8},{10,11... | collective-permute-start | bytes 98312 | tf_op jit(solution)/shard_map/ppermute | solution.py:33
  24.6 6.1 %collective-permute-start.7 = (bf16[128,128]{1,0:T(8,128)(2,1)S(1)}, bf16[128,128]{1,0:T(8,128)(2,1)S(1)}, u32[]{:S(2)}, u32[]{:S(2)}) collective-permute-start(bf16[128,128]{1,0:T(8,128)(2,1)S(1)} %fusion.1), channel_id=1, source_target_pairs={{0,6},{1,7},{2,4},{3,5},{4,2},{5,3},{6,0},{7,1},{8,14},{9,15},{10,... | collective-permute-start | bytes 98312 | tf_op jit(solution)/shard_map/ppermute | solution.py:33
  26.1 4.9 %collective-permute-start.8 = (bf16[128,128]{1,0:T(8,128)(2,1)S(1)}, bf16[128,128]{1,0:T(8,128)(2,1)S(1)}, u32[]{:S(2)}, u32[]{:S(2)}) collective-permute-start(bf16[128,128]{1,0:T(8,128)(2,1)S(1)} %fusion.1), channel_id=1, source_target_pairs={{0,4},{1,5},{2,6},{3,7},{4,0},{5,1},{6,2},{7,3},{8,12},{9,13},{10,... | collective-permute-start | bytes 98312 | tf_op jit(solution)/shard_map/ppermute | solution.py:33
  26.8 4.6 %collective-permute-start.9 = (bf16[128,128]{1,0:T(8,128)(2,1)S(1)}, bf16[128,128]{1,0:T(8,128)(2,1)S(1)}, u32[]{:S(2)}, u32[]{:S(2)}) collective-permute-start(bf16[128,128]{1,0:T(8,128)(2,1)S(1)} %fusion.1), channel_id=1, source_target_pairs={{0,2},{1,3},{2,0},{3,1},{4,6},{5,7},{6,4},{7,5},{8,10},{9,11},{10,... | collective-permute-start | bytes 98312 | tf_op jit(solution)/shard_map/ppermute | solution.py:33
  29.0 5.2 %collective-permute-start.11 = (f32[2,8192]{1,0:T(2,128)S(1)}, f32[2,8192]{1,0:T(2,128)S(1)}, u32[]{:S(2)}, u32[]{:S(2)}) collective-permute-start(f32[2,8192]{1,0:T(2,128)S(1)} %get-tuple-element.40), channel_id=1, source_target_pairs={{0,8},{8,16},{16,24},{24,0},{1,9},{9,17},{17,25},{25,1},{2,10},{10... | collective-permute-start | bytes 196616 | tf_op jit(solution)/shard_map/ppermute | solution.py:28
  31.8 2.4 %collective-permute-start.10 = (bf16[256,128]{1,0:T(8,128)(2,1)S(1)}, bf16[256,128]{1,0:T(8,128)(2,1)S(1)}, u32[]{:S(2)}, u32[]{:S(2)}) collective-permute-start(bf16[256,128]{1,0:T(8,128)(2,1)S(1)} %shard_map.75.own_ref), channel_id=1, source_target_pairs={{0,1},{1,0},{2,3},{3,2},{4,5},{5,4},{6,7},{7,6},{8,9},{9,8},{10,11... | collective-permute-start | bytes 196616 | tf_op jit(solution)/shard_map/ppermute | solution.py:33
  35.6 5.2 %collective-permute-start.12 = (f32[2,8192]{1,0:T(2,128)S(1)}, f32[2,8192]{1,0:T(2,128)S(1)}, u32[]{:S(2)}, u32[]{:S(2)}) collective-permute-start(f32[2,8192]{1,0:T(2,128)S(1)} %get-tuple-element.41), channel_id=1, source_target_pairs={{0,8},{8,16},{16,24},{24,0},{1,9},{9,17},{17,25},{25,1},{2,10},{10... | collective-permute-start | bytes 196616 | tf_op jit(solution)/shard_map/ppermute | solution.py:28
  41.5 1.3 %collective-permute-start.13 = (bf16[128,128]{1,0:T(8,128)(2,1)S(1)}, bf16[128,128]{1,0:T(8,128)(2,1)S(1)}, u32[]{:S(2)}, u32[]{:S(2)}) collective-permute-start(bf16[128,128]{1,0:T(8,128)(2,1)S(1)} %get-tuple-element.45), channel_id=1, source_target_pairs={{0,1},{1,0},{2,3},{3,2},{4,5},{5,4},{6,7},{7,6},{8,9},{9,8},{10,11... | collective-permute-start | bytes 98312 | tf_op jit(solution)/shard_map/ppermute | solution.py:33
  42.8 5.8 %collective-permute-start.14 = (bf16[128,128]{1,0:T(8,128)(2,1)S(1)}, bf16[128,128]{1,0:T(8,128)(2,1)S(1)}, u32[]{:S(2)}, u32[]{:S(2)}) collective-permute-start(bf16[128,128]{1,0:T(8,128)(2,1)S(1)} %fusion.2), channel_id=1, source_target_pairs={{0,6},{1,7},{2,4},{3,5},{4,2},{5,3},{6,0},{7,1},{8,14},{9,15},{10,... | collective-permute-start | bytes 98312 | tf_op jit(solution)/shard_map/ppermute | solution.py:33
  44.4 5.2 %collective-permute-start.15 = (bf16[128,128]{1,0:T(8,128)(2,1)S(1)}, bf16[128,128]{1,0:T(8,128)(2,1)S(1)}, u32[]{:S(2)}, u32[]{:S(2)}) collective-permute-start(bf16[128,128]{1,0:T(8,128)(2,1)S(1)} %fusion.2), channel_id=1, source_target_pairs={{0,4},{1,5},{2,6},{3,7},{4,0},{5,1},{6,2},{7,3},{8,12},{9,13},{10,... | collective-permute-start | bytes 98312 | tf_op jit(solution)/shard_map/ppermute | solution.py:33
  44.9 4.8 %collective-permute-start.16 = (bf16[128,128]{1,0:T(8,128)(2,1)S(1)}, bf16[128,128]{1,0:T(8,128)(2,1)S(1)}, u32[]{:S(2)}, u32[]{:S(2)}) collective-permute-start(bf16[128,128]{1,0:T(8,128)(2,1)S(1)} %fusion.2), channel_id=1, source_target_pairs={{0,2},{1,3},{2,0},{3,1},{4,6},{5,7},{6,4},{7,5},{8,10},{9,11},{10,... | collective-permute-start | bytes 98312 | tf_op jit(solution)/shard_map/ppermute | solution.py:33
  47.3 5.2 %collective-permute-start.18 = (f32[2,8192]{1,0:T(2,128)S(1)}, f32[2,8192]{1,0:T(2,128)S(1)}, u32[]{:S(2)}, u32[]{:S(2)}) collective-permute-start(f32[2,8192]{1,0:T(2,128)S(1)} %get-tuple-element.46), channel_id=1, source_target_pairs={{0,8},{8,16},{16,24},{24,0},{1,9},{9,17},{17,25},{25,1},{2,10},{10... | collective-permute-start | bytes 196616 | tf_op jit(solution)/shard_map/ppermute | solution.py:28
  50.3 2.2 %collective-permute-start.17 = (bf16[256,128]{1,0:T(8,128)(2,1)S(1)}, bf16[256,128]{1,0:T(8,128)(2,1)S(1)}, u32[]{:S(2)}, u32[]{:S(2)}) collective-permute-start(bf16[256,128]{1,0:T(8,128)(2,1)S(1)} %shard_map.79.own_ref), channel_id=1, source_target_pairs={{0,1},{1,0},{2,3},{3,2},{4,5},{5,4},{6,7},{7,6},{8,9},{9,8},{10,11... | collective-permute-start | bytes 196616 | tf_op jit(solution)/shard_map/ppermute | solution.py:33
  53.8 5.2 %collective-permute-start.19 = (f32[2,8192]{1,0:T(2,128)S(1)}, f32[2,8192]{1,0:T(2,128)S(1)}, u32[]{:S(2)}, u32[]{:S(2)}) collective-permute-start(f32[2,8192]{1,0:T(2,128)S(1)} %get-tuple-element.47), channel_id=1, source_target_pairs={{0,8},{8,16},{16,24},{24,0},{1,9},{9,17},{17,25},{25,1},{2,10},{10... | collective-permute-start | bytes 196616 | tf_op jit(solution)/shard_map/ppermute | solution.py:28
  59.8 1.3 %collective-permute-start.20 = (bf16[128,128]{1,0:T(8,128)(2,1)S(1)}, bf16[128,128]{1,0:T(8,128)(2,1)S(1)}, u32[]{:S(2)}, u32[]{:S(2)}) collective-permute-start(bf16[128,128]{1,0:T(8,128)(2,1)S(1)} %get-tuple-element.51), channel_id=1, source_target_pairs={{0,1},{1,0},{2,3},{3,2},{4,5},{5,4},{6,7},{7,6},{8,9},{9,8},{10,11... | collective-permute-start | bytes 98312 | tf_op jit(solution)/shard_map/ppermute | solution.py:33
  61.1 5.8 %collective-permute-start.21 = (bf16[128,128]{1,0:T(8,128)(2,1)S(1)}, bf16[128,128]{1,0:T(8,128)(2,1)S(1)}, u32[]{:S(2)}, u32[]{:S(2)}) collective-permute-start(bf16[128,128]{1,0:T(8,128)(2,1)S(1)} %fusion.3), channel_id=1, source_target_pairs={{0,6},{1,7},{2,4},{3,5},{4,2},{5,3},{6,0},{7,1},{8,14},{9,15},{10,... | collective-permute-start | bytes 98312 | tf_op jit(solution)/shard_map/ppermute | solution.py:33
  62.6 5.2 %collective-permute-start.22 = (bf16[128,128]{1,0:T(8,128)(2,1)S(1)}, bf16[128,128]{1,0:T(8,128)(2,1)S(1)}, u32[]{:S(2)}, u32[]{:S(2)}) collective-permute-start(bf16[128,128]{1,0:T(8,128)(2,1)S(1)} %fusion.3), channel_id=1, source_target_pairs={{0,4},{1,5},{2,6},{3,7},{4,0},{5,1},{6,2},{7,3},{8,12},{9,13},{10,... | collective-permute-start | bytes 98312 | tf_op jit(solution)/shard_map/ppermute | solution.py:33
  63.2 4.8 %collective-permute-start.23 = (bf16[128,128]{1,0:T(8,128)(2,1)S(1)}, bf16[128,128]{1,0:T(8,128)(2,1)S(1)}, u32[]{:S(2)}, u32[]{:S(2)}) collective-permute-start(bf16[128,128]{1,0:T(8,128)(2,1)S(1)} %fusion.3), channel_id=1, source_target_pairs={{0,2},{1,3},{2,0},{3,1},{4,6},{5,7},{6,4},{7,5},{8,10},{9,11},{10,... | collective-permute-start | bytes 98312 | tf_op jit(solution)/shard_map/ppermute | solution.py:33
  68.5 0.7 copy-start.2
  68.5 2.5 %collective-permute-start.24 = (bf16[256,128]{1,0:T(8,128)(2,1)S(1)}, bf16[256,128]{1,0:T(8,128)(2,1)S(1)}, u32[]{:S(2)}, u32[]{:S(2)}) collective-permute-start(bf16[256,128]{1,0:T(8,128)(2,1)S(1)} %shard_map.83.own_ref), channel_id=1, source_target_pairs={{0,1},{1,0},{2,3},{3,2},{4,5},{5,4},{6,7},{7,6},{8,9},{9,8},{10,11... | collective-permute-start | bytes 196616 | tf_op jit(solution)/shard_map/ppermute | solution.py:33
  70.9 6.7 %collective-permute-start.28 = (f32[2,8192]{1,0:T(2,128)S(1)}, f32[2,8192]{1,0:T(2,128)S(1)}, u32[]{:S(2)}, u32[]{:S(2)}) collective-permute-start(f32[2,8192]{1,0:T(2,128)S(1)} %get-tuple-element.57), channel_id=1, source_target_pairs={{0,8},{8,16},{16,24},{24,0},{1,9},{9,17},{17,25},{25,1},{2,10},{10... | collective-permute-start | bytes 196616 | tf_op jit(solution)/shard_map/ppermute | solution.py:28
  73.0 6.6 %collective-permute-start.25 = (f32[32,4,128]{2,1,0:T(4,128)S(1)}, f32[32,4,128]{2,1,0:T(4,128)S(1)}, u32[]{:S(2)}, u32[]{:S(2)}) collective-permute-start(f32[32,4,128]{2,1,0:T(4,128)S(1)} %get-tuple-element.54), channel_id=1, source_target_pairs={{0,8},{8,0},{16,24},{24,16},{1,9},{9,1},{17,25},{25,17},{2,10},{10... | collective-permute-start | bytes 196616 | tf_op jit(solution)/shard_map/ppermute | solution.py:335
  76.1 4.5 %collective-permute-start.26 = (f32[32,4,128]{2,1,0:T(4,128)S(1)}, f32[32,4,128]{2,1,0:T(4,128)S(1)}, u32[]{:S(2)}, u32[]{:S(2)}) collective-permute-start(f32[32,4,128]{2,1,0:T(4,128)S(1)} %get-tuple-element.55), channel_id=1, source_target_pairs={{0,16},{8,24},{16,0},{24,8},{1,17},{9,25},{17,1},{25,9},{2,18},{10... | collective-permute-start | bytes 196616 | tf_op jit(solution)/shard_map/ppermute | solution.py:335
  76.6 5.2 %collective-permute-start.27 = (f32[32,4,128]{2,1,0:T(4,128)S(1)}, f32[32,4,128]{2,1,0:T(4,128)S(1)}, u32[]{:S(2)}, u32[]{:S(2)}) collective-permute-start(f32[32,4,128]{2,1,0:T(4,128)S(1)} %get-tuple-element.56), channel_id=1, source_target_pairs={{0,24},{8,16},{16,8},{24,0},{1,25},{9,17},{17,9},{25,1},{2,26},{10... | collective-permute-start | bytes 196616 | tf_op jit(solution)/shard_map/ppermute | solution.py:335

commit v5 on v4

--- a/solution.py
+++ b/solution.py
@@ -139,10 +139,9 @@
     return [pl.ds(start, width) for start in range(0, count, width)]
 
 
-def share(resident, opposing, kept_ref, sent_ref):
+def share(resident, opposing):
     even = lax.rem(lax.axis_index("dom"), 2) == 0
-    kept_ref[...] = jnp.where(even, resident, opposing)
-    sent_ref[...] = jnp.where(even, opposing, resident).astype(jnp.bfloat16)
+    return jnp.where(even, resident, opposing), jnp.where(even, opposing, resident).astype(jnp.bfloat16)
 
 
 def chosen(which, own_ref, other_ref):
@@ -165,50 +164,30 @@
         densities.append(
             sum(deposit(line(beam, 0, tile), line(beam, 2, tile)) for tile in columns(beam.shape[1]))
         )
-    share(*densities, kept_ref, sent_ref)
+    kept_ref[...], sent_ref[...] = share(*densities)
 
 
 def line(ref, row, tile):
     return jnp.broadcast_to(ref[row : row + 1, tile], (LINES, tile.size))
 
 
-def rows(sources, tile):
-    if len(sources) == 1:
-        return [line(sources[0], row, tile) for row in range(4)]
-    return [line(sources[row % 2], row // 2, tile) for row in range(4)]
+def rows(ref, tile):
+    return [line(ref, row, tile) for row in range(4)]
 
 
 def table_kernel(scale, density_ref, smooth_ref, slope_ref, table_ref):
     table_ref[...] = table_of(density_ref[...], smooth_ref[...], slope_ref[...], scale)
 
 
-def opposing_kernel(own_ref, other_ref, *refs):
-    table = chosen(0, own_ref, other_ref)
-    *sources, place_ref, moment_ref = refs
-    for tile in columns(place_ref.shape[1]):
-        x, moment_x, y, moment_y = kick(*rows(sources, tile), table)
-        place_ref[0:1, tile] = x[:1]
-        place_ref[1:2, tile] = y[:1]
-        moment_ref[0:1, tile] = moment_x[:1]
-        moment_ref[1:2, tile] = moment_y[:1]
-
-
-def resident_kernel(own_ref, other_ref, beam_ref, moved_ref, part_ref):
-    table = chosen(1, own_ref, other_ref)
+def beam_kernel(which, own_ref, other_ref, beam_ref, moved_ref, density_ref):
+    table = chosen(which, own_ref, other_ref)
     total = 0.0
     for tile in columns(beam_ref.shape[1]):
-        new = kick(*rows([beam_ref], tile), table)
+        new = kick(*rows(beam_ref, tile), table)
         for row in range(4):
             moved_ref[row : row + 1, tile] = new[row][:1]
         total = total + deposit(new[0], new[2])
-    part_ref[...] = total
-
-
-def arrival_kernel(place_ref, resident_ref, kept_ref, sent_ref):
-    total = sum(
-        deposit(line(place_ref, 0, tile), line(place_ref, 1, tile)) for tile in columns(place_ref.shape[1])
-    )
-    share(resident_ref[...], total, kept_ref, sent_ref)
+    density_ref[...] = total.astype(density_ref.dtype)
 
 
 def last_kernel(slots_ref, own_ref, other_ref, beam_ref, *refs):
@@ -216,7 +195,7 @@
     table = chosen(1, own_ref, other_ref)
     slots_out[...] = jnp.zeros_like(slots_out)
     for tile in columns(beam_ref.shape[1]):
-        new = kick(*rows([beam_ref], tile), table)
+        new = kick(*rows(beam_ref, tile), table)
         for row in range(4):
             moved_ref[row : row + 1, tile] = new[row][:1]
     for block in range(beam_ref.shape[1] // BLOCK):
@@ -226,10 +205,10 @@
         ref[...] = slots_out[distance * capacity : (distance + 1) * capacity]
 
 
-def final_kernel(own_ref, other_ref, place_ref, moment_ref, out_ref):
+def final_kernel(own_ref, other_ref, beam_ref, out_ref):
     table = chosen(0, own_ref, other_ref)
-    for tile in columns(place_ref.shape[1]):
-        new = kick(*rows([place_ref, moment_ref], tile), table)
+    for tile in columns(beam_ref.shape[1]):
+        new = kick(*rows(beam_ref, tile), table)
         for row in range(4):
             out_ref[row : row + 1, tile] = new[row][:1]
 
@@ -277,25 +256,24 @@
 
 def shards(beam_first, beam_second, green_smooth, green_slope, destination):
     resident = beam_first[0, 0]
-    opposing = (beam_second[0, 0],)
+    opposing = beam_second[0, 0]
     groups = lax.axis_size("dom")
     stations = lax.axis_size("station")
     count = resident.shape[1]
     block_count = count // BLOCK
     capacity = max(2, 2 * block_count // stations)
     scale = STRENGTH * GRID * GRID / (count * groups)
-    half, whole = array(2, count), array(4, count)
-    density = array(GRID, GRID)
-    shares = (density, array(GRID, GRID, dtype=jnp.bfloat16))
+    whole = array(4, count)
+    density, rounded = array(GRID, GRID), array(GRID, GRID, dtype=jnp.bfloat16)
     table = array(2 * GRID, GRID, dtype=jnp.bfloat16)
     vmem, smem = (pl.BlockSpec(memory_space=space) for space in (pltpu.VMEM, pltpu.SMEM))
-    resident, *opposing, kept, sent = local(
+    resident, opposing, kept, sent = local(
         first_kernel,
-        (whole, whole, *shares),
+        (whole, whole, density, rounded),
         in_specs=[pl.BlockSpec(memory_space=pltpu.HBM)] * 2,
         out_specs=(vmem,) * 4,
         scratch_shapes=[pltpu.SemaphoreType.DMA((2,))],
-    )(*(pltpu.with_memory_space_constraint(value, pltpu.HBM) for value in (resident, opposing[0])))
+    )(*(pltpu.with_memory_space_constraint(value, pltpu.HBM) for value in (resident, opposing)))
     wide = array(GRID, 3 * GRID, dtype=jnp.bfloat16)
     smooth, slope = local(greens_kernel, (wide, wide))(green_smooth, green_slope)
 
@@ -313,13 +291,13 @@
     )(destination[0, :, 0])
     pair = both_tables(kept, sent)
     for _ in range(FRONTS - 1):
-        positions, moments = local(opposing_kernel, (half, half))(*pair, *opposing)
-        positions = shifted(positions, "station", 1)
-        moments = shifted(moments, "station", 1)
-        opposing = (positions, moments)
-        resident, part = local(resident_kernel, (whole, density))(*pair, resident)
-        kept, sent = local(arrival_kernel, shares)(positions, part)
-        pair = both_tables(kept, sent)
+        opposing, part = local(functools.partial(beam_kernel, 0), (whole, rounded))(*pair, opposing)
+        part = shifted(part, "station", 1)
+        opposing = shifted(opposing, "station", 1)
+        resident, total = local(functools.partial(beam_kernel, 1), (whole, density))(
+            *pair, resident
+        )
+        pair = both_tables(*share(total, part.astype(jnp.float32)))
     blocks = array(capacity, 4, BLOCK)
     parts = local(
         last_kernel,
@@ -337,7 +315,7 @@
         else part
         for distance, part in enumerate(parts)
     ]
-    opposing = local(final_kernel, whole)(*pair, *opposing)
+    opposing = local(final_kernel, whole)(*pair, opposing)
     arrived = local(
         gather_kernel,
         array(stations, capacity, 4, BLOCK),

time: 82.8 us -> 83 us (level)
    ppermute x6, starting transfers between devices: 2.33 us -> 3.18 us  [shifted(): return lax.ppermute(value, axis, pairs)]
    pallas_call x11 -> x8, Pallas kernels: 17.1 us -> 17.2 us  [the longest x3 6.45 us: shards(): local(functools.partial(beam_kernel, 0), (whole, rounded))(*pair, opposing)]
where the time goes in v5:
time: 83 us; the launch traced here: 82.8 us
  waiting for transfers between devices  29.8 us (36%)
  starting transfers between devices  27.2 us (33%)
  Pallas kernels  24.3 us (29%)
  between operations  1.05 us (1%)
    ppermute x20, starting transfers between devices, paired(): return lax.ppermute(value, axis, pairs)  20 us
    ppermute x20, waiting for transfers between devices, paired(): return lax.ppermute(value, axis, pairs)  15.5 us
    ppermute x6, waiting for transfers between devices, shifted(): return lax.ppermute(value, axis, pairs)  12.2 us
    pallas_call x3, Pallas kernels, shards(): local(functools.partial(beam_kernel, 0), (whole, rounded))(*pair, opposing)  6.45 us
    pallas_call x3, Pallas kernels, shards(): local(functools.partial(beam_kernel, 1), (whole, density))(*pair, resident)  6.44 us
    ppermute x3, starting transfers between devices, shards(): lax.ppermute(part, 'station', [(source, source ^ distance) for source in...  4 us
    ppermute x6, starting transfers between devices, shifted(): return lax.ppermute(value, axis, pairs)  3.18 us
    pallas_call x1, Pallas kernels, shards(): local(first_kernel, (whole, whole, density, rounded), in_specs=[pl.BlockS...  2.27 us
  transfers between devices with their start and end apart: 29, of which 23 were waited for; matrix products, arithmetic and copies ran while one was open for 0% of the time, Pallas kernels for 17%

profile of v5, /device:TPU:0, one launch (start us, length us, event | category | flops | bytes accessed | tf_op | source)
XLA Modules:
  0.0 82.8 jit_solution(17404743798210263345)
XLA Ops:
  0.6 2.3 %shard_map.69 = (f32[4,8192]{1,0:T(4,128)S(1)}, f32[4,8192]{1,0:T(4,128)S(1)}, f32[128,128]{1,0:T(8,128)S(1)}, bf16[128,128]{1,0:T(8,128)(2,1)S(1)}) custom-call(f32[4,8192]{1,0:T(4,128)} %bitcast.8, f32[4,8192]{1,0:T(4,128)} %bitcast.9), custom_call_target="tpu_custom_call" | custom-call | tf_op jit(solution)/shard_map/pallas_call | solution.py:270
  2.9 0.6 collective-permute-start
  3.5 0.9 %collective-permute-done = bf16[128,128]{1,0:T(8,128)(2,1)S(1)} collective-permute-done((bf16[128,128]{1,0:T(8,128)(2,1)S(1)}, bf16[128,128]{1,0:T(8,128)(2,1)S(1)}, u32[]{:S(2)}, u32[]{:S(2)}) %collective-permute-start) | collective-permute-done | bytes 32800 | tf_op jit(solution)/shard_map/ppermute | solution.py:33
  4.3 5.0 %collective-permute-start.1 = (bf16[128,128]{1,0:T(8,128)(2,1)S(1)}, bf16[128,128]{1,0:T(8,128)(2,1)S(1)}, u32[]{:S(2)}, u32[]{:S(2)}) collective-permute-start(bf16[128,128]{1,0:T(8,128)(2,1)S(1)} %fusion.6), channel_id=1, source_target_pairs={{0,6},{1,7},{2,4},{3,5},{4,2},{5,3},{6,0},{7,1},{8,14},{9,15},{10,... | collective-permute-start | bytes 98312 | tf_op jit(solution)/shard_map/ppermute | solution.py:33
  9.3 0.6 collective-permute-start.3
  10.0 0.7 shard_map.70
  10.7 0.6 collective-permute-done.1
  11.2 2.9 %collective-permute-done.2 = bf16[128,128]{1,0:T(8,128)(2,1)S(1)} collective-permute-done((bf16[128,128]{1,0:T(8,128)(2,1)S(1)}, bf16[128,128]{1,0:T(8,128)(2,1)S(1)}, u32[]{:S(2)}, u32[]{:S(2)}) %collective-permute-start.2) | collective-permute-done | bytes 32800 | tf_op jit(solution)/shard_map/ppermute | solution.py:33
  14.2 0.5 shard_map.71.own_ref
  14.7 1.2 %collective-permute-done.4.other_ref = bf16[256,128]{1,0:T(8,128)(2,1)S(1)} collective-permute-done((bf16[256,128]{1,0:T(8,128)(2,1)S(1)}, bf16[256,128]{1,0:T(8,128)(2,1)S(1)}, u32[]{:S(2)}, u32[]{:S(2)}) %collective-permute-start.4) | collective-permute-done | bytes 65568 | tf_op jit(solution)/shard_map/ppermute | solution.py:33
  16.0 2.2 %shard_map.73 = (f32[4,8192]{1,0:T(4,128)S(1)}, bf16[128,128]{1,0:T(8,128)(2,1)S(1)}) custom-call(bf16[256,128]{1,0:T(8,128)(2,1)S(1)} %shard_map.71.own_ref, bf16[256,128]{1,0:T(8,128)(2,1)S(1)} %collective-permute-done.4.other_ref, f32[4,8192]{1,0:T(4,128)S(1)} %get-tuple-element.30.beam_ref), custom_call_target="tpu_custom_call" | custom-call | tf_op jit(solution)/shard_map/pallas_call | solution.py:294
  18.1 1.6 %collective-permute-start.5 = (bf16[128,128]{1,0:T(8,128)(2,1)S(1)}, bf16[128,128]{1,0:T(8,128)(2,1)S(1)}, u32[]{:S(2)}, u32[]{:S(2)}) collective-permute-start(bf16[128,128]{1,0:T(8,128)(2,1)S(1)} %get-tuple-element.31), channel_id=1, source_target_pairs={{0,8},{8,16},{16,24},{24,0},{1,9},{9,17},{17,25},{25,1},{2,10},{10... | collective-permute-start | bytes 98312 | tf_op jit(solution)/shard_map/ppermute | solution.py:28
  19.7 2.1 %shard_map.72 = (f32[4,8192]{1,0:T(4,128)S(1)}, f32[128,128]{1,0:T(8,128)S(1)}) custom-call(bf16[256,128]{1,0:T(8,128)(2,1)S(1)} %shard_map.71.own_ref, bf16[256,128]{1,0:T(8,128)(2,1)S(1)} %collective-permute-done.4.other_ref, f32[4,8192]{1,0:T(4,128)S(1)} %get-tuple-element.28.beam_ref), custom_call_target="tpu_custom_call" | custom-call | tf_op jit(solution)/shard_map/pallas_call | solution.py:297
  21.8 1.2 %collective-permute-done.5 = bf16[128,128]{1,0:T(8,128)(2,1)S(1)} collective-permute-done((bf16[128,128]{1,0:T(8,128)(2,1)S(1)}, bf16[128,128]{1,0:T(8,128)(2,1)S(1)}, u32[]{:S(2)}, u32[]{:S(2)}) %collective-permute-start.5) | collective-permute-done | bytes 32800 | tf_op jit(solution)/shard_map/ppermute | solution.py:28
  23.1 1.2 %collective-permute-done.6 = bf16[128,128]{1,0:T(8,128)(2,1)S(1)} collective-permute-done((bf16[128,128]{1,0:T(8,128)(2,1)S(1)}, bf16[128,128]{1,0:T(8,128)(2,1)S(1)}, u32[]{:S(2)}, u32[]{:S(2)}) %collective-permute-start.6) | collective-permute-done | bytes 32800 | tf_op jit(solution)/shard_map/ppermute | solution.py:33
  24.3 1.6 %collective-permute-start.7 = (bf16[128,128]{1,0:T(8,128)(2,1)S(1)}, bf16[128,128]{1,0:T(8,128)(2,1)S(1)}, u32[]{:S(2)}, u32[]{:S(2)}) collective-permute-start(bf16[128,128]{1,0:T(8,128)(2,1)S(1)} %fusion.9), channel_id=1, source_target_pairs={{0,6},{1,7},{2,4},{3,5},{4,2},{5,3},{6,0},{7,1},{8,14},{9,15},{10,... | collective-permute-start | bytes 98312 | tf_op jit(solution)/shard_map/ppermute | solution.py:33
  25.9 0.6 collective-permute-start.8
  26.5 2.3 %collective-permute-start.9 = (bf16[128,128]{1,0:T(8,128)(2,1)S(1)}, bf16[128,128]{1,0:T(8,128)(2,1)S(1)}, u32[]{:S(2)}, u32[]{:S(2)}) collective-permute-start(bf16[128,128]{1,0:T(8,128)(2,1)S(1)} %fusion.9), channel_id=1, source_target_pairs={{0,2},{1,3},{2,0},{3,1},{4,6},{5,7},{6,4},{7,5},{8,10},{9,11},{10,... | collective-permute-start | bytes 98312 | tf_op jit(solution)/shard_map/ppermute | solution.py:33
  28.8 0.6 collective-permute-start.11
  29.4 1.0 %collective-permute-done.7 = bf16[128,128]{1,0:T(8,128)(2,1)S(1)} collective-permute-done((bf16[128,128]{1,0:T(8,128)(2,1)S(1)}, bf16[128,128]{1,0:T(8,128)(2,1)S(1)}, u32[]{:S(2)}, u32[]{:S(2)}) %collective-permute-start.7) | collective-permute-done | bytes 32800 | tf_op jit(solution)/shard_map/ppermute | solution.py:33
  31.6 3.0 %collective-permute-done.11.beam_ref = f32[4,8192]{1,0:T(4,128)S(1)} collective-permute-done((f32[4,8192]{1,0:T(4,128)S(1)}, f32[4,8192]{1,0:T(4,128)S(1)}, u32[]{:S(2)}, u32[]{:S(2)}) %collective-permute-start.11) | collective-permute-done | bytes 131104 | tf_op jit(solution)/shard_map/ppermute | solution.py:28
  34.6 2.2 %shard_map.76 = (f32[4,8192]{1,0:T(4,128)S(1)}, bf16[128,128]{1,0:T(8,128)(2,1)S(1)}) custom-call(bf16[256,128]{1,0:T(8,128)(2,1)S(1)} %shard_map.74.own_ref, bf16[256,128]{1,0:T(8,128)(2,1)S(1)} %collective-permute-done.10.other_ref, f32[4,8192]{1,0:T(4,128)S(1)} %collective-permute-done.11.beam_ref), custom_call_target="tpu_custom_call" | custom-call | tf_op jit(solution)/shard_map/pallas_call | solution.py:294
  37.0 2.1 %shard_map.75 = (f32[4,8192]{1,0:T(4,128)S(1)}, f32[128,128]{1,0:T(8,128)S(1)}) custom-call(bf16[256,128]{1,0:T(8,128)(2,1)S(1)} %shard_map.74.own_ref, bf16[256,128]{1,0:T(8,128)(2,1)S(1)} %collective-permute-done.10.other_ref, f32[4,8192]{1,0:T(4,128)S(1)} %get-tuple-element.32.beam_ref), custom_call_target="tpu_custom_call" | custom-call | tf_op jit(solution)/shard_map/pallas_call | solution.py:297
  39.2 2.6 %collective-permute-done.12 = bf16[128,128]{1,0:T(8,128)(2,1)S(1)} collective-permute-done((bf16[128,128]{1,0:T(8,128)(2,1)S(1)}, bf16[128,128]{1,0:T(8,128)(2,1)S(1)}, u32[]{:S(2)}, u32[]{:S(2)}) %collective-permute-start.12) | collective-permute-done | bytes 32800 | tf_op jit(solution)/shard_map/ppermute | solution.py:28
  41.9 1.2 %collective-permute-done.13 = bf16[128,128]{1,0:T(8,128)(2,1)S(1)} collective-permute-done((bf16[128,128]{1,0:T(8,128)(2,1)S(1)}, bf16[128,128]{1,0:T(8,128)(2,1)S(1)}, u32[]{:S(2)}, u32[]{:S(2)}) %collective-permute-start.13) | collective-permute-done | bytes 32800 | tf_op jit(solution)/shard_map/ppermute | solution.py:33
  43.1 1.6 %collective-permute-start.14 = (bf16[128,128]{1,0:T(8,128)(2,1)S(1)}, bf16[128,128]{1,0:T(8,128)(2,1)S(1)}, u32[]{:S(2)}, u32[]{:S(2)}) collective-permute-start(bf16[128,128]{1,0:T(8,128)(2,1)S(1)} %fusion.8), channel_id=1, source_target_pairs={{0,6},{1,7},{2,4},{3,5},{4,2},{5,3},{6,0},{7,1},{8,14},{9,15},{10,... | collective-permute-start | bytes 98312 | tf_op jit(solution)/shard_map/ppermute | solution.py:33
  44.7 2.9 %collective-permute-start.16 = (bf16[128,128]{1,0:T(8,128)(2,1)S(1)}, bf16[128,128]{1,0:T(8,128)(2,1)S(1)}, u32[]{:S(2)}, u32[]{:S(2)}) collective-permute-start(bf16[128,128]{1,0:T(8,128)(2,1)S(1)} %fusion.8), channel_id=1, source_target_pairs={{0,2},{1,3},{2,0},{3,1},{4,6},{5,7},{6,4},{7,5},{8,10},{9,11},{10,... | collective-permute-start | bytes 98312 | tf_op jit(solution)/shard_map/ppermute | solution.py:33
  47.9 1.0 %collective-permute-done.14 = bf16[128,128]{1,0:T(8,128)(2,1)S(1)} collective-permute-done((bf16[128,128]{1,0:T(8,128)(2,1)S(1)}, bf16[128,128]{1,0:T(8,128)(2,1)S(1)}, u32[]{:S(2)}, u32[]{:S(2)}) %collective-permute-start.14) | collective-permute-done | bytes 32800 | tf_op jit(solution)/shard_map/ppermute | solution.py:33
  48.9 0.9 %collective-permute-done.15 = bf16[128,128]{1,0:T(8,128)(2,1)S(1)} collective-permute-done((bf16[128,128]{1,0:T(8,128)(2,1)S(1)}, bf16[128,128]{1,0:T(8,128)(2,1)S(1)}, u32[]{:S(2)}, u32[]{:S(2)}) %collective-permute-start.15) | collective-permute-done | bytes 32800 | tf_op jit(solution)/shard_map/ppermute | solution.py:33
  50.1 0.5 shard_map.77.own_ref
  50.7 2.8 %collective-permute-done.18.beam_ref = f32[4,8192]{1,0:T(4,128)S(1)} collective-permute-done((f32[4,8192]{1,0:T(4,128)S(1)}, f32[4,8192]{1,0:T(4,128)S(1)}, u32[]{:S(2)}, u32[]{:S(2)}) %collective-permute-start.18) | collective-permute-done | bytes 131104 | tf_op jit(solution)/shard_map/ppermute | solution.py:28
  53.5 2.2 %shard_map.79 = (f32[4,8192]{1,0:T(4,128)S(1)}, bf16[128,128]{1,0:T(8,128)(2,1)S(1)}) custom-call(bf16[256,128]{1,0:T(8,128)(2,1)S(1)} %shard_map.77.own_ref, bf16[256,128]{1,0:T(8,128)(2,1)S(1)} %collective-permute-done.17.other_ref, f32[4,8192]{1,0:T(4,128)S(1)} %collective-permute-done.18.beam_ref), custom_call_target="tpu_custom_call" | custom-call | tf_op jit(solution)/shard_map/pallas_call | solution.py:294
  55.7 2.1 %shard_map.78 = (f32[4,8192]{1,0:T(4,128)S(1)}, f32[128,128]{1,0:T(8,128)S(1)}) custom-call(bf16[256,128]{1,0:T(8,128)(2,1)S(1)} %shard_map.77.own_ref, bf16[256,128]{1,0:T(8,128)(2,1)S(1)} %collective-permute-done.17.other_ref, f32[4,8192]{1,0:T(4,128)S(1)} %get-tuple-element.36.beam_ref), custom_call_target="tpu_custom_call" | custom-call | tf_op jit(solution)/shard_map/pallas_call | solution.py:297
  57.8 2.6 %collective-permute-done.19 = bf16[128,128]{1,0:T(8,128)(2,1)S(1)} collective-permute-done((bf16[128,128]{1,0:T(8,128)(2,1)S(1)}, bf16[128,128]{1,0:T(8,128)(2,1)S(1)}, u32[]{:S(2)}, u32[]{:S(2)}) %collective-permute-start.19) | collective-permute-done | bytes 32800 | tf_op jit(solution)/shard_map/ppermute | solution.py:28
  60.6 1.2 %collective-permute-done.20 = bf16[128,128]{1,0:T(8,128)(2,1)S(1)} collective-permute-done((bf16[128,128]{1,0:T(8,128)(2,1)S(1)}, bf16[128,128]{1,0:T(8,128)(2,1)S(1)}, u32[]{:S(2)}, u32[]{:S(2)}) %collective-permute-start.20) | collective-permute-done | bytes 32800 | tf_op jit(solution)/shard_map/ppermute | solution.py:33
  61.8 1.6 %collective-permute-start.21 = (bf16[128,128]{1,0:T(8,128)(2,1)S(1)}, bf16[128,128]{1,0:T(8,128)(2,1)S(1)}, u32[]{:S(2)}, u32[]{:S(2)}) collective-permute-start(bf16[128,128]{1,0:T(8,128)(2,1)S(1)} %fusion.7), channel_id=1, source_target_pairs={{0,6},{1,7},{2,4},{3,5},{4,2},{5,3},{6,0},{7,1},{8,14},{9,15},{10,... | collective-permute-start | bytes 98312 | tf_op jit(solution)/shard_map/ppermute | solution.py:33
  63.4 2.9 %collective-permute-start.23 = (bf16[128,128]{1,0:T(8,128)(2,1)S(1)}, bf16[128,128]{1,0:T(8,128)(2,1)S(1)}, u32[]{:S(2)}, u32[]{:S(2)}) collective-permute-start(bf16[128,128]{1,0:T(8,128)(2,1)S(1)} %fusion.7), channel_id=1, source_target_pairs={{0,2},{1,3},{2,0},{3,1},{4,6},{5,7},{6,4},{7,5},{8,10},{9,11},{10,... | collective-permute-start | bytes 98312 | tf_op jit(solution)/shard_map/ppermute | solution.py:33
  66.2 1.3 %collective-permute-done.21 = bf16[128,128]{1,0:T(8,128)(2,1)S(1)} collective-permute-done((bf16[128,128]{1,0:T(8,128)(2,1)S(1)}, bf16[128,128]{1,0:T(8,128)(2,1)S(1)}, u32[]{:S(2)}, u32[]{:S(2)}) %collective-permute-start.21) | collective-permute-done | bytes 32800 | tf_op jit(solution)/shard_map/ppermute | solution.py:33
  67.6 0.9 %collective-permute-done.22 = bf16[128,128]{1,0:T(8,128)(2,1)S(1)} collective-permute-done((bf16[128,128]{1,0:T(8,128)(2,1)S(1)}, bf16[128,128]{1,0:T(8,128)(2,1)S(1)}, u32[]{:S(2)}, u32[]{:S(2)}) %collective-permute-start.22) | collective-permute-done | bytes 32800 | tf_op jit(solution)/shard_map/ppermute | solution.py:33
  70.0 1.7 %shard_map.68.slots_ref = s32[64]{0:T(128)S(1)} custom-call(s32[64]{0:T(128)S(1)} %bitcast.5), custom_call_target="tpu_custom_call" | custom-call | tf_op jit(solution)/shard_map/pallas_call | solution.py:285
  71.7 2.0 %shard_map.81 = (f32[32,4,128]{2,1,0:T(4,128)S(1)}, f32[32,4,128]{2,1,0:T(4,128)S(1)}, f32[32,4,128]{2,1,0:T(4,128)S(1)}, f32[32,4,128]{2,1,0:T(4,128)S(1)}) custom-call(s32[64]{0:T(128)S(1)} %shard_map.68.slots_ref, bf16[256,128]{1,0:T(8,128)(2,1)S(1)} %shard_map.80.own_ref, bf16[256,128]{1,0:T(8,128)(2,1)S(1)} %collective-permute-done.24.other_ref, ...), custom_call_target="tpu_custom_call" | custom-call | tf_op jit(solution)/shard_map/pallas_call | solution.py:302
  73.8 2.5 %collective-permute-start.25 = (f32[32,4,128]{2,1,0:T(4,128)S(1)}, f32[32,4,128]{2,1,0:T(4,128)S(1)}, u32[]{:S(2)}, u32[]{:S(2)}) collective-permute-start(f32[32,4,128]{2,1,0:T(4,128)S(1)} %get-tuple-element.42), channel_id=1, source_target_pairs={{0,8},{8,0},{16,24},{24,16},{1,9},{9,1},{17,25},{25,17},{2,10},{10... | collective-permute-start | bytes 196616 | tf_op jit(solution)/shard_map/ppermute | solution.py:313
  76.3 0.5 collective-permute-start.26
  76.8 1.0 %collective-permute-start.27 = (f32[32,4,128]{2,1,0:T(4,128)S(1)}, f32[32,4,128]{2,1,0:T(4,128)S(1)}, u32[]{:S(2)}, u32[]{:S(2)}) collective-permute-start(f32[32,4,128]{2,1,0:T(4,128)S(1)} %get-tuple-element.44), channel_id=1, source_target_pairs={{0,24},{8,16},{16,8},{24,0},{1,25},{9,17},{17,9},{25,1},{2,26},{10... | collective-permute-start | bytes 196616 | tf_op jit(solution)/shard_map/ppermute | solution.py:313
  77.8 2.1 %shard_map.83 = f32[4,8192]{1,0:T(4,128)} custom-call(bf16[256,128]{1,0:T(8,128)(2,1)S(1)} %shard_map.80.own_ref, bf16[256,128]{1,0:T(8,128)(2,1)S(1)} %collective-permute-done.24.other_ref, f32[4,8192]{1,0:T(4,128)S(1)} %collective-permute-done.28.beam_ref), custom_call_target="tpu_custom_call" | custom-call | tf_op jit(solution)/shard_map/pallas_call | solution.py:318
  79.9 1.3 %collective-permute-done.26.refs_2_ = f32[32,4,128]{2,1,0:T(4,128)S(1)} collective-permute-done((f32[32,4,128]{2,1,0:T(4,128)S(1)}, f32[32,4,128]{2,1,0:T(4,128)S(1)}, u32[]{:S(2)}, u32[]{:S(2)}) %collective-permute-start.26) | collective-permute-done | bytes 65568 | tf_op jit(solution)/shard_map/ppermute | solution.py:313
  81.2 0.7 collective-permute-done.27.refs_3_
  81.9 0.7 shard_map.82
  (43 shorter events, 4.0 us)
Async XLA Ops:
  2.9 1.4 %collective-permute-start = (bf16[128,128]{1,0:T(8,128)(2,1)S(1)}, bf16[128,128]{1,0:T(8,128)(2,1)S(1)}, u32[]{:S(2)}, u32[]{:S(2)}) collective-permute-start(bf16[128,128]{1,0:T(8,128)(2,1)S(1)} %get-tuple-element.25), channel_id=1, source_target_pairs={{0,1},{1,0},{2,3},{3,2},{4,5},{5,4},{6,7},{7,6},{8,9},{9,8},{10,11... | collective-permute-start | bytes 98312 | tf_op jit(solution)/shard_map/ppermute | solution.py:33
  4.3 5.7 %copy-start = (f32[128,128]{1,0:T(8,128)S(1)}, f32[128,128]{1,0:T(8,128)}, u32[]{:S(2)}) copy-start(f32[128,128]{1,0:T(8,128)} %smooth_ref.1) | copy-start | bytes 196612
  4.3 5.7 %copy-start.1 = (f32[128,128]{1,0:T(8,128)S(1)}, f32[128,128]{1,0:T(8,128)}, u32[]{:S(2)}) copy-start(f32[128,128]{1,0:T(8,128)} %slope_ref.1) | copy-start | bytes 196612
  4.3 6.9 %collective-permute-start.1 = (bf16[128,128]{1,0:T(8,128)(2,1)S(1)}, bf16[128,128]{1,0:T(8,128)(2,1)S(1)}, u32[]{:S(2)}, u32[]{:S(2)}) collective-permute-start(bf16[128,128]{1,0:T(8,128)(2,1)S(1)} %fusion.6), channel_id=1, source_target_pairs={{0,6},{1,7},{2,4},{3,5},{4,2},{5,3},{6,0},{7,1},{8,14},{9,15},{10,... | collective-permute-start | bytes 98312 | tf_op jit(solution)/shard_map/ppermute | solution.py:33
  9.3 4.8 %collective-permute-start.2 = (bf16[128,128]{1,0:T(8,128)(2,1)S(1)}, bf16[128,128]{1,0:T(8,128)(2,1)S(1)}, u32[]{:S(2)}, u32[]{:S(2)}) collective-permute-start(bf16[128,128]{1,0:T(8,128)(2,1)S(1)} %fusion.6), channel_id=1, source_target_pairs={{0,4},{1,5},{2,6},{3,7},{4,0},{5,1},{6,2},{7,3},{8,12},{9,13},{10,... | collective-permute-start | bytes 98312 | tf_op jit(solution)/shard_map/ppermute | solution.py:33
  9.3 4.8 %collective-permute-start.3 = (bf16[128,128]{1,0:T(8,128)(2,1)S(1)}, bf16[128,128]{1,0:T(8,128)(2,1)S(1)}, u32[]{:S(2)}, u32[]{:S(2)}) collective-permute-start(bf16[128,128]{1,0:T(8,128)(2,1)S(1)} %fusion.6), channel_id=1, source_target_pairs={{0,2},{1,3},{2,0},{3,1},{4,6},{5,7},{6,4},{7,5},{8,10},{9,11},{10,... | collective-permute-start | bytes 98312 | tf_op jit(solution)/shard_map/ppermute | solution.py:33
  14.7 1.3 %collective-permute-start.4 = (bf16[256,128]{1,0:T(8,128)(2,1)S(1)}, bf16[256,128]{1,0:T(8,128)(2,1)S(1)}, u32[]{:S(2)}, u32[]{:S(2)}) collective-permute-start(bf16[256,128]{1,0:T(8,128)(2,1)S(1)} %shard_map.71.own_ref), channel_id=1, source_target_pairs={{0,1},{1,0},{2,3},{3,2},{4,5},{5,4},{6,7},{7,6},{8,9},{9,8},{10,11... | collective-permute-start | bytes 196616 | tf_op jit(solution)/shard_map/ppermute | solution.py:33
  18.1 4.9 %collective-permute-start.5 = (bf16[128,128]{1,0:T(8,128)(2,1)S(1)}, bf16[128,128]{1,0:T(8,128)(2,1)S(1)}, u32[]{:S(2)}, u32[]{:S(2)}) collective-permute-start(bf16[128,128]{1,0:T(8,128)(2,1)S(1)} %get-tuple-element.31), channel_id=1, source_target_pairs={{0,8},{8,16},{16,24},{24,0},{1,9},{9,17},{17,25},{25,1},{2,10},{10... | collective-permute-start | bytes 98312 | tf_op jit(solution)/shard_map/ppermute | solution.py:28
  23.0 1.3 %collective-permute-start.6 = (bf16[128,128]{1,0:T(8,128)(2,1)S(1)}, bf16[128,128]{1,0:T(8,128)(2,1)S(1)}, u32[]{:S(2)}, u32[]{:S(2)}) collective-permute-start(bf16[128,128]{1,0:T(8,128)(2,1)S(1)} %fusion.1), channel_id=1, source_target_pairs={{0,1},{1,0},{2,3},{3,2},{4,5},{5,4},{6,7},{7,6},{8,9},{9,8},{10,11... | collective-permute-start | bytes 98312 | tf_op jit(solution)/shard_map/ppermute | solution.py:33
  24.3 6.1 %collective-permute-start.7 = (bf16[128,128]{1,0:T(8,128)(2,1)S(1)}, bf16[128,128]{1,0:T(8,128)(2,1)S(1)}, u32[]{:S(2)}, u32[]{:S(2)}) collective-permute-start(bf16[128,128]{1,0:T(8,128)(2,1)S(1)} %fusion.9), channel_id=1, source_target_pairs={{0,6},{1,7},{2,4},{3,5},{4,2},{5,3},{6,0},{7,1},{8,14},{9,15},{10,... | collective-permute-start | bytes 98312 | tf_op jit(solution)/shard_map/ppermute | solution.py:33
  25.9 4.9 %collective-permute-start.8 = (bf16[128,128]{1,0:T(8,128)(2,1)S(1)}, bf16[128,128]{1,0:T(8,128)(2,1)S(1)}, u32[]{:S(2)}, u32[]{:S(2)}) collective-permute-start(bf16[128,128]{1,0:T(8,128)(2,1)S(1)} %fusion.9), channel_id=1, source_target_pairs={{0,4},{1,5},{2,6},{3,7},{4,0},{5,1},{6,2},{7,3},{8,12},{9,13},{10,... | collective-permute-start | bytes 98312 | tf_op jit(solution)/shard_map/ppermute | solution.py:33
  26.5 4.6 %collective-permute-start.9 = (bf16[128,128]{1,0:T(8,128)(2,1)S(1)}, bf16[128,128]{1,0:T(8,128)(2,1)S(1)}, u32[]{:S(2)}, u32[]{:S(2)}) collective-permute-start(bf16[128,128]{1,0:T(8,128)(2,1)S(1)} %fusion.9), channel_id=1, source_target_pairs={{0,2},{1,3},{2,0},{3,1},{4,6},{5,7},{6,4},{7,5},{8,10},{9,11},{10,... | collective-permute-start | bytes 98312 | tf_op jit(solution)/shard_map/ppermute | solution.py:33
  28.8 5.9 %collective-permute-start.11 = (f32[4,8192]{1,0:T(4,128)S(1)}, f32[4,8192]{1,0:T(4,128)S(1)}, u32[]{:S(2)}, u32[]{:S(2)}) collective-permute-start(f32[4,8192]{1,0:T(4,128)S(1)} %get-tuple-element.34), channel_id=1, source_target_pairs={{0,8},{8,16},{16,24},{24,0},{1,9},{9,17},{17,25},{25,1},{2,10},{10... | collective-permute-start | bytes 393224 | tf_op jit(solution)/shard_map/ppermute | solution.py:28
  31.6 3.1 %collective-permute-start.10 = (bf16[256,128]{1,0:T(8,128)(2,1)S(1)}, bf16[256,128]{1,0:T(8,128)(2,1)S(1)}, u32[]{:S(2)}, u32[]{:S(2)}) collective-permute-start(bf16[256,128]{1,0:T(8,128)(2,1)S(1)} %shard_map.74.own_ref), channel_id=1, source_target_pairs={{0,1},{1,0},{2,3},{3,2},{4,5},{5,4},{6,7},{7,6},{8,9},{9,8},{10,11... | collective-permute-start | bytes 196616 | tf_op jit(solution)/shard_map/ppermute | solution.py:33
  36.8 5.0 %collective-permute-start.12 = (bf16[128,128]{1,0:T(8,128)(2,1)S(1)}, bf16[128,128]{1,0:T(8,128)(2,1)S(1)}, u32[]{:S(2)}, u32[]{:S(2)}) collective-permute-start(bf16[128,128]{1,0:T(8,128)(2,1)S(1)} %get-tuple-element.35), channel_id=1, source_target_pairs={{0,8},{8,16},{16,24},{24,0},{1,9},{9,17},{17,25},{25,1},{2,10},{10... | collective-permute-start | bytes 98312 | tf_op jit(solution)/shard_map/ppermute | solution.py:28
  41.8 1.3 %collective-permute-start.13 = (bf16[128,128]{1,0:T(8,128)(2,1)S(1)}, bf16[128,128]{1,0:T(8,128)(2,1)S(1)}, u32[]{:S(2)}, u32[]{:S(2)}) collective-permute-start(bf16[128,128]{1,0:T(8,128)(2,1)S(1)} %fusion.3), channel_id=1, source_target_pairs={{0,1},{1,0},{2,3},{3,2},{4,5},{5,4},{6,7},{7,6},{8,9},{9,8},{10,11... | collective-permute-start | bytes 98312 | tf_op jit(solution)/shard_map/ppermute | solution.py:33
  43.1 5.8 %collective-permute-start.14 = (bf16[128,128]{1,0:T(8,128)(2,1)S(1)}, bf16[128,128]{1,0:T(8,128)(2,1)S(1)}, u32[]{:S(2)}, u32[]{:S(2)}) collective-permute-start(bf16[128,128]{1,0:T(8,128)(2,1)S(1)} %fusion.8), channel_id=1, source_target_pairs={{0,6},{1,7},{2,4},{3,5},{4,2},{5,3},{6,0},{7,1},{8,14},{9,15},{10,... | collective-permute-start | bytes 98312 | tf_op jit(solution)/shard_map/ppermute | solution.py:33
  44.7 5.2 %collective-permute-start.15 = (bf16[128,128]{1,0:T(8,128)(2,1)S(1)}, bf16[128,128]{1,0:T(8,128)(2,1)S(1)}, u32[]{:S(2)}, u32[]{:S(2)}) collective-permute-start(bf16[128,128]{1,0:T(8,128)(2,1)S(1)} %fusion.8), channel_id=1, source_target_pairs={{0,4},{1,5},{2,6},{3,7},{4,0},{5,1},{6,2},{7,3},{8,12},{9,13},{10,... | collective-permute-start | bytes 98312 | tf_op jit(solution)/shard_map/ppermute | solution.py:33
  44.7 5.4 %collective-permute-start.16 = (bf16[128,128]{1,0:T(8,128)(2,1)S(1)}, bf16[128,128]{1,0:T(8,128)(2,1)S(1)}, u32[]{:S(2)}, u32[]{:S(2)}) collective-permute-start(bf16[128,128]{1,0:T(8,128)(2,1)S(1)} %fusion.8), channel_id=1, source_target_pairs={{0,2},{1,3},{2,0},{3,1},{4,6},{5,7},{6,4},{7,5},{8,10},{9,11},{10,... | collective-permute-start | bytes 98312 | tf_op jit(solution)/shard_map/ppermute | solution.py:33
  47.6 5.9 %collective-permute-start.18 = (f32[4,8192]{1,0:T(4,128)S(1)}, f32[4,8192]{1,0:T(4,128)S(1)}, u32[]{:S(2)}, u32[]{:S(2)}) collective-permute-start(f32[4,8192]{1,0:T(4,128)S(1)} %get-tuple-element.38), channel_id=1, source_target_pairs={{0,8},{8,16},{16,24},{24,0},{1,9},{9,17},{17,25},{25,1},{2,10},{10... | collective-permute-start | bytes 393224 | tf_op jit(solution)/shard_map/ppermute | solution.py:28
  50.6 2.9 %collective-permute-start.17 = (bf16[256,128]{1,0:T(8,128)(2,1)S(1)}, bf16[256,128]{1,0:T(8,128)(2,1)S(1)}, u32[]{:S(2)}, u32[]{:S(2)}) collective-permute-start(bf16[256,128]{1,0:T(8,128)(2,1)S(1)} %shard_map.77.own_ref), channel_id=1, source_target_pairs={{0,1},{1,0},{2,3},{3,2},{4,5},{5,4},{6,7},{7,6},{8,9},{9,8},{10,11... | collective-permute-start | bytes 196616 | tf_op jit(solution)/shard_map/ppermute | solution.py:33
  55.6 4.9 %collective-permute-start.19 = (bf16[128,128]{1,0:T(8,128)(2,1)S(1)}, bf16[128,128]{1,0:T(8,128)(2,1)S(1)}, u32[]{:S(2)}, u32[]{:S(2)}) collective-permute-start(bf16[128,128]{1,0:T(8,128)(2,1)S(1)} %get-tuple-element.39), channel_id=1, source_target_pairs={{0,8},{8,16},{16,24},{24,0},{1,9},{9,17},{17,25},{25,1},{2,10},{10... | collective-permute-start | bytes 98312 | tf_op jit(solution)/shard_map/ppermute | solution.py:28
  60.5 1.3 %collective-permute-start.20 = (bf16[128,128]{1,0:T(8,128)(2,1)S(1)}, bf16[128,128]{1,0:T(8,128)(2,1)S(1)}, u32[]{:S(2)}, u32[]{:S(2)}) collective-permute-start(bf16[128,128]{1,0:T(8,128)(2,1)S(1)} %fusion.5), channel_id=1, source_target_pairs={{0,1},{1,0},{2,3},{3,2},{4,5},{5,4},{6,7},{7,6},{8,9},{9,8},{10,11... | collective-permute-start | bytes 98312 | tf_op jit(solution)/shard_map/ppermute | solution.py:33
  61.8 5.8 %collective-permute-start.21 = (bf16[128,128]{1,0:T(8,128)(2,1)S(1)}, bf16[128,128]{1,0:T(8,128)(2,1)S(1)}, u32[]{:S(2)}, u32[]{:S(2)}) collective-permute-start(bf16[128,128]{1,0:T(8,128)(2,1)S(1)} %fusion.7), channel_id=1, source_target_pairs={{0,6},{1,7},{2,4},{3,5},{4,2},{5,3},{6,0},{7,1},{8,14},{9,15},{10,... | collective-permute-start | bytes 98312 | tf_op jit(solution)/shard_map/ppermute | solution.py:33
  63.4 5.2 %collective-permute-start.22 = (bf16[128,128]{1,0:T(8,128)(2,1)S(1)}, bf16[128,128]{1,0:T(8,128)(2,1)S(1)}, u32[]{:S(2)}, u32[]{:S(2)}) collective-permute-start(bf16[128,128]{1,0:T(8,128)(2,1)S(1)} %fusion.7), channel_id=1, source_target_pairs={{0,4},{1,5},{2,6},{3,7},{4,0},{5,1},{6,2},{7,3},{8,12},{9,13},{10,... | collective-permute-start | bytes 98312 | tf_op jit(solution)/shard_map/ppermute | solution.py:33
  63.4 5.4 %collective-permute-start.23 = (bf16[128,128]{1,0:T(8,128)(2,1)S(1)}, bf16[128,128]{1,0:T(8,128)(2,1)S(1)}, u32[]{:S(2)}, u32[]{:S(2)}) collective-permute-start(bf16[128,128]{1,0:T(8,128)(2,1)S(1)} %fusion.7), channel_id=1, source_target_pairs={{0,2},{1,3},{2,0},{3,1},{4,6},{5,7},{6,4},{7,5},{8,10},{9,11},{10,... | collective-permute-start | bytes 98312 | tf_op jit(solution)/shard_map/ppermute | solution.py:33
  69.2 2.5 %collective-permute-start.24 = (bf16[256,128]{1,0:T(8,128)(2,1)S(1)}, bf16[256,128]{1,0:T(8,128)(2,1)S(1)}, u32[]{:S(2)}, u32[]{:S(2)}) collective-permute-start(bf16[256,128]{1,0:T(8,128)(2,1)S(1)} %shard_map.80.own_ref), channel_id=1, source_target_pairs={{0,1},{1,0},{2,3},{3,2},{4,5},{5,4},{6,7},{7,6},{8,9},{9,8},{10,11... | collective-permute-start | bytes 196616 | tf_op jit(solution)/shard_map/ppermute | solution.py:33
  69.3 0.7 copy-start.2
  69.3 8.5 %collective-permute-start.28 = (f32[4,8192]{1,0:T(4,128)S(1)}, f32[4,8192]{1,0:T(4,128)S(1)}, u32[]{:S(2)}, u32[]{:S(2)}) collective-permute-start(f32[4,8192]{1,0:T(4,128)S(1)} %get-tuple-element.45), channel_id=1, source_target_pairs={{0,8},{8,16},{16,24},{24,0},{1,9},{9,17},{17,25},{25,1},{2,10},{10... | collective-permute-start | bytes 393224 | tf_op jit(solution)/shard_map/ppermute | solution.py:28
  73.8 6.1 %collective-permute-start.25 = (f32[32,4,128]{2,1,0:T(4,128)S(1)}, f32[32,4,128]{2,1,0:T(4,128)S(1)}, u32[]{:S(2)}, u32[]{:S(2)}) collective-permute-start(f32[32,4,128]{2,1,0:T(4,128)S(1)} %get-tuple-element.42), channel_id=1, source_target_pairs={{0,8},{8,0},{16,24},{24,16},{1,9},{9,1},{17,25},{25,17},{2,10},{10... | collective-permute-start | bytes 196616 | tf_op jit(solution)/shard_map/ppermute | solution.py:313
  76.3 5.0 %collective-permute-start.26 = (f32[32,4,128]{2,1,0:T(4,128)S(1)}, f32[32,4,128]{2,1,0:T(4,128)S(1)}, u32[]{:S(2)}, u32[]{:S(2)}) collective-permute-start(f32[32,4,128]{2,1,0:T(4,128)S(1)} %get-tuple-element.43), channel_id=1, source_target_pairs={{0,16},{8,24},{16,0},{24,8},{1,17},{9,25},{17,1},{25,9},{2,18},{10... | collective-permute-start | bytes 196616 | tf_op jit(solution)/shard_map/ppermute | solution.py:313
  76.8 5.2 %collective-permute-start.27 = (f32[32,4,128]{2,1,0:T(4,128)S(1)}, f32[32,4,128]{2,1,0:T(4,128)S(1)}, u32[]{:S(2)}, u32[]{:S(2)}) collective-permute-start(f32[32,4,128]{2,1,0:T(4,128)S(1)} %get-tuple-element.44), channel_id=1, source_target_pairs={{0,24},{8,16},{16,8},{24,0},{1,25},{9,17},{17,9},{25,1},{2,26},{10... | collective-permute-start | bytes 196616 | tf_op jit(solution)/shard_map/ppermute | solution.py:313

commit v6 on v5

--- a/solution.py
+++ b/solution.py
@@ -28,15 +28,30 @@
     return lax.ppermute(value, axis, pairs)
 
 
+def crossed(value):
+    stations, groups = lax.axis_size("station"), lax.axis_size("dom")
+    pairs = [
+        (station * groups + index, (station + 1) % stations * groups + (index ^ 1))
+        for station in range(stations)
+        for index in range(groups)
+    ]
+    return lax.ppermute(value, ("station", "dom"), pairs)
+
+
 def paired(value, axis, distance):
     pairs = [(source, source ^ distance) for source in range(lax.axis_size(axis))]
     return lax.ppermute(value, axis, pairs)
 
 
+def across(chip):
+    return 2 * chip + chip % 2
+
+
 def summed(kept, sent, axis):
     value = kept + paired(sent, axis, 1).astype(jnp.float32)
     sent = value.astype(jnp.bfloat16)
-    far = [paired(sent, axis, distance) for distance in range(2, lax.axis_size(axis), 2)]
+    chips = lax.axis_size(axis) // 2
+    far = [paired(sent, axis, across(chip)) for chip in range(1, chips)]
     return value + sum(part.astype(jnp.float32) for part in reversed(far))
 
 
@@ -139,13 +154,18 @@
     return [pl.ds(start, width) for start in range(0, count, width)]
 
 
+def keeps():
+    index = lax.axis_index("dom")
+    return lax.rem(index + index // 2, 2)
+
+
 def share(resident, opposing):
-    even = lax.rem(lax.axis_index("dom"), 2) == 0
+    even = keeps() == 0
     return jnp.where(even, resident, opposing), jnp.where(even, opposing, resident).astype(jnp.bfloat16)
 
 
 def chosen(which, own_ref, other_ref):
-    own = lax.rem(lax.axis_index("dom"), 2) == which
+    own = keeps() == which
     return jnp.where(own, own_ref[...], other_ref[...])
 
 
@@ -292,7 +312,7 @@
     pair = both_tables(kept, sent)
     for _ in range(FRONTS - 1):
         opposing, part = local(functools.partial(beam_kernel, 0), (whole, rounded))(*pair, opposing)
-        part = shifted(part, "station", 1)
+        part = crossed(part)
         opposing = shifted(opposing, "station", 1)
         resident, total = local(functools.partial(beam_kernel, 1), (whole, density))(
             *pair, resident

time: 83 us -> 81.9 us (0.987)
  starting transfers between devices: 27.2 us -> 25.5 us
    ppermute x6 -> x3, waiting for transfers between devices: 12.2 us -> 6.1 us  [shifted(): return lax.ppermute(value, axis, pairs)]
    ppermute x0 -> x3, waiting for transfers between devices: none -> 5.21 us  [crossed(): return lax.ppermute(value, ('station', 'dom'), pairs)]
    ppermute x20, starting transfers between devices: 20 us -> 18.2 us  [paired(): return lax.ppermute(value, axis, pairs)]
    ppermute x20, waiting for transfers between devices: 15.5 us -> 17.3 us  [paired(): return lax.ppermute(value, axis, pairs)]
    ppermute x0 -> x3, starting transfers between devices: none -> 1.61 us  [crossed(): return lax.ppermute(value, ('station', 'dom'), pairs)]
    ppermute x6 -> x3, starting transfers between devices: 3.18 us -> 1.82 us  [shifted(): return lax.ppermute(value, axis, pairs)]
  transfers between devices with their start and end apart: 29 -> 29, of which waited for: 23 -> 20; matrix products, arithmetic and copies ran while one was open for 0% -> 0% of each run, Pallas kernels for 17% -> 17%
where the time goes in v6:
time: 81.9 us; the launch traced here: 81.7 us
  waiting for transfers between devices  30.6 us (37%)
  starting transfers between devices  25.5 us (31%)
  Pallas kernels  24.3 us (30%)
  between operations  1.01 us (1%)
    ppermute x20, starting transfers between devices, paired(): return lax.ppermute(value, axis, pairs)  18.2 us
    ppermute x20, waiting for transfers between devices, paired(): return lax.ppermute(value, axis, pairs)  17.3 us
    pallas_call x3, Pallas kernels, shards(): local(functools.partial(beam_kernel, 0), (whole, rounded))(*pair, opposing)  6.45 us
    pallas_call x3, Pallas kernels, shards(): local(functools.partial(beam_kernel, 1), (whole, density))(*pair, resident)  6.43 us
    ppermute x3, waiting for transfers between devices, shifted(): return lax.ppermute(value, axis, pairs)  6.1 us
    ppermute x3, waiting for transfers between devices, crossed(): return lax.ppermute(value, ('station', 'dom'), pairs)  5.21 us
    ppermute x3, starting transfers between devices, shards(): lax.ppermute(part, 'station', [(source, source ^ distance) for source in...  3.96 us
    pallas_call x1, Pallas kernels, shards(): local(first_kernel, (whole, whole, density, rounded), in_specs=[pl.BlockS...  2.27 us
  transfers between devices with their start and end apart: 29, of which 20 were waited for; matrix products, arithmetic and copies ran while one was open for 0% of the time, Pallas kernels for 17%

profile of v6, /device:TPU:0, one launch (start us, length us, event | category | flops | bytes accessed | tf_op | source)
XLA Modules:
  0.0 81.7 jit_solution(1954990970541071613)
XLA Ops:
  0.6 2.3 %shard_map.69 = (f32[4,8192]{1,0:T(4,128)S(1)}, f32[4,8192]{1,0:T(4,128)S(1)}, f32[128,128]{1,0:T(8,128)S(1)}, bf16[128,128]{1,0:T(8,128)(2,1)S(1)}) custom-call(f32[4,8192]{1,0:T(4,128)} %bitcast.8, f32[4,8192]{1,0:T(4,128)} %bitcast.9), custom_call_target="tpu_custom_call" | custom-call | tf_op jit(solution)/shard_map/pallas_call | solution.py:290
  2.9 0.6 collective-permute-start
  3.5 0.9 %collective-permute-done = bf16[128,128]{1,0:T(8,128)(2,1)S(1)} collective-permute-done((bf16[128,128]{1,0:T(8,128)(2,1)S(1)}, bf16[128,128]{1,0:T(8,128)(2,1)S(1)}, u32[]{:S(2)}, u32[]{:S(2)}) %collective-permute-start) | collective-permute-done | bytes 32800 | tf_op jit(solution)/shard_map/ppermute | solution.py:43
  4.3 4.8 %collective-permute-start.1 = (bf16[128,128]{1,0:T(8,128)(2,1)S(1)}, bf16[128,128]{1,0:T(8,128)(2,1)S(1)}, u32[]{:S(2)}, u32[]{:S(2)}) collective-permute-start(bf16[128,128]{1,0:T(8,128)(2,1)S(1)} %fusion.6), channel_id=1, source_target_pairs={{0,7},{1,6},{2,5},{3,4},{4,3},{5,2},{6,1},{7,0},{8,15},{9,14},{10,... | collective-permute-start | bytes 98312 | tf_op jit(solution)/shard_map/ppermute | solution.py:43
  9.5 0.7 shard_map.70
  10.1 0.8 collective-permute-done.1
  10.9 3.0 %collective-permute-done.2 = bf16[128,128]{1,0:T(8,128)(2,1)S(1)} collective-permute-done((bf16[128,128]{1,0:T(8,128)(2,1)S(1)}, bf16[128,128]{1,0:T(8,128)(2,1)S(1)}, u32[]{:S(2)}, u32[]{:S(2)}) %collective-permute-start.2) | collective-permute-done | bytes 32800 | tf_op jit(solution)/shard_map/ppermute | solution.py:43
  14.5 1.2 %collective-permute-done.4.other_ref = bf16[256,128]{1,0:T(8,128)(2,1)S(1)} collective-permute-done((bf16[256,128]{1,0:T(8,128)(2,1)S(1)}, bf16[256,128]{1,0:T(8,128)(2,1)S(1)}, u32[]{:S(2)}, u32[]{:S(2)}) %collective-permute-start.4) | collective-permute-done | bytes 65568 | tf_op jit(solution)/shard_map/ppermute | solution.py:43
  15.7 2.1 %shard_map.73 = (f32[4,8192]{1,0:T(4,128)S(1)}, bf16[128,128]{1,0:T(8,128)(2,1)S(1)}) custom-call(bf16[256,128]{1,0:T(8,128)(2,1)S(1)} %shard_map.71.own_ref, bf16[256,128]{1,0:T(8,128)(2,1)S(1)} %collective-permute-done.4.other_ref, f32[4,8192]{1,0:T(4,128)S(1)} %get-tuple-element.30.beam_ref), custom_call_target="tpu_custom_call" | custom-call | tf_op jit(solution)/shard_map/pallas_call | solution.py:314
  17.9 1.3 %collective-permute-start.5 = (bf16[128,128]{1,0:T(8,128)(2,1)S(1)}, bf16[128,128]{1,0:T(8,128)(2,1)S(1)}, u32[]{:S(2)}, u32[]{:S(2)}) collective-permute-start(bf16[128,128]{1,0:T(8,128)(2,1)S(1)} %get-tuple-element.31), channel_id=1, source_target_pairs={{0,9},{1,8},{2,11},{3,10},{4,13},{5,12},{6,15},{7,14},{8,17},{9,16... | collective-permute-start | bytes 98312 | tf_op jit(solution)/shard_map/ppermute | solution.py:38
  19.2 2.1 %shard_map.72 = (f32[4,8192]{1,0:T(4,128)S(1)}, f32[128,128]{1,0:T(8,128)S(1)}) custom-call(bf16[256,128]{1,0:T(8,128)(2,1)S(1)} %shard_map.71.own_ref, bf16[256,128]{1,0:T(8,128)(2,1)S(1)} %collective-permute-done.4.other_ref, f32[4,8192]{1,0:T(4,128)S(1)} %get-tuple-element.28.beam_ref), custom_call_target="tpu_custom_call" | custom-call | tf_op jit(solution)/shard_map/pallas_call | solution.py:317
  21.4 0.8 %collective-permute-done.5 = bf16[128,128]{1,0:T(8,128)(2,1)S(1)} collective-permute-done((bf16[128,128]{1,0:T(8,128)(2,1)S(1)}, bf16[128,128]{1,0:T(8,128)(2,1)S(1)}, u32[]{:S(2)}, u32[]{:S(2)}) %collective-permute-start.5) | collective-permute-done | bytes 32800 | tf_op jit(solution)/shard_map/ppermute | solution.py:38
  22.4 1.0 %collective-permute-done.6 = bf16[128,128]{1,0:T(8,128)(2,1)S(1)} collective-permute-done((bf16[128,128]{1,0:T(8,128)(2,1)S(1)}, bf16[128,128]{1,0:T(8,128)(2,1)S(1)}, u32[]{:S(2)}, u32[]{:S(2)}) %collective-permute-start.6) | collective-permute-done | bytes 32800 | tf_op jit(solution)/shard_map/ppermute | solution.py:43
  23.5 1.3 %collective-permute-start.7 = (bf16[128,128]{1,0:T(8,128)(2,1)S(1)}, bf16[128,128]{1,0:T(8,128)(2,1)S(1)}, u32[]{:S(2)}, u32[]{:S(2)}) collective-permute-start(bf16[128,128]{1,0:T(8,128)(2,1)S(1)} %fusion.9), channel_id=1, source_target_pairs={{0,7},{1,6},{2,5},{3,4},{4,3},{5,2},{6,1},{7,0},{8,15},{9,14},{10,... | collective-permute-start | bytes 98312 | tf_op jit(solution)/shard_map/ppermute | solution.py:43
  25.2 2.2 %collective-permute-start.9 = (bf16[128,128]{1,0:T(8,128)(2,1)S(1)}, bf16[128,128]{1,0:T(8,128)(2,1)S(1)}, u32[]{:S(2)}, u32[]{:S(2)}) collective-permute-start(bf16[128,128]{1,0:T(8,128)(2,1)S(1)} %fusion.9), channel_id=1, source_target_pairs={{0,3},{1,2},{2,1},{3,0},{4,7},{5,6},{6,5},{7,4},{8,11},{9,10},{10,... | collective-permute-start | bytes 98312 | tf_op jit(solution)/shard_map/ppermute | solution.py:43
  27.4 0.7 collective-permute-start.11
  28.1 0.6 collective-permute-done.7
  28.7 1.7 %collective-permute-done.8 = bf16[128,128]{1,0:T(8,128)(2,1)S(1)} collective-permute-done((bf16[128,128]{1,0:T(8,128)(2,1)S(1)}, bf16[128,128]{1,0:T(8,128)(2,1)S(1)}, u32[]{:S(2)}, u32[]{:S(2)}) %collective-permute-start.8) | collective-permute-done | bytes 32800 | tf_op jit(solution)/shard_map/ppermute | solution.py:43
  30.5 0.5 shard_map.74.own_ref
  31.1 3.0 %collective-permute-done.11.beam_ref = f32[4,8192]{1,0:T(4,128)S(1)} collective-permute-done((f32[4,8192]{1,0:T(4,128)S(1)}, f32[4,8192]{1,0:T(4,128)S(1)}, u32[]{:S(2)}, u32[]{:S(2)}) %collective-permute-start.11) | collective-permute-done | bytes 131104 | tf_op jit(solution)/shard_map/ppermute | solution.py:28
  34.1 2.2 %shard_map.76 = (f32[4,8192]{1,0:T(4,128)S(1)}, bf16[128,128]{1,0:T(8,128)(2,1)S(1)}) custom-call(bf16[256,128]{1,0:T(8,128)(2,1)S(1)} %shard_map.74.own_ref, bf16[256,128]{1,0:T(8,128)(2,1)S(1)} %collective-permute-done.10.other_ref, f32[4,8192]{1,0:T(4,128)S(1)} %collective-permute-done.11.beam_ref), custom_call_target="tpu_custom_call" | custom-call | tf_op jit(solution)/shard_map/pallas_call | solution.py:314
  36.5 2.1 %shard_map.75 = (f32[4,8192]{1,0:T(4,128)S(1)}, f32[128,128]{1,0:T(8,128)S(1)}) custom-call(bf16[256,128]{1,0:T(8,128)(2,1)S(1)} %shard_map.74.own_ref, bf16[256,128]{1,0:T(8,128)(2,1)S(1)} %collective-permute-done.10.other_ref, f32[4,8192]{1,0:T(4,128)S(1)} %get-tuple-element.32.beam_ref), custom_call_target="tpu_custom_call" | custom-call | tf_op jit(solution)/shard_map/pallas_call | solution.py:317
  38.7 2.2 %collective-permute-done.12 = bf16[128,128]{1,0:T(8,128)(2,1)S(1)} collective-permute-done((bf16[128,128]{1,0:T(8,128)(2,1)S(1)}, bf16[128,128]{1,0:T(8,128)(2,1)S(1)}, u32[]{:S(2)}, u32[]{:S(2)}) %collective-permute-start.12) | collective-permute-done | bytes 32800 | tf_op jit(solution)/shard_map/ppermute | solution.py:38
  41.0 1.2 %collective-permute-done.13 = bf16[128,128]{1,0:T(8,128)(2,1)S(1)} collective-permute-done((bf16[128,128]{1,0:T(8,128)(2,1)S(1)}, bf16[128,128]{1,0:T(8,128)(2,1)S(1)}, u32[]{:S(2)}, u32[]{:S(2)}) %collective-permute-start.13) | collective-permute-done | bytes 32800 | tf_op jit(solution)/shard_map/ppermute | solution.py:43
  42.2 1.3 %collective-permute-start.14 = (bf16[128,128]{1,0:T(8,128)(2,1)S(1)}, bf16[128,128]{1,0:T(8,128)(2,1)S(1)}, u32[]{:S(2)}, u32[]{:S(2)}) collective-permute-start(bf16[128,128]{1,0:T(8,128)(2,1)S(1)} %fusion.8), channel_id=1, source_target_pairs={{0,7},{1,6},{2,5},{3,4},{4,3},{5,2},{6,1},{7,0},{8,15},{9,14},{10,... | collective-permute-start | bytes 98312 | tf_op jit(solution)/shard_map/ppermute | solution.py:43
  43.5 2.6 %collective-permute-start.16 = (bf16[128,128]{1,0:T(8,128)(2,1)S(1)}, bf16[128,128]{1,0:T(8,128)(2,1)S(1)}, u32[]{:S(2)}, u32[]{:S(2)}) collective-permute-start(bf16[128,128]{1,0:T(8,128)(2,1)S(1)} %fusion.8), channel_id=1, source_target_pairs={{0,3},{1,2},{2,1},{3,0},{4,7},{5,6},{6,5},{7,4},{8,11},{9,10},{10,... | collective-permute-start | bytes 98312 | tf_op jit(solution)/shard_map/ppermute | solution.py:43
  46.1 0.6 collective-permute-start.18
  46.7 0.8 collective-permute-done.14
  47.4 1.7 %collective-permute-done.15 = bf16[128,128]{1,0:T(8,128)(2,1)S(1)} collective-permute-done((bf16[128,128]{1,0:T(8,128)(2,1)S(1)}, bf16[128,128]{1,0:T(8,128)(2,1)S(1)}, u32[]{:S(2)}, u32[]{:S(2)}) %collective-permute-start.15) | collective-permute-done | bytes 32800 | tf_op jit(solution)/shard_map/ppermute | solution.py:43
  49.8 3.0 %collective-permute-done.18.beam_ref = f32[4,8192]{1,0:T(4,128)S(1)} collective-permute-done((f32[4,8192]{1,0:T(4,128)S(1)}, f32[4,8192]{1,0:T(4,128)S(1)}, u32[]{:S(2)}, u32[]{:S(2)}) %collective-permute-start.18) | collective-permute-done | bytes 131104 | tf_op jit(solution)/shard_map/ppermute | solution.py:28
  52.8 2.1 %shard_map.79 = (f32[4,8192]{1,0:T(4,128)S(1)}, bf16[128,128]{1,0:T(8,128)(2,1)S(1)}) custom-call(bf16[256,128]{1,0:T(8,128)(2,1)S(1)} %shard_map.77.own_ref, bf16[256,128]{1,0:T(8,128)(2,1)S(1)} %collective-permute-done.17.other_ref, f32[4,8192]{1,0:T(4,128)S(1)} %collective-permute-done.18.beam_ref), custom_call_target="tpu_custom_call" | custom-call | tf_op jit(solution)/shard_map/pallas_call | solution.py:314
  55.1 2.1 %shard_map.78 = (f32[4,8192]{1,0:T(4,128)S(1)}, f32[128,128]{1,0:T(8,128)S(1)}) custom-call(bf16[256,128]{1,0:T(8,128)(2,1)S(1)} %shard_map.77.own_ref, bf16[256,128]{1,0:T(8,128)(2,1)S(1)} %collective-permute-done.17.other_ref, f32[4,8192]{1,0:T(4,128)S(1)} %get-tuple-element.36.beam_ref), custom_call_target="tpu_custom_call" | custom-call | tf_op jit(solution)/shard_map/pallas_call | solution.py:317
  57.2 2.2 %collective-permute-done.19 = bf16[128,128]{1,0:T(8,128)(2,1)S(1)} collective-permute-done((bf16[128,128]{1,0:T(8,128)(2,1)S(1)}, bf16[128,128]{1,0:T(8,128)(2,1)S(1)}, u32[]{:S(2)}, u32[]{:S(2)}) %collective-permute-start.19) | collective-permute-done | bytes 32800 | tf_op jit(solution)/shard_map/ppermute | solution.py:38
  59.5 1.2 %collective-permute-done.20 = bf16[128,128]{1,0:T(8,128)(2,1)S(1)} collective-permute-done((bf16[128,128]{1,0:T(8,128)(2,1)S(1)}, bf16[128,128]{1,0:T(8,128)(2,1)S(1)}, u32[]{:S(2)}, u32[]{:S(2)}) %collective-permute-start.20) | collective-permute-done | bytes 32800 | tf_op jit(solution)/shard_map/ppermute | solution.py:43
  60.7 1.3 %collective-permute-start.21 = (bf16[128,128]{1,0:T(8,128)(2,1)S(1)}, bf16[128,128]{1,0:T(8,128)(2,1)S(1)}, u32[]{:S(2)}, u32[]{:S(2)}) collective-permute-start(bf16[128,128]{1,0:T(8,128)(2,1)S(1)} %fusion.7), channel_id=1, source_target_pairs={{0,7},{1,6},{2,5},{3,4},{4,3},{5,2},{6,1},{7,0},{8,15},{9,14},{10,... | collective-permute-start | bytes 98312 | tf_op jit(solution)/shard_map/ppermute | solution.py:43
  62.0 2.6 %collective-permute-start.23 = (bf16[128,128]{1,0:T(8,128)(2,1)S(1)}, bf16[128,128]{1,0:T(8,128)(2,1)S(1)}, u32[]{:S(2)}, u32[]{:S(2)}) collective-permute-start(bf16[128,128]{1,0:T(8,128)(2,1)S(1)} %fusion.7), channel_id=1, source_target_pairs={{0,3},{1,2},{2,1},{3,0},{4,7},{5,6},{6,5},{7,4},{8,11},{9,10},{10,... | collective-permute-start | bytes 98312 | tf_op jit(solution)/shard_map/ppermute | solution.py:43
  64.6 1.3 %collective-permute-done.21 = bf16[128,128]{1,0:T(8,128)(2,1)S(1)} collective-permute-done((bf16[128,128]{1,0:T(8,128)(2,1)S(1)}, bf16[128,128]{1,0:T(8,128)(2,1)S(1)}, u32[]{:S(2)}, u32[]{:S(2)}) %collective-permute-start.21) | collective-permute-done | bytes 32800 | tf_op jit(solution)/shard_map/ppermute | solution.py:43
  65.9 1.7 %collective-permute-done.22 = bf16[128,128]{1,0:T(8,128)(2,1)S(1)} collective-permute-done((bf16[128,128]{1,0:T(8,128)(2,1)S(1)}, bf16[128,128]{1,0:T(8,128)(2,1)S(1)}, u32[]{:S(2)}, u32[]{:S(2)}) %collective-permute-start.22) | collective-permute-done | bytes 32800 | tf_op jit(solution)/shard_map/ppermute | solution.py:43
  68.3 0.6 collective-permute-start.28
  68.9 1.7 %shard_map.68.slots_ref = s32[64]{0:T(128)S(1)} custom-call(s32[64]{0:T(128)S(1)} %bitcast.5), custom_call_target="tpu_custom_call" | custom-call | tf_op jit(solution)/shard_map/pallas_call | solution.py:305
  70.7 2.0 %shard_map.81 = (f32[32,4,128]{2,1,0:T(4,128)S(1)}, f32[32,4,128]{2,1,0:T(4,128)S(1)}, f32[32,4,128]{2,1,0:T(4,128)S(1)}, f32[32,4,128]{2,1,0:T(4,128)S(1)}) custom-call(s32[64]{0:T(128)S(1)} %shard_map.68.slots_ref, bf16[256,128]{1,0:T(8,128)(2,1)S(1)} %shard_map.80.own_ref, bf16[256,128]{1,0:T(8,128)(2,1)S(1)} %collective-permute-done.24.other_ref, ...), custom_call_target="tpu_custom_call" | custom-call | tf_op jit(solution)/shard_map/pallas_call | solution.py:322
  72.8 2.4 %collective-permute-start.25 = (f32[32,4,128]{2,1,0:T(4,128)S(1)}, f32[32,4,128]{2,1,0:T(4,128)S(1)}, u32[]{:S(2)}, u32[]{:S(2)}) collective-permute-start(f32[32,4,128]{2,1,0:T(4,128)S(1)} %get-tuple-element.42), channel_id=1, source_target_pairs={{0,8},{8,0},{16,24},{24,16},{1,9},{9,1},{17,25},{25,17},{2,10},{10... | collective-permute-start | bytes 196616 | tf_op jit(solution)/shard_map/ppermute | solution.py:333
  75.2 0.5 collective-permute-start.26
  75.7 1.0 %collective-permute-start.27 = (f32[32,4,128]{2,1,0:T(4,128)S(1)}, f32[32,4,128]{2,1,0:T(4,128)S(1)}, u32[]{:S(2)}, u32[]{:S(2)}) collective-permute-start(f32[32,4,128]{2,1,0:T(4,128)S(1)} %get-tuple-element.44), channel_id=1, source_target_pairs={{0,24},{8,16},{16,8},{24,0},{1,25},{9,17},{17,9},{25,1},{2,26},{10... | collective-permute-start | bytes 196616 | tf_op jit(solution)/shard_map/ppermute | solution.py:333
  76.7 2.1 %shard_map.83 = f32[4,8192]{1,0:T(4,128)} custom-call(bf16[256,128]{1,0:T(8,128)(2,1)S(1)} %shard_map.80.own_ref, bf16[256,128]{1,0:T(8,128)(2,1)S(1)} %collective-permute-done.24.other_ref, f32[4,8192]{1,0:T(4,128)S(1)} %collective-permute-done.28.beam_ref), custom_call_target="tpu_custom_call" | custom-call | tf_op jit(solution)/shard_map/pallas_call | solution.py:338
  78.8 1.4 %collective-permute-done.26.refs_2_ = f32[32,4,128]{2,1,0:T(4,128)S(1)} collective-permute-done((f32[32,4,128]{2,1,0:T(4,128)S(1)}, f32[32,4,128]{2,1,0:T(4,128)S(1)}, u32[]{:S(2)}, u32[]{:S(2)}) %collective-permute-start.26) | collective-permute-done | bytes 65568 | tf_op jit(solution)/shard_map/ppermute | solution.py:333
  80.1 0.7 collective-permute-done.27.refs_3_
  80.9 0.7 shard_map.82
  (43 shorter events, 3.5 us)
Async XLA Ops:
  2.9 1.4 %collective-permute-start = (bf16[128,128]{1,0:T(8,128)(2,1)S(1)}, bf16[128,128]{1,0:T(8,128)(2,1)S(1)}, u32[]{:S(2)}, u32[]{:S(2)}) collective-permute-start(bf16[128,128]{1,0:T(8,128)(2,1)S(1)} %get-tuple-element.25), channel_id=1, source_target_pairs={{0,1},{1,0},{2,3},{3,2},{4,5},{5,4},{6,7},{7,6},{8,9},{9,8},{10,11... | collective-permute-start | bytes 98312 | tf_op jit(solution)/shard_map/ppermute | solution.py:43
  4.3 5.1 %copy-start = (f32[128,128]{1,0:T(8,128)S(1)}, f32[128,128]{1,0:T(8,128)}, u32[]{:S(2)}) copy-start(f32[128,128]{1,0:T(8,128)} %smooth_ref.1) | copy-start | bytes 196612
  4.3 5.1 %copy-start.1 = (f32[128,128]{1,0:T(8,128)S(1)}, f32[128,128]{1,0:T(8,128)}, u32[]{:S(2)}) copy-start(f32[128,128]{1,0:T(8,128)} %slope_ref.1) | copy-start | bytes 196612
  4.3 6.6 %collective-permute-start.1 = (bf16[128,128]{1,0:T(8,128)(2,1)S(1)}, bf16[128,128]{1,0:T(8,128)(2,1)S(1)}, u32[]{:S(2)}, u32[]{:S(2)}) collective-permute-start(bf16[128,128]{1,0:T(8,128)(2,1)S(1)} %fusion.6), channel_id=1, source_target_pairs={{0,7},{1,6},{2,5},{3,4},{4,3},{5,2},{6,1},{7,0},{8,15},{9,14},{10,... | collective-permute-start | bytes 98312 | tf_op jit(solution)/shard_map/ppermute | solution.py:43
  9.1 4.8 %collective-permute-start.2 = (bf16[128,128]{1,0:T(8,128)(2,1)S(1)}, bf16[128,128]{1,0:T(8,128)(2,1)S(1)}, u32[]{:S(2)}, u32[]{:S(2)}) collective-permute-start(bf16[128,128]{1,0:T(8,128)(2,1)S(1)} %fusion.6), channel_id=1, source_target_pairs={{0,4},{1,5},{2,6},{3,7},{4,0},{5,1},{6,2},{7,3},{8,12},{9,13},{10,... | collective-permute-start | bytes 98312 | tf_op jit(solution)/shard_map/ppermute | solution.py:43
  9.1 4.8 %collective-permute-start.3 = (bf16[128,128]{1,0:T(8,128)(2,1)S(1)}, bf16[128,128]{1,0:T(8,128)(2,1)S(1)}, u32[]{:S(2)}, u32[]{:S(2)}) collective-permute-start(bf16[128,128]{1,0:T(8,128)(2,1)S(1)} %fusion.6), channel_id=1, source_target_pairs={{0,3},{1,2},{2,1},{3,0},{4,7},{5,6},{6,5},{7,4},{8,11},{9,10},{10,... | collective-permute-start | bytes 98312 | tf_op jit(solution)/shard_map/ppermute | solution.py:43
  14.4 1.3 %collective-permute-start.4 = (bf16[256,128]{1,0:T(8,128)(2,1)S(1)}, bf16[256,128]{1,0:T(8,128)(2,1)S(1)}, u32[]{:S(2)}, u32[]{:S(2)}) collective-permute-start(bf16[256,128]{1,0:T(8,128)(2,1)S(1)} %shard_map.71.own_ref), channel_id=1, source_target_pairs={{0,1},{1,0},{2,3},{3,2},{4,5},{5,4},{6,7},{7,6},{8,9},{9,8},{10,11... | collective-permute-start | bytes 196616 | tf_op jit(solution)/shard_map/ppermute | solution.py:43
  17.9 4.3 %collective-permute-start.5 = (bf16[128,128]{1,0:T(8,128)(2,1)S(1)}, bf16[128,128]{1,0:T(8,128)(2,1)S(1)}, u32[]{:S(2)}, u32[]{:S(2)}) collective-permute-start(bf16[128,128]{1,0:T(8,128)(2,1)S(1)} %get-tuple-element.31), channel_id=1, source_target_pairs={{0,9},{1,8},{2,11},{3,10},{4,13},{5,12},{6,15},{7,14},{8,17},{9,16... | collective-permute-start | bytes 98312 | tf_op jit(solution)/shard_map/ppermute | solution.py:38
  22.2 1.3 %collective-permute-start.6 = (bf16[128,128]{1,0:T(8,128)(2,1)S(1)}, bf16[128,128]{1,0:T(8,128)(2,1)S(1)}, u32[]{:S(2)}, u32[]{:S(2)}) collective-permute-start(bf16[128,128]{1,0:T(8,128)(2,1)S(1)} %fusion.1), channel_id=1, source_target_pairs={{0,1},{1,0},{2,3},{3,2},{4,5},{5,4},{6,7},{7,6},{8,9},{9,8},{10,11... | collective-permute-start | bytes 98312 | tf_op jit(solution)/shard_map/ppermute | solution.py:43
  23.5 5.2 %collective-permute-start.7 = (bf16[128,128]{1,0:T(8,128)(2,1)S(1)}, bf16[128,128]{1,0:T(8,128)(2,1)S(1)}, u32[]{:S(2)}, u32[]{:S(2)}) collective-permute-start(bf16[128,128]{1,0:T(8,128)(2,1)S(1)} %fusion.9), channel_id=1, source_target_pairs={{0,7},{1,6},{2,5},{3,4},{4,3},{5,2},{6,1},{7,0},{8,15},{9,14},{10,... | collective-permute-start | bytes 98312 | tf_op jit(solution)/shard_map/ppermute | solution.py:43
  24.8 5.6 %collective-permute-start.8 = (bf16[128,128]{1,0:T(8,128)(2,1)S(1)}, bf16[128,128]{1,0:T(8,128)(2,1)S(1)}, u32[]{:S(2)}, u32[]{:S(2)}) collective-permute-start(bf16[128,128]{1,0:T(8,128)(2,1)S(1)} %fusion.9), channel_id=1, source_target_pairs={{0,4},{1,5},{2,6},{3,7},{4,0},{5,1},{6,2},{7,3},{8,12},{9,13},{10,... | collective-permute-start | bytes 98312 | tf_op jit(solution)/shard_map/ppermute | solution.py:43
  25.2 5.3 %collective-permute-start.9 = (bf16[128,128]{1,0:T(8,128)(2,1)S(1)}, bf16[128,128]{1,0:T(8,128)(2,1)S(1)}, u32[]{:S(2)}, u32[]{:S(2)}) collective-permute-start(bf16[128,128]{1,0:T(8,128)(2,1)S(1)} %fusion.9), channel_id=1, source_target_pairs={{0,3},{1,2},{2,1},{3,0},{4,7},{5,6},{6,5},{7,4},{8,11},{9,10},{10,... | collective-permute-start | bytes 98312 | tf_op jit(solution)/shard_map/ppermute | solution.py:43
  27.4 6.7 %collective-permute-start.11 = (f32[4,8192]{1,0:T(4,128)S(1)}, f32[4,8192]{1,0:T(4,128)S(1)}, u32[]{:S(2)}, u32[]{:S(2)}) collective-permute-start(f32[4,8192]{1,0:T(4,128)S(1)} %get-tuple-element.34), channel_id=1, source_target_pairs={{0,8},{8,16},{16,24},{24,0},{1,9},{9,17},{17,25},{25,1},{2,10},{10... | collective-permute-start | bytes 393224 | tf_op jit(solution)/shard_map/ppermute | solution.py:28
  31.0 3.2 %collective-permute-start.10 = (bf16[256,128]{1,0:T(8,128)(2,1)S(1)}, bf16[256,128]{1,0:T(8,128)(2,1)S(1)}, u32[]{:S(2)}, u32[]{:S(2)}) collective-permute-start(bf16[256,128]{1,0:T(8,128)(2,1)S(1)} %shard_map.74.own_ref), channel_id=1, source_target_pairs={{0,1},{1,0},{2,3},{3,2},{4,5},{5,4},{6,7},{7,6},{8,9},{9,8},{10,11... | collective-permute-start | bytes 196616 | tf_op jit(solution)/shard_map/ppermute | solution.py:43
  36.3 4.6 %collective-permute-start.12 = (bf16[128,128]{1,0:T(8,128)(2,1)S(1)}, bf16[128,128]{1,0:T(8,128)(2,1)S(1)}, u32[]{:S(2)}, u32[]{:S(2)}) collective-permute-start(bf16[128,128]{1,0:T(8,128)(2,1)S(1)} %get-tuple-element.35), channel_id=1, source_target_pairs={{0,9},{1,8},{2,11},{3,10},{4,13},{5,12},{6,15},{7,14},{8,17},{9,16... | collective-permute-start | bytes 98312 | tf_op jit(solution)/shard_map/ppermute | solution.py:38
  40.9 1.3 %collective-permute-start.13 = (bf16[128,128]{1,0:T(8,128)(2,1)S(1)}, bf16[128,128]{1,0:T(8,128)(2,1)S(1)}, u32[]{:S(2)}, u32[]{:S(2)}) collective-permute-start(bf16[128,128]{1,0:T(8,128)(2,1)S(1)} %fusion.3), channel_id=1, source_target_pairs={{0,1},{1,0},{2,3},{3,2},{4,5},{5,4},{6,7},{7,6},{8,9},{9,8},{10,11... | collective-permute-start | bytes 98312 | tf_op jit(solution)/shard_map/ppermute | solution.py:43
  42.2 5.2 %collective-permute-start.14 = (bf16[128,128]{1,0:T(8,128)(2,1)S(1)}, bf16[128,128]{1,0:T(8,128)(2,1)S(1)}, u32[]{:S(2)}, u32[]{:S(2)}) collective-permute-start(bf16[128,128]{1,0:T(8,128)(2,1)S(1)} %fusion.8), channel_id=1, source_target_pairs={{0,7},{1,6},{2,5},{3,4},{4,3},{5,2},{6,1},{7,0},{8,15},{9,14},{10,... | collective-permute-start | bytes 98312 | tf_op jit(solution)/shard_map/ppermute | solution.py:43
  43.5 5.6 %collective-permute-start.15 = (bf16[128,128]{1,0:T(8,128)(2,1)S(1)}, bf16[128,128]{1,0:T(8,128)(2,1)S(1)}, u32[]{:S(2)}, u32[]{:S(2)}) collective-permute-start(bf16[128,128]{1,0:T(8,128)(2,1)S(1)} %fusion.8), channel_id=1, source_target_pairs={{0,4},{1,5},{2,6},{3,7},{4,0},{5,1},{6,2},{7,3},{8,12},{9,13},{10,... | collective-permute-start | bytes 98312 | tf_op jit(solution)/shard_map/ppermute | solution.py:43
  43.5 5.6 %collective-permute-start.16 = (bf16[128,128]{1,0:T(8,128)(2,1)S(1)}, bf16[128,128]{1,0:T(8,128)(2,1)S(1)}, u32[]{:S(2)}, u32[]{:S(2)}) collective-permute-start(bf16[128,128]{1,0:T(8,128)(2,1)S(1)} %fusion.8), channel_id=1, source_target_pairs={{0,3},{1,2},{2,1},{3,0},{4,7},{5,6},{6,5},{7,4},{8,11},{9,10},{10,... | collective-permute-start | bytes 98312 | tf_op jit(solution)/shard_map/ppermute | solution.py:43
  46.1 6.7 %collective-permute-start.18 = (f32[4,8192]{1,0:T(4,128)S(1)}, f32[4,8192]{1,0:T(4,128)S(1)}, u32[]{:S(2)}, u32[]{:S(2)}) collective-permute-start(f32[4,8192]{1,0:T(4,128)S(1)} %get-tuple-element.38), channel_id=1, source_target_pairs={{0,8},{8,16},{16,24},{24,0},{1,9},{9,17},{17,25},{25,1},{2,10},{10... | collective-permute-start | bytes 393224 | tf_op jit(solution)/shard_map/ppermute | solution.py:28
  49.7 3.2 %collective-permute-start.17 = (bf16[256,128]{1,0:T(8,128)(2,1)S(1)}, bf16[256,128]{1,0:T(8,128)(2,1)S(1)}, u32[]{:S(2)}, u32[]{:S(2)}) collective-permute-start(bf16[256,128]{1,0:T(8,128)(2,1)S(1)} %shard_map.77.own_ref), channel_id=1, source_target_pairs={{0,1},{1,0},{2,3},{3,2},{4,5},{5,4},{6,7},{7,6},{8,9},{9,8},{10,11... | collective-permute-start | bytes 196616 | tf_op jit(solution)/shard_map/ppermute | solution.py:43
  55.0 4.4 %collective-permute-start.19 = (bf16[128,128]{1,0:T(8,128)(2,1)S(1)}, bf16[128,128]{1,0:T(8,128)(2,1)S(1)}, u32[]{:S(2)}, u32[]{:S(2)}) collective-permute-start(bf16[128,128]{1,0:T(8,128)(2,1)S(1)} %get-tuple-element.39), channel_id=1, source_target_pairs={{0,9},{1,8},{2,11},{3,10},{4,13},{5,12},{6,15},{7,14},{8,17},{9,16... | collective-permute-start | bytes 98312 | tf_op jit(solution)/shard_map/ppermute | solution.py:38
  59.4 1.3 %collective-permute-start.20 = (bf16[128,128]{1,0:T(8,128)(2,1)S(1)}, bf16[128,128]{1,0:T(8,128)(2,1)S(1)}, u32[]{:S(2)}, u32[]{:S(2)}) collective-permute-start(bf16[128,128]{1,0:T(8,128)(2,1)S(1)} %fusion.5), channel_id=1, source_target_pairs={{0,1},{1,0},{2,3},{3,2},{4,5},{5,4},{6,7},{7,6},{8,9},{9,8},{10,11... | collective-permute-start | bytes 98312 | tf_op jit(solution)/shard_map/ppermute | solution.py:43
  60.7 5.2 %collective-permute-start.21 = (bf16[128,128]{1,0:T(8,128)(2,1)S(1)}, bf16[128,128]{1,0:T(8,128)(2,1)S(1)}, u32[]{:S(2)}, u32[]{:S(2)}) collective-permute-start(bf16[128,128]{1,0:T(8,128)(2,1)S(1)} %fusion.7), channel_id=1, source_target_pairs={{0,7},{1,6},{2,5},{3,4},{4,3},{5,2},{6,1},{7,0},{8,15},{9,14},{10,... | collective-permute-start | bytes 98312 | tf_op jit(solution)/shard_map/ppermute | solution.py:43
  62.0 5.6 %collective-permute-start.22 = (bf16[128,128]{1,0:T(8,128)(2,1)S(1)}, bf16[128,128]{1,0:T(8,128)(2,1)S(1)}, u32[]{:S(2)}, u32[]{:S(2)}) collective-permute-start(bf16[128,128]{1,0:T(8,128)(2,1)S(1)} %fusion.7), channel_id=1, source_target_pairs={{0,4},{1,5},{2,6},{3,7},{4,0},{5,1},{6,2},{7,3},{8,12},{9,13},{10,... | collective-permute-start | bytes 98312 | tf_op jit(solution)/shard_map/ppermute | solution.py:43
  62.0 5.6 %collective-permute-start.23 = (bf16[128,128]{1,0:T(8,128)(2,1)S(1)}, bf16[128,128]{1,0:T(8,128)(2,1)S(1)}, u32[]{:S(2)}, u32[]{:S(2)}) collective-permute-start(bf16[128,128]{1,0:T(8,128)(2,1)S(1)} %fusion.7), channel_id=1, source_target_pairs={{0,3},{1,2},{2,1},{3,0},{4,7},{5,6},{6,5},{7,4},{8,11},{9,10},{10,... | collective-permute-start | bytes 98312 | tf_op jit(solution)/shard_map/ppermute | solution.py:43
  68.2 2.5 %collective-permute-start.24 = (bf16[256,128]{1,0:T(8,128)(2,1)S(1)}, bf16[256,128]{1,0:T(8,128)(2,1)S(1)}, u32[]{:S(2)}, u32[]{:S(2)}) collective-permute-start(bf16[256,128]{1,0:T(8,128)(2,1)S(1)} %shard_map.80.own_ref), channel_id=1, source_target_pairs={{0,1},{1,0},{2,3},{3,2},{4,5},{5,4},{6,7},{7,6},{8,9},{9,8},{10,11... | collective-permute-start | bytes 196616 | tf_op jit(solution)/shard_map/ppermute | solution.py:43
  68.3 0.7 copy-start.2
  68.3 8.4 %collective-permute-start.28 = (f32[4,8192]{1,0:T(4,128)S(1)}, f32[4,8192]{1,0:T(4,128)S(1)}, u32[]{:S(2)}, u32[]{:S(2)}) collective-permute-start(f32[4,8192]{1,0:T(4,128)S(1)} %get-tuple-element.45), channel_id=1, source_target_pairs={{0,8},{8,16},{16,24},{24,0},{1,9},{9,17},{17,25},{25,1},{2,10},{10... | collective-permute-start | bytes 393224 | tf_op jit(solution)/shard_map/ppermute | solution.py:28
  72.8 6.0 %collective-permute-start.25 = (f32[32,4,128]{2,1,0:T(4,128)S(1)}, f32[32,4,128]{2,1,0:T(4,128)S(1)}, u32[]{:S(2)}, u32[]{:S(2)}) collective-permute-start(f32[32,4,128]{2,1,0:T(4,128)S(1)} %get-tuple-element.42), channel_id=1, source_target_pairs={{0,8},{8,0},{16,24},{24,16},{1,9},{9,1},{17,25},{25,17},{2,10},{10... | collective-permute-start | bytes 196616 | tf_op jit(solution)/shard_map/ppermute | solution.py:333
  75.2 5.0 %collective-permute-start.26 = (f32[32,4,128]{2,1,0:T(4,128)S(1)}, f32[32,4,128]{2,1,0:T(4,128)S(1)}, u32[]{:S(2)}, u32[]{:S(2)}) collective-permute-start(f32[32,4,128]{2,1,0:T(4,128)S(1)} %get-tuple-element.43), channel_id=1, source_target_pairs={{0,16},{8,24},{16,0},{24,8},{1,17},{9,25},{17,1},{25,9},{2,18},{10... | collective-permute-start | bytes 196616 | tf_op jit(solution)/shard_map/ppermute | solution.py:333
  75.7 5.2 %collective-permute-start.27 = (f32[32,4,128]{2,1,0:T(4,128)S(1)}, f32[32,4,128]{2,1,0:T(4,128)S(1)}, u32[]{:S(2)}, u32[]{:S(2)}) collective-permute-start(f32[32,4,128]{2,1,0:T(4,128)S(1)} %get-tuple-element.44), channel_id=1, source_target_pairs={{0,24},{8,16},{16,8},{24,0},{1,25},{9,17},{17,9},{25,1},{2,26},{10... | collective-permute-start | bytes 196616 | tf_op jit(solution)/shard_map/ppermute | solution.py:333

commit v7 on v6

--- a/solution.py
+++ b/solution.py
@@ -44,7 +44,7 @@
 
 
 def across(chip):
-    return 2 * chip + chip % 2
+    return 2 * chip + chip // 2 % 2
 
 
 def summed(kept, sent, axis):
@@ -156,7 +156,7 @@
 
 def keeps():
     index = lax.axis_index("dom")
-    return lax.rem(index + index // 2, 2)
+    return lax.rem(index + index // 4, 2)
 
 
 def share(resident, opposing):
@@ -330,9 +330,7 @@
         ],
     )(place, *pair, resident)
     parts = [
-        lax.ppermute(part, "station", [(source, source ^ distance) for source in range(stations)])
-        if distance
-        else part
+        paired(part, "station", distance) if distance else part
         for distance, part in enumerate(parts)
     ]
     opposing = local(final_kernel, whole)(*pair, opposing)

time: 81.9 us -> 80.7 us (0.985)
  waiting for transfers between devices: 30.6 us -> 27.2 us
  starting transfers between devices: 25.5 us -> 27.9 us
    ppermute x20 -> x23, starting transfers between devices: 18.2 us -> 23.8 us  [paired(): return lax.ppermute(value, axis, pairs)]
    ppermute x3 -> x0, starting transfers between devices: 3.96 us -> none  [shards(): lax.ppermute(part, 'station', [(source, source ^ distance) for source in...]
    ppermute x3 -> x0, waiting for transfers between devices: 2.06 us -> none  [shards(): lax.ppermute(part, 'station', [(source, source ^ distance) for source in...]
    ppermute x20 -> x23, waiting for transfers between devices: 17.3 us -> 16.8 us  [paired(): return lax.ppermute(value, axis, pairs)]
  transfers between devices with their start and end apart: 29 -> 29, of which waited for: 20 -> 21; matrix products, arithmetic and copies ran while one was open for 0% -> 0% of each run, Pallas kernels for 17% -> 17%
where the time goes in v7:
time: 80.7 us; the launch traced here: 80.5 us
  starting transfers between devices  27.9 us (35%)
  waiting for transfers between devices  27.2 us (34%)
  Pallas kernels  24.3 us (30%)
  between operations  1.01 us (1%)
    ppermute x23, starting transfers between devices, paired(): return lax.ppermute(value, axis, pairs)  23.8 us
    ppermute x23, waiting for transfers between devices, paired(): return lax.ppermute(value, axis, pairs)  16.8 us
    pallas_call x3, Pallas kernels, shards(): local(functools.partial(beam_kernel, 0), (whole, rounded))(*pair, opposing)  6.44 us
    pallas_call x3, Pallas kernels, shards(): local(functools.partial(beam_kernel, 1), (whole, density))(*pair, resident)  6.43 us
    ppermute x3, waiting for transfers between devices, shifted(): return lax.ppermute(value, axis, pairs)  5.58 us
    ppermute x3, waiting for transfers between devices, crossed(): return lax.ppermute(value, ('station', 'dom'), pairs)  4.81 us
    ppermute x3, starting transfers between devices, shifted(): return lax.ppermute(value, axis, pairs)  2.37 us
    pallas_call x1, Pallas kernels, shards(): local(first_kernel, (whole, whole, density, rounded), in_specs=[pl.BlockS...  2.27 us
  transfers between devices with their start and end apart: 29, of which 21 were waited for; matrix products, arithmetic and copies ran while one was open for 0% of the time, Pallas kernels for 17%

profile of v7, /device:TPU:0, one launch (start us, length us, event | category | flops | bytes accessed | tf_op | source)
XLA Modules:
  0.0 80.5 jit_solution(14945490164322131948)
XLA Ops:
  0.6 2.3 %shard_map.69 = (f32[4,8192]{1,0:T(4,128)S(1)}, f32[4,8192]{1,0:T(4,128)S(1)}, f32[128,128]{1,0:T(8,128)S(1)}, bf16[128,128]{1,0:T(8,128)(2,1)S(1)}) custom-call(f32[4,8192]{1,0:T(4,128)} %bitcast.8, f32[4,8192]{1,0:T(4,128)} %bitcast.9), custom_call_target="tpu_custom_call" | custom-call | tf_op jit(solution)/shard_map/pallas_call | solution.py:290
  2.9 0.6 collective-permute-start
  3.5 0.9 %collective-permute-done = bf16[128,128]{1,0:T(8,128)(2,1)S(1)} collective-permute-done((bf16[128,128]{1,0:T(8,128)(2,1)S(1)}, bf16[128,128]{1,0:T(8,128)(2,1)S(1)}, u32[]{:S(2)}, u32[]{:S(2)}) %collective-permute-start) | collective-permute-done | bytes 32800 | tf_op jit(solution)/shard_map/ppermute | solution.py:43
  4.3 4.8 %collective-permute-start.1 = (bf16[128,128]{1,0:T(8,128)(2,1)S(1)}, bf16[128,128]{1,0:T(8,128)(2,1)S(1)}, u32[]{:S(2)}, u32[]{:S(2)}) collective-permute-start(bf16[128,128]{1,0:T(8,128)(2,1)S(1)} %fusion.6), channel_id=1, source_target_pairs={{0,7},{1,6},{2,5},{3,4},{4,3},{5,2},{6,1},{7,0},{8,15},{9,14},{10,... | collective-permute-start | bytes 98312 | tf_op jit(solution)/shard_map/ppermute | solution.py:43
  9.1 0.6 collective-permute-start.3
  9.7 0.7 shard_map.70
  10.9 2.5 %collective-permute-done.2 = bf16[128,128]{1,0:T(8,128)(2,1)S(1)} collective-permute-done((bf16[128,128]{1,0:T(8,128)(2,1)S(1)}, bf16[128,128]{1,0:T(8,128)(2,1)S(1)}, u32[]{:S(2)}, u32[]{:S(2)}) %collective-permute-start.2) | collective-permute-done | bytes 32800 | tf_op jit(solution)/shard_map/ppermute | solution.py:43
  13.4 0.5 shard_map.71.own_ref
  14.3 0.9 %collective-permute-done.4.other_ref = bf16[256,128]{1,0:T(8,128)(2,1)S(1)} collective-permute-done((bf16[256,128]{1,0:T(8,128)(2,1)S(1)}, bf16[256,128]{1,0:T(8,128)(2,1)S(1)}, u32[]{:S(2)}, u32[]{:S(2)}) %collective-permute-start.4) | collective-permute-done | bytes 65568 | tf_op jit(solution)/shard_map/ppermute | solution.py:43
  15.2 2.1 %shard_map.73 = (f32[4,8192]{1,0:T(4,128)S(1)}, bf16[128,128]{1,0:T(8,128)(2,1)S(1)}) custom-call(bf16[256,128]{1,0:T(8,128)(2,1)S(1)} %shard_map.71.own_ref, bf16[256,128]{1,0:T(8,128)(2,1)S(1)} %collective-permute-done.4.other_ref, f32[4,8192]{1,0:T(4,128)S(1)} %get-tuple-element.30.beam_ref), custom_call_target="tpu_custom_call" | custom-call | tf_op jit(solution)/shard_map/pallas_call | solution.py:314
  17.3 1.5 %collective-permute-start.5 = (bf16[128,128]{1,0:T(8,128)(2,1)S(1)}, bf16[128,128]{1,0:T(8,128)(2,1)S(1)}, u32[]{:S(2)}, u32[]{:S(2)}) collective-permute-start(bf16[128,128]{1,0:T(8,128)(2,1)S(1)} %get-tuple-element.31), channel_id=1, source_target_pairs={{0,9},{1,8},{2,11},{3,10},{4,13},{5,12},{6,15},{7,14},{8,17},{9,16... | collective-permute-start | bytes 98312 | tf_op jit(solution)/shard_map/ppermute | solution.py:38
  18.8 2.1 %shard_map.72 = (f32[4,8192]{1,0:T(4,128)S(1)}, f32[128,128]{1,0:T(8,128)S(1)}) custom-call(bf16[256,128]{1,0:T(8,128)(2,1)S(1)} %shard_map.71.own_ref, bf16[256,128]{1,0:T(8,128)(2,1)S(1)} %collective-permute-done.4.other_ref, f32[4,8192]{1,0:T(4,128)S(1)} %get-tuple-element.28.beam_ref), custom_call_target="tpu_custom_call" | custom-call | tf_op jit(solution)/shard_map/pallas_call | solution.py:317
  21.0 0.7 collective-permute-done.5
  22.0 0.9 %collective-permute-done.6 = bf16[128,128]{1,0:T(8,128)(2,1)S(1)} collective-permute-done((bf16[128,128]{1,0:T(8,128)(2,1)S(1)}, bf16[128,128]{1,0:T(8,128)(2,1)S(1)}, u32[]{:S(2)}, u32[]{:S(2)}) %collective-permute-start.6) | collective-permute-done | bytes 32800 | tf_op jit(solution)/shard_map/ppermute | solution.py:43
  22.9 2.0 %collective-permute-start.7 = (bf16[128,128]{1,0:T(8,128)(2,1)S(1)}, bf16[128,128]{1,0:T(8,128)(2,1)S(1)}, u32[]{:S(2)}, u32[]{:S(2)}) collective-permute-start(bf16[128,128]{1,0:T(8,128)(2,1)S(1)} %fusion.9), channel_id=1, source_target_pairs={{0,7},{1,6},{2,5},{3,4},{4,3},{5,2},{6,1},{7,0},{8,15},{9,14},{10,... | collective-permute-start | bytes 98312 | tf_op jit(solution)/shard_map/ppermute | solution.py:43
  25.4 1.7 %collective-permute-start.9 = (bf16[128,128]{1,0:T(8,128)(2,1)S(1)}, bf16[128,128]{1,0:T(8,128)(2,1)S(1)}, u32[]{:S(2)}, u32[]{:S(2)}) collective-permute-start(bf16[128,128]{1,0:T(8,128)(2,1)S(1)} %fusion.9), channel_id=1, source_target_pairs={{0,2},{1,3},{2,0},{3,1},{4,6},{5,7},{6,4},{7,5},{8,10},{9,11},{10,... | collective-permute-start | bytes 98312 | tf_op jit(solution)/shard_map/ppermute | solution.py:43
  27.1 0.8 %collective-permute-start.11 = (f32[4,8192]{1,0:T(4,128)S(1)}, f32[4,8192]{1,0:T(4,128)S(1)}, u32[]{:S(2)}, u32[]{:S(2)}) collective-permute-start(f32[4,8192]{1,0:T(4,128)S(1)} %get-tuple-element.34), channel_id=1, source_target_pairs={{0,8},{8,16},{16,24},{24,0},{1,9},{9,17},{17,25},{25,1},{2,10},{10... | collective-permute-start | bytes 393224 | tf_op jit(solution)/shard_map/ppermute | solution.py:28
  28.1 1.0 %collective-permute-done.8 = bf16[128,128]{1,0:T(8,128)(2,1)S(1)} collective-permute-done((bf16[128,128]{1,0:T(8,128)(2,1)S(1)}, bf16[128,128]{1,0:T(8,128)(2,1)S(1)}, u32[]{:S(2)}, u32[]{:S(2)}) %collective-permute-start.8) | collective-permute-done | bytes 32800 | tf_op jit(solution)/shard_map/ppermute | solution.py:43
  29.2 0.7 collective-permute-done.9
  29.9 0.5 shard_map.74.own_ref
  30.6 2.8 %collective-permute-done.11.beam_ref = f32[4,8192]{1,0:T(4,128)S(1)} collective-permute-done((f32[4,8192]{1,0:T(4,128)S(1)}, f32[4,8192]{1,0:T(4,128)S(1)}, u32[]{:S(2)}, u32[]{:S(2)}) %collective-permute-start.11) | collective-permute-done | bytes 131104 | tf_op jit(solution)/shard_map/ppermute | solution.py:28
  33.5 2.1 %shard_map.76 = (f32[4,8192]{1,0:T(4,128)S(1)}, bf16[128,128]{1,0:T(8,128)(2,1)S(1)}) custom-call(bf16[256,128]{1,0:T(8,128)(2,1)S(1)} %shard_map.74.own_ref, bf16[256,128]{1,0:T(8,128)(2,1)S(1)} %collective-permute-done.10.other_ref, f32[4,8192]{1,0:T(4,128)S(1)} %collective-permute-done.11.beam_ref), custom_call_target="tpu_custom_call" | custom-call | tf_op jit(solution)/shard_map/pallas_call | solution.py:314
  35.9 2.1 %shard_map.75 = (f32[4,8192]{1,0:T(4,128)S(1)}, f32[128,128]{1,0:T(8,128)S(1)}) custom-call(bf16[256,128]{1,0:T(8,128)(2,1)S(1)} %shard_map.74.own_ref, bf16[256,128]{1,0:T(8,128)(2,1)S(1)} %collective-permute-done.10.other_ref, f32[4,8192]{1,0:T(4,128)S(1)} %get-tuple-element.32.beam_ref), custom_call_target="tpu_custom_call" | custom-call | tf_op jit(solution)/shard_map/pallas_call | solution.py:317
  38.0 2.1 %collective-permute-done.12 = bf16[128,128]{1,0:T(8,128)(2,1)S(1)} collective-permute-done((bf16[128,128]{1,0:T(8,128)(2,1)S(1)}, bf16[128,128]{1,0:T(8,128)(2,1)S(1)}, u32[]{:S(2)}, u32[]{:S(2)}) %collective-permute-start.12) | collective-permute-done | bytes 32800 | tf_op jit(solution)/shard_map/ppermute | solution.py:38
  40.2 1.2 %collective-permute-done.13 = bf16[128,128]{1,0:T(8,128)(2,1)S(1)} collective-permute-done((bf16[128,128]{1,0:T(8,128)(2,1)S(1)}, bf16[128,128]{1,0:T(8,128)(2,1)S(1)}, u32[]{:S(2)}, u32[]{:S(2)}) %collective-permute-start.13) | collective-permute-done | bytes 32800 | tf_op jit(solution)/shard_map/ppermute | solution.py:43
  41.4 1.8 %collective-permute-start.14 = (bf16[128,128]{1,0:T(8,128)(2,1)S(1)}, bf16[128,128]{1,0:T(8,128)(2,1)S(1)}, u32[]{:S(2)}, u32[]{:S(2)}) collective-permute-start(bf16[128,128]{1,0:T(8,128)(2,1)S(1)} %fusion.8), channel_id=1, source_target_pairs={{0,7},{1,6},{2,5},{3,4},{4,3},{5,2},{6,1},{7,0},{8,15},{9,14},{10,... | collective-permute-start | bytes 98312 | tf_op jit(solution)/shard_map/ppermute | solution.py:43
  43.2 2.3 %collective-permute-start.16 = (bf16[128,128]{1,0:T(8,128)(2,1)S(1)}, bf16[128,128]{1,0:T(8,128)(2,1)S(1)}, u32[]{:S(2)}, u32[]{:S(2)}) collective-permute-start(bf16[128,128]{1,0:T(8,128)(2,1)S(1)} %fusion.8), channel_id=1, source_target_pairs={{0,2},{1,3},{2,0},{3,1},{4,6},{5,7},{6,4},{7,5},{8,10},{9,11},{10,... | collective-permute-start | bytes 98312 | tf_op jit(solution)/shard_map/ppermute | solution.py:43
  45.6 0.7 collective-permute-start.18
  46.6 1.7 %collective-permute-done.15 = bf16[128,128]{1,0:T(8,128)(2,1)S(1)} collective-permute-done((bf16[128,128]{1,0:T(8,128)(2,1)S(1)}, bf16[128,128]{1,0:T(8,128)(2,1)S(1)}, u32[]{:S(2)}, u32[]{:S(2)}) %collective-permute-start.15) | collective-permute-done | bytes 32800 | tf_op jit(solution)/shard_map/ppermute | solution.py:43
  49.0 2.8 %collective-permute-done.18.beam_ref = f32[4,8192]{1,0:T(4,128)S(1)} collective-permute-done((f32[4,8192]{1,0:T(4,128)S(1)}, f32[4,8192]{1,0:T(4,128)S(1)}, u32[]{:S(2)}, u32[]{:S(2)}) %collective-permute-start.18) | collective-permute-done | bytes 131104 | tf_op jit(solution)/shard_map/ppermute | solution.py:28
  51.8 2.1 %shard_map.79 = (f32[4,8192]{1,0:T(4,128)S(1)}, bf16[128,128]{1,0:T(8,128)(2,1)S(1)}) custom-call(bf16[256,128]{1,0:T(8,128)(2,1)S(1)} %shard_map.77.own_ref, bf16[256,128]{1,0:T(8,128)(2,1)S(1)} %collective-permute-done.17.other_ref, f32[4,8192]{1,0:T(4,128)S(1)} %collective-permute-done.18.beam_ref), custom_call_target="tpu_custom_call" | custom-call | tf_op jit(solution)/shard_map/pallas_call | solution.py:314
  54.0 2.1 %shard_map.78 = (f32[4,8192]{1,0:T(4,128)S(1)}, f32[128,128]{1,0:T(8,128)S(1)}) custom-call(bf16[256,128]{1,0:T(8,128)(2,1)S(1)} %shard_map.77.own_ref, bf16[256,128]{1,0:T(8,128)(2,1)S(1)} %collective-permute-done.17.other_ref, f32[4,8192]{1,0:T(4,128)S(1)} %get-tuple-element.36.beam_ref), custom_call_target="tpu_custom_call" | custom-call | tf_op jit(solution)/shard_map/pallas_call | solution.py:317
  56.1 2.1 %collective-permute-done.19 = bf16[128,128]{1,0:T(8,128)(2,1)S(1)} collective-permute-done((bf16[128,128]{1,0:T(8,128)(2,1)S(1)}, bf16[128,128]{1,0:T(8,128)(2,1)S(1)}, u32[]{:S(2)}, u32[]{:S(2)}) %collective-permute-start.19) | collective-permute-done | bytes 32800 | tf_op jit(solution)/shard_map/ppermute | solution.py:38
  58.3 1.2 %collective-permute-done.20 = bf16[128,128]{1,0:T(8,128)(2,1)S(1)} collective-permute-done((bf16[128,128]{1,0:T(8,128)(2,1)S(1)}, bf16[128,128]{1,0:T(8,128)(2,1)S(1)}, u32[]{:S(2)}, u32[]{:S(2)}) %collective-permute-start.20) | collective-permute-done | bytes 32800 | tf_op jit(solution)/shard_map/ppermute | solution.py:43
  59.5 1.8 %collective-permute-start.21 = (bf16[128,128]{1,0:T(8,128)(2,1)S(1)}, bf16[128,128]{1,0:T(8,128)(2,1)S(1)}, u32[]{:S(2)}, u32[]{:S(2)}) collective-permute-start(bf16[128,128]{1,0:T(8,128)(2,1)S(1)} %fusion.7), channel_id=1, source_target_pairs={{0,7},{1,6},{2,5},{3,4},{4,3},{5,2},{6,1},{7,0},{8,15},{9,14},{10,... | collective-permute-start | bytes 98312 | tf_op jit(solution)/shard_map/ppermute | solution.py:43
  61.4 2.3 %collective-permute-start.23 = (bf16[128,128]{1,0:T(8,128)(2,1)S(1)}, bf16[128,128]{1,0:T(8,128)(2,1)S(1)}, u32[]{:S(2)}, u32[]{:S(2)}) collective-permute-start(bf16[128,128]{1,0:T(8,128)(2,1)S(1)} %fusion.7), channel_id=1, source_target_pairs={{0,2},{1,3},{2,0},{3,1},{4,6},{5,7},{6,4},{7,5},{8,10},{9,11},{10,... | collective-permute-start | bytes 98312 | tf_op jit(solution)/shard_map/ppermute | solution.py:43
  63.7 1.0 %collective-permute-done.21 = bf16[128,128]{1,0:T(8,128)(2,1)S(1)} collective-permute-done((bf16[128,128]{1,0:T(8,128)(2,1)S(1)}, bf16[128,128]{1,0:T(8,128)(2,1)S(1)}, u32[]{:S(2)}, u32[]{:S(2)}) %collective-permute-start.21) | collective-permute-done | bytes 32800 | tf_op jit(solution)/shard_map/ppermute | solution.py:43
  64.7 1.7 %collective-permute-done.22 = bf16[128,128]{1,0:T(8,128)(2,1)S(1)} collective-permute-done((bf16[128,128]{1,0:T(8,128)(2,1)S(1)}, bf16[128,128]{1,0:T(8,128)(2,1)S(1)}, u32[]{:S(2)}, u32[]{:S(2)}) %collective-permute-start.22) | collective-permute-done | bytes 32800 | tf_op jit(solution)/shard_map/ppermute | solution.py:43
  67.1 0.9 %collective-permute-start.28 = (f32[4,8192]{1,0:T(4,128)S(1)}, f32[4,8192]{1,0:T(4,128)S(1)}, u32[]{:S(2)}, u32[]{:S(2)}) collective-permute-start(f32[4,8192]{1,0:T(4,128)S(1)} %get-tuple-element.45), channel_id=1, source_target_pairs={{0,8},{8,16},{16,24},{24,0},{1,9},{9,17},{17,25},{25,1},{2,10},{10... | collective-permute-start | bytes 393224 | tf_op jit(solution)/shard_map/ppermute | solution.py:28
  68.0 1.7 %shard_map.68.slots_ref = s32[64]{0:T(128)S(1)} custom-call(s32[64]{0:T(128)S(1)} %bitcast.5), custom_call_target="tpu_custom_call" | custom-call | tf_op jit(solution)/shard_map/pallas_call | solution.py:305
  69.7 2.0 %shard_map.81 = (f32[32,4,128]{2,1,0:T(4,128)S(1)}, f32[32,4,128]{2,1,0:T(4,128)S(1)}, f32[32,4,128]{2,1,0:T(4,128)S(1)}, f32[32,4,128]{2,1,0:T(4,128)S(1)}) custom-call(s32[64]{0:T(128)S(1)} %shard_map.68.slots_ref, bf16[256,128]{1,0:T(8,128)(2,1)S(1)} %shard_map.80.own_ref, bf16[256,128]{1,0:T(8,128)(2,1)S(1)} %collective-permute-done.24.other_ref, ...), custom_call_target="tpu_custom_call" | custom-call | tf_op jit(solution)/shard_map/pallas_call | solution.py:322
  71.8 2.2 %collective-permute-start.25 = (f32[32,4,128]{2,1,0:T(4,128)S(1)}, f32[32,4,128]{2,1,0:T(4,128)S(1)}, u32[]{:S(2)}, u32[]{:S(2)}) collective-permute-start(f32[32,4,128]{2,1,0:T(4,128)S(1)} %get-tuple-element.42), channel_id=1, source_target_pairs={{0,8},{8,0},{16,24},{24,16},{1,9},{9,1},{17,25},{25,17},{2,10},{10... | collective-permute-start | bytes 196616 | tf_op jit(solution)/shard_map/ppermute | solution.py:43
  74.0 0.5 collective-permute-start.26
  74.5 1.0 %collective-permute-start.27 = (f32[32,4,128]{2,1,0:T(4,128)S(1)}, f32[32,4,128]{2,1,0:T(4,128)S(1)}, u32[]{:S(2)}, u32[]{:S(2)}) collective-permute-start(f32[32,4,128]{2,1,0:T(4,128)S(1)} %get-tuple-element.44), channel_id=1, source_target_pairs={{0,24},{8,16},{16,8},{24,0},{1,25},{9,17},{17,9},{25,1},{2,26},{10... | collective-permute-start | bytes 196616 | tf_op jit(solution)/shard_map/ppermute | solution.py:43
  75.5 2.1 %shard_map.83 = f32[4,8192]{1,0:T(4,128)} custom-call(bf16[256,128]{1,0:T(8,128)(2,1)S(1)} %shard_map.80.own_ref, bf16[256,128]{1,0:T(8,128)(2,1)S(1)} %collective-permute-done.24.other_ref, f32[4,8192]{1,0:T(4,128)S(1)} %collective-permute-done.28.beam_ref), custom_call_target="tpu_custom_call" | custom-call | tf_op jit(solution)/shard_map/pallas_call | solution.py:336
  77.6 1.3 %collective-permute-done.26.refs_2_ = f32[32,4,128]{2,1,0:T(4,128)S(1)} collective-permute-done((f32[32,4,128]{2,1,0:T(4,128)S(1)}, f32[32,4,128]{2,1,0:T(4,128)S(1)}, u32[]{:S(2)}, u32[]{:S(2)}) %collective-permute-start.26) | collective-permute-done | bytes 65568 | tf_op jit(solution)/shard_map/ppermute | solution.py:43
  78.9 0.7 collective-permute-done.27.refs_3_
  79.6 0.7 shard_map.82
  (43 shorter events, 4.4 us)
Async XLA Ops:
  2.9 1.4 %collective-permute-start = (bf16[128,128]{1,0:T(8,128)(2,1)S(1)}, bf16[128,128]{1,0:T(8,128)(2,1)S(1)}, u32[]{:S(2)}, u32[]{:S(2)}) collective-permute-start(bf16[128,128]{1,0:T(8,128)(2,1)S(1)} %get-tuple-element.25), channel_id=1, source_target_pairs={{0,1},{1,0},{2,3},{3,2},{4,5},{5,4},{6,7},{7,6},{8,9},{9,8},{10,11... | collective-permute-start | bytes 98312 | tf_op jit(solution)/shard_map/ppermute | solution.py:43
  4.3 5.4 %copy-start = (f32[128,128]{1,0:T(8,128)S(1)}, f32[128,128]{1,0:T(8,128)}, u32[]{:S(2)}) copy-start(f32[128,128]{1,0:T(8,128)} %smooth_ref.1) | copy-start | bytes 196612
  4.3 5.4 %copy-start.1 = (f32[128,128]{1,0:T(8,128)S(1)}, f32[128,128]{1,0:T(8,128)}, u32[]{:S(2)}) copy-start(f32[128,128]{1,0:T(8,128)} %slope_ref.1) | copy-start | bytes 196612
  4.3 6.5 %collective-permute-start.1 = (bf16[128,128]{1,0:T(8,128)(2,1)S(1)}, bf16[128,128]{1,0:T(8,128)(2,1)S(1)}, u32[]{:S(2)}, u32[]{:S(2)}) collective-permute-start(bf16[128,128]{1,0:T(8,128)(2,1)S(1)} %fusion.6), channel_id=1, source_target_pairs={{0,7},{1,6},{2,5},{3,4},{4,3},{5,2},{6,1},{7,0},{8,15},{9,14},{10,... | collective-permute-start | bytes 98312 | tf_op jit(solution)/shard_map/ppermute | solution.py:43
  9.1 4.3 %collective-permute-start.2 = (bf16[128,128]{1,0:T(8,128)(2,1)S(1)}, bf16[128,128]{1,0:T(8,128)(2,1)S(1)}, u32[]{:S(2)}, u32[]{:S(2)}) collective-permute-start(bf16[128,128]{1,0:T(8,128)(2,1)S(1)} %fusion.6), channel_id=1, source_target_pairs={{0,5},{1,4},{2,7},{3,6},{4,1},{5,0},{6,3},{7,2},{8,13},{9,12},{10,... | collective-permute-start | bytes 98312 | tf_op jit(solution)/shard_map/ppermute | solution.py:43
  9.1 4.3 %collective-permute-start.3 = (bf16[128,128]{1,0:T(8,128)(2,1)S(1)}, bf16[128,128]{1,0:T(8,128)(2,1)S(1)}, u32[]{:S(2)}, u32[]{:S(2)}) collective-permute-start(bf16[128,128]{1,0:T(8,128)(2,1)S(1)} %fusion.6), channel_id=1, source_target_pairs={{0,2},{1,3},{2,0},{3,1},{4,6},{5,7},{6,4},{7,5},{8,10},{9,11},{10,... | collective-permute-start | bytes 98312 | tf_op jit(solution)/shard_map/ppermute | solution.py:43
  13.9 1.3 %collective-permute-start.4 = (bf16[256,128]{1,0:T(8,128)(2,1)S(1)}, bf16[256,128]{1,0:T(8,128)(2,1)S(1)}, u32[]{:S(2)}, u32[]{:S(2)}) collective-permute-start(bf16[256,128]{1,0:T(8,128)(2,1)S(1)} %shard_map.71.own_ref), channel_id=1, source_target_pairs={{0,1},{1,0},{2,3},{3,2},{4,5},{5,4},{6,7},{7,6},{8,9},{9,8},{10,11... | collective-permute-start | bytes 196616 | tf_op jit(solution)/shard_map/ppermute | solution.py:43
  17.3 4.3 %collective-permute-start.5 = (bf16[128,128]{1,0:T(8,128)(2,1)S(1)}, bf16[128,128]{1,0:T(8,128)(2,1)S(1)}, u32[]{:S(2)}, u32[]{:S(2)}) collective-permute-start(bf16[128,128]{1,0:T(8,128)(2,1)S(1)} %get-tuple-element.31), channel_id=1, source_target_pairs={{0,9},{1,8},{2,11},{3,10},{4,13},{5,12},{6,15},{7,14},{8,17},{9,16... | collective-permute-start | bytes 98312 | tf_op jit(solution)/shard_map/ppermute | solution.py:38
  21.7 1.3 %collective-permute-start.6 = (bf16[128,128]{1,0:T(8,128)(2,1)S(1)}, bf16[128,128]{1,0:T(8,128)(2,1)S(1)}, u32[]{:S(2)}, u32[]{:S(2)}) collective-permute-start(bf16[128,128]{1,0:T(8,128)(2,1)S(1)} %fusion.1), channel_id=1, source_target_pairs={{0,1},{1,0},{2,3},{3,2},{4,5},{5,4},{6,7},{7,6},{8,9},{9,8},{10,11... | collective-permute-start | bytes 98312 | tf_op jit(solution)/shard_map/ppermute | solution.py:43
  22.9 5.2 %collective-permute-start.7 = (bf16[128,128]{1,0:T(8,128)(2,1)S(1)}, bf16[128,128]{1,0:T(8,128)(2,1)S(1)}, u32[]{:S(2)}, u32[]{:S(2)}) collective-permute-start(bf16[128,128]{1,0:T(8,128)(2,1)S(1)} %fusion.9), channel_id=1, source_target_pairs={{0,7},{1,6},{2,5},{3,4},{4,3},{5,2},{6,1},{7,0},{8,15},{9,14},{10,... | collective-permute-start | bytes 98312 | tf_op jit(solution)/shard_map/ppermute | solution.py:43
  24.9 4.2 %collective-permute-start.8 = (bf16[128,128]{1,0:T(8,128)(2,1)S(1)}, bf16[128,128]{1,0:T(8,128)(2,1)S(1)}, u32[]{:S(2)}, u32[]{:S(2)}) collective-permute-start(bf16[128,128]{1,0:T(8,128)(2,1)S(1)} %fusion.9), channel_id=1, source_target_pairs={{0,5},{1,4},{2,7},{3,6},{4,1},{5,0},{6,3},{7,2},{8,13},{9,12},{10,... | collective-permute-start | bytes 98312 | tf_op jit(solution)/shard_map/ppermute | solution.py:43
  25.4 4.5 %collective-permute-start.9 = (bf16[128,128]{1,0:T(8,128)(2,1)S(1)}, bf16[128,128]{1,0:T(8,128)(2,1)S(1)}, u32[]{:S(2)}, u32[]{:S(2)}) collective-permute-start(bf16[128,128]{1,0:T(8,128)(2,1)S(1)} %fusion.9), channel_id=1, source_target_pairs={{0,2},{1,3},{2,0},{3,1},{4,6},{5,7},{6,4},{7,5},{8,10},{9,11},{10,... | collective-permute-start | bytes 98312 | tf_op jit(solution)/shard_map/ppermute | solution.py:43
  27.1 6.3 %collective-permute-start.11 = (f32[4,8192]{1,0:T(4,128)S(1)}, f32[4,8192]{1,0:T(4,128)S(1)}, u32[]{:S(2)}, u32[]{:S(2)}) collective-permute-start(f32[4,8192]{1,0:T(4,128)S(1)} %get-tuple-element.34), channel_id=1, source_target_pairs={{0,8},{8,16},{16,24},{24,0},{1,9},{9,17},{17,25},{25,1},{2,10},{10... | collective-permute-start | bytes 393224 | tf_op jit(solution)/shard_map/ppermute | solution.py:28
  30.4 3.1 %collective-permute-start.10 = (bf16[256,128]{1,0:T(8,128)(2,1)S(1)}, bf16[256,128]{1,0:T(8,128)(2,1)S(1)}, u32[]{:S(2)}, u32[]{:S(2)}) collective-permute-start(bf16[256,128]{1,0:T(8,128)(2,1)S(1)} %shard_map.74.own_ref), channel_id=1, source_target_pairs={{0,1},{1,0},{2,3},{3,2},{4,5},{5,4},{6,7},{7,6},{8,9},{9,8},{10,11... | collective-permute-start | bytes 196616 | tf_op jit(solution)/shard_map/ppermute | solution.py:43
  35.6 4.5 %collective-permute-start.12 = (bf16[128,128]{1,0:T(8,128)(2,1)S(1)}, bf16[128,128]{1,0:T(8,128)(2,1)S(1)}, u32[]{:S(2)}, u32[]{:S(2)}) collective-permute-start(bf16[128,128]{1,0:T(8,128)(2,1)S(1)} %get-tuple-element.35), channel_id=1, source_target_pairs={{0,9},{1,8},{2,11},{3,10},{4,13},{5,12},{6,15},{7,14},{8,17},{9,16... | collective-permute-start | bytes 98312 | tf_op jit(solution)/shard_map/ppermute | solution.py:38
  40.1 1.3 %collective-permute-start.13 = (bf16[128,128]{1,0:T(8,128)(2,1)S(1)}, bf16[128,128]{1,0:T(8,128)(2,1)S(1)}, u32[]{:S(2)}, u32[]{:S(2)}) collective-permute-start(bf16[128,128]{1,0:T(8,128)(2,1)S(1)} %fusion.3), channel_id=1, source_target_pairs={{0,1},{1,0},{2,3},{3,2},{4,5},{5,4},{6,7},{7,6},{8,9},{9,8},{10,11... | collective-permute-start | bytes 98312 | tf_op jit(solution)/shard_map/ppermute | solution.py:43
  41.4 5.2 %collective-permute-start.14 = (bf16[128,128]{1,0:T(8,128)(2,1)S(1)}, bf16[128,128]{1,0:T(8,128)(2,1)S(1)}, u32[]{:S(2)}, u32[]{:S(2)}) collective-permute-start(bf16[128,128]{1,0:T(8,128)(2,1)S(1)} %fusion.8), channel_id=1, source_target_pairs={{0,7},{1,6},{2,5},{3,4},{4,3},{5,2},{6,1},{7,0},{8,15},{9,14},{10,... | collective-permute-start | bytes 98312 | tf_op jit(solution)/shard_map/ppermute | solution.py:43
  43.2 5.1 %collective-permute-start.15 = (bf16[128,128]{1,0:T(8,128)(2,1)S(1)}, bf16[128,128]{1,0:T(8,128)(2,1)S(1)}, u32[]{:S(2)}, u32[]{:S(2)}) collective-permute-start(bf16[128,128]{1,0:T(8,128)(2,1)S(1)} %fusion.8), channel_id=1, source_target_pairs={{0,5},{1,4},{2,7},{3,6},{4,1},{5,0},{6,3},{7,2},{8,13},{9,12},{10,... | collective-permute-start | bytes 98312 | tf_op jit(solution)/shard_map/ppermute | solution.py:43
  43.2 5.1 %collective-permute-start.16 = (bf16[128,128]{1,0:T(8,128)(2,1)S(1)}, bf16[128,128]{1,0:T(8,128)(2,1)S(1)}, u32[]{:S(2)}, u32[]{:S(2)}) collective-permute-start(bf16[128,128]{1,0:T(8,128)(2,1)S(1)} %fusion.8), channel_id=1, source_target_pairs={{0,2},{1,3},{2,0},{3,1},{4,6},{5,7},{6,4},{7,5},{8,10},{9,11},{10,... | collective-permute-start | bytes 98312 | tf_op jit(solution)/shard_map/ppermute | solution.py:43
  45.6 6.2 %collective-permute-start.18 = (f32[4,8192]{1,0:T(4,128)S(1)}, f32[4,8192]{1,0:T(4,128)S(1)}, u32[]{:S(2)}, u32[]{:S(2)}) collective-permute-start(f32[4,8192]{1,0:T(4,128)S(1)} %get-tuple-element.38), channel_id=1, source_target_pairs={{0,8},{8,16},{16,24},{24,0},{1,9},{9,17},{17,25},{25,1},{2,10},{10... | collective-permute-start | bytes 393224 | tf_op jit(solution)/shard_map/ppermute | solution.py:28
  48.8 2.9 %collective-permute-start.17 = (bf16[256,128]{1,0:T(8,128)(2,1)S(1)}, bf16[256,128]{1,0:T(8,128)(2,1)S(1)}, u32[]{:S(2)}, u32[]{:S(2)}) collective-permute-start(bf16[256,128]{1,0:T(8,128)(2,1)S(1)} %shard_map.77.own_ref), channel_id=1, source_target_pairs={{0,1},{1,0},{2,3},{3,2},{4,5},{5,4},{6,7},{7,6},{8,9},{9,8},{10,11... | collective-permute-start | bytes 196616 | tf_op jit(solution)/shard_map/ppermute | solution.py:43
  53.9 4.3 %collective-permute-start.19 = (bf16[128,128]{1,0:T(8,128)(2,1)S(1)}, bf16[128,128]{1,0:T(8,128)(2,1)S(1)}, u32[]{:S(2)}, u32[]{:S(2)}) collective-permute-start(bf16[128,128]{1,0:T(8,128)(2,1)S(1)} %get-tuple-element.39), channel_id=1, source_target_pairs={{0,9},{1,8},{2,11},{3,10},{4,13},{5,12},{6,15},{7,14},{8,17},{9,16... | collective-permute-start | bytes 98312 | tf_op jit(solution)/shard_map/ppermute | solution.py:38
  58.2 1.3 %collective-permute-start.20 = (bf16[128,128]{1,0:T(8,128)(2,1)S(1)}, bf16[128,128]{1,0:T(8,128)(2,1)S(1)}, u32[]{:S(2)}, u32[]{:S(2)}) collective-permute-start(bf16[128,128]{1,0:T(8,128)(2,1)S(1)} %fusion.5), channel_id=1, source_target_pairs={{0,1},{1,0},{2,3},{3,2},{4,5},{5,4},{6,7},{7,6},{8,9},{9,8},{10,11... | collective-permute-start | bytes 98312 | tf_op jit(solution)/shard_map/ppermute | solution.py:43
  59.5 5.2 %collective-permute-start.21 = (bf16[128,128]{1,0:T(8,128)(2,1)S(1)}, bf16[128,128]{1,0:T(8,128)(2,1)S(1)}, u32[]{:S(2)}, u32[]{:S(2)}) collective-permute-start(bf16[128,128]{1,0:T(8,128)(2,1)S(1)} %fusion.7), channel_id=1, source_target_pairs={{0,7},{1,6},{2,5},{3,4},{4,3},{5,2},{6,1},{7,0},{8,15},{9,14},{10,... | collective-permute-start | bytes 98312 | tf_op jit(solution)/shard_map/ppermute | solution.py:43
  61.4 5.1 %collective-permute-start.22 = (bf16[128,128]{1,0:T(8,128)(2,1)S(1)}, bf16[128,128]{1,0:T(8,128)(2,1)S(1)}, u32[]{:S(2)}, u32[]{:S(2)}) collective-permute-start(bf16[128,128]{1,0:T(8,128)(2,1)S(1)} %fusion.7), channel_id=1, source_target_pairs={{0,5},{1,4},{2,7},{3,6},{4,1},{5,0},{6,3},{7,2},{8,13},{9,12},{10,... | collective-permute-start | bytes 98312 | tf_op jit(solution)/shard_map/ppermute | solution.py:43
  61.4 5.1 %collective-permute-start.23 = (bf16[128,128]{1,0:T(8,128)(2,1)S(1)}, bf16[128,128]{1,0:T(8,128)(2,1)S(1)}, u32[]{:S(2)}, u32[]{:S(2)}) collective-permute-start(bf16[128,128]{1,0:T(8,128)(2,1)S(1)} %fusion.7), channel_id=1, source_target_pairs={{0,2},{1,3},{2,0},{3,1},{4,6},{5,7},{6,4},{7,5},{8,10},{9,11},{10,... | collective-permute-start | bytes 98312 | tf_op jit(solution)/shard_map/ppermute | solution.py:43
  66.9 2.8 %collective-permute-start.24 = (bf16[256,128]{1,0:T(8,128)(2,1)S(1)}, bf16[256,128]{1,0:T(8,128)(2,1)S(1)}, u32[]{:S(2)}, u32[]{:S(2)}) collective-permute-start(bf16[256,128]{1,0:T(8,128)(2,1)S(1)} %shard_map.80.own_ref), channel_id=1, source_target_pairs={{0,1},{1,0},{2,3},{3,2},{4,5},{5,4},{6,7},{7,6},{8,9},{9,8},{10,11... | collective-permute-start | bytes 196616 | tf_op jit(solution)/shard_map/ppermute | solution.py:43
  67.1 0.9 %copy-start.2 = (s32[1,64,1]{1,2,0:T(1,128)S(1)}, s32[1,64,1]{1,2,0:T(1,128)}, u32[]{:S(2)}) copy-start(s32[1,64,1]{1,2,0:T(1,128)} %param.9) | copy-start | bytes 772
  67.1 8.4 %collective-permute-start.28 = (f32[4,8192]{1,0:T(4,128)S(1)}, f32[4,8192]{1,0:T(4,128)S(1)}, u32[]{:S(2)}, u32[]{:S(2)}) collective-permute-start(f32[4,8192]{1,0:T(4,128)S(1)} %get-tuple-element.45), channel_id=1, source_target_pairs={{0,8},{8,16},{16,24},{24,0},{1,9},{9,17},{17,25},{25,1},{2,10},{10... | collective-permute-start | bytes 393224 | tf_op jit(solution)/shard_map/ppermute | solution.py:28
  71.8 5.8 %collective-permute-start.25 = (f32[32,4,128]{2,1,0:T(4,128)S(1)}, f32[32,4,128]{2,1,0:T(4,128)S(1)}, u32[]{:S(2)}, u32[]{:S(2)}) collective-permute-start(f32[32,4,128]{2,1,0:T(4,128)S(1)} %get-tuple-element.42), channel_id=1, source_target_pairs={{0,8},{8,0},{16,24},{24,16},{1,9},{9,1},{17,25},{25,17},{2,10},{10... | collective-permute-start | bytes 196616 | tf_op jit(solution)/shard_map/ppermute | solution.py:43
  74.0 4.9 %collective-permute-start.26 = (f32[32,4,128]{2,1,0:T(4,128)S(1)}, f32[32,4,128]{2,1,0:T(4,128)S(1)}, u32[]{:S(2)}, u32[]{:S(2)}) collective-permute-start(f32[32,4,128]{2,1,0:T(4,128)S(1)} %get-tuple-element.43), channel_id=1, source_target_pairs={{0,16},{8,24},{16,0},{24,8},{1,17},{9,25},{17,1},{25,9},{2,18},{10... | collective-permute-start | bytes 196616 | tf_op jit(solution)/shard_map/ppermute | solution.py:43
  74.5 5.2 %collective-permute-start.27 = (f32[32,4,128]{2,1,0:T(4,128)S(1)}, f32[32,4,128]{2,1,0:T(4,128)S(1)}, u32[]{:S(2)}, u32[]{:S(2)}) collective-permute-start(f32[32,4,128]{2,1,0:T(4,128)S(1)} %get-tuple-element.44), channel_id=1, source_target_pairs={{0,24},{8,16},{16,8},{24,0},{1,25},{9,17},{17,9},{25,1},{2,26},{10... | collective-permute-start | bytes 196616 | tf_op jit(solution)/shard_map/ppermute | solution.py:43
